TPU v7x, 32 devices: a whole 2x2x4 slice. The times are simulated.
32 devices in a mesh: wide: 8 (over z, x), narrow: 4 (over y, core).
Axes of the slice: x: 2, y: 2, z: 4, core: 2. Of those that a mesh axis runs over, the one named last changes fastest.
Arguments:
- tokens: bfloat16 [3, 10240, 768], P(None, 'wide'), may hold values from -6 to 6
- image_lengths: int32 [3, 8, 8], P(None, 'wide'), may hold values from 1 to 196, 1280 in all within a row
- heads_weight: bfloat16 [768, 3, 768], P('wide', None, 'narrow'), may hold values from -0.21875 to 0.21875
- heads_bias: float32 [2, 768], P(None, 'narrow'), may hold values from -3 to 3
- out_weight: bfloat16 [768, 768], P('narrow', 'wide'), may hold values from -1.75 to 1.75
- out_bias: float32 [768], replicated, may hold values from -3 to 3
- up_weight: bfloat16 [768, 3072], P('wide', 'narrow'), may hold values from -0.21875 to 0.21875
- up_bias: float32 [3072], P('narrow'), may hold values from -3 to 3
- down_weight: bfloat16 [3072, 768], P('narrow', 'wide'), may hold values from -0.109375 to 0.109375
- down_bias: float32 [768], replicated, may hold values from -3 to 3
- first_gain: float32 [768], replicated, may hold values from 0.1 to 1.9
- first_shift: float32 [768], replicated, may hold values from -3 to 3
- second_gain: float32 [768], replicated, may hold values from 0.1 to 1.9
- second_shift: float32 [768], replicated, may hold values from -3 to 3
- mixer_scale: float32 [768], replicated, may hold values from 0.5 to 2
- feed_scale: float32 [768], replicated, may hold values from 0.5 to 2
- cotangent: bfloat16 [3, 10240, 768], P(None, 'wide'), may hold values from -6 to 6
Outputs:
- layer_out: bfloat16 [3, 10240, 768], P(None, 'wide')
- token_grad: bfloat16 [3, 10240, 768], P(None, ('wide', 'narrow'))
- heads_weight_grad: float32 [768, 3, 768], P(None, None, 'narrow')
- heads_bias_grad: float32 [2, 768], P(None, 'narrow')
- out_weight_grad: float32 [768, 768], P('narrow')
- out_bias_grad: float32 [768], replicated
- up_weight_grad: float32 [768, 3072], P(None, 'narrow')
- up_bias_grad: float32 [3072], P('narrow')
- down_weight_grad: float32 [3072, 768], P('narrow')
- down_bias_grad: float32 [768], replicated
- first_gain_grad: float32 [768], replicated
- first_shift_grad: float32 [768], replicated
- second_gain_grad: float32 [768], replicated
- second_shift_grad: float32 [768], replicated
- mixer_scale_grad: float32 [768], replicated
- feed_scale_grad: float32 [768], replicated
Inputs may be any that keep to these rules, and one draw needn't show every extreme that they name: `image_lengths`: each row of 8 numbers gives the lengths of the images packed in order into one micro-batch of one index of wide; they sum to 1280, and the largest is 196.
All inputs are finite; a program needn't handle non-finite values.
Results may differ from a plain program's by a relative error of at most 0.02.
Values may be sent and summed in bfloat16 or wider, within the bound.
No kernel may reach another device: no remote copies, remote signals or barrier semaphores. Data moves between devices by JAX's collectives and lax.ppermute only.
A program may use at most 256 MiB of HBM per device.

v0:
```python
from functools import partial
from functools import reduce

import jax
import jax.numpy as jnp
from jax import lax
from jax.sharding import PartitionSpec as P

HEAD_DIM = 64
QUERY_BLOCK = 640


epsilon = 1e-06


def norm_parts(values_in):
    center = jnp.mean(values_in, axis=-1, keepdims=True)
    shifted = values_in - center
    inverse = lax.rsqrt(jnp.mean(shifted * shifted, axis=-1, keepdims=True) + epsilon)
    return (shifted * inverse, inverse)


def norm_back(grad_in, unit_rows, inverse, gain_row):
    scaled = grad_in * gain_row
    return inverse * (
        scaled
        - jnp.mean(scaled, axis=-1, keepdims=True)
        - unit_rows * jnp.mean(scaled * unit_rows, axis=-1, keepdims=True)
    )


def image_index(sizes_row, row_count):
    bounds = jnp.cumsum(sizes_row)
    places = jnp.arange(row_count, dtype=jnp.int32)
    return jnp.sum((places[:, None] >= bounds[None, :]).astype(jnp.int32), axis=1)


def exact_gelu(values_in):
    return jax.nn.gelu(values_in, approximate=False)


def attend_forward(key_heads, value_heads, attention_scale, block_items):
    query_heads, same_image = block_items
    raw_scores = (
        jnp.einsum("qhc,khc->hqk", query_heads, key_heads, preferred_element_type=jnp.float32)
        * attention_scale
    )
    scores = jnp.where(same_image[None], raw_scores, -1e30)
    row_max = jnp.max(scores, axis=-1, keepdims=True)
    exp_scores = jnp.exp(scores - row_max)
    exp_total = jnp.sum(exp_scores, axis=-1, keepdims=True)
    soft_weights = (exp_scores / exp_total).astype(jnp.bfloat16)
    context = jnp.einsum(
        "hqk,khc->qhc", soft_weights, value_heads, preferred_element_type=jnp.float32
    )
    return (context, row_max + jnp.log(exp_total))


def attend_back(key_heads, value_heads, attention_scale, running, block_items):
    query_heads, context_grad, same_image, log_total = block_items
    raw_scores = (
        jnp.einsum("qhc,khc->hqk", query_heads, key_heads, preferred_element_type=jnp.float32)
        * attention_scale
    )
    scores = jnp.where(same_image[None], raw_scores, -1e30)
    soft_weights = jnp.exp(scores - log_total)
    weight_grad = jnp.einsum(
        "qhc,khc->hqk", context_grad, value_heads, preferred_element_type=jnp.float32
    )
    row_delta = jnp.sum(soft_weights * weight_grad, axis=-1, keepdims=True)
    score_grad = (soft_weights * (weight_grad - row_delta)).astype(jnp.bfloat16)
    query_grad = (
        jnp.einsum("hqk,khc->qhc", score_grad, key_heads, preferred_element_type=jnp.float32)
        * attention_scale
    )
    key_grad = (
        jnp.einsum("hqk,qhc->khc", score_grad, query_heads, preferred_element_type=jnp.float32)
        * attention_scale
    )
    value_grad = jnp.einsum(
        "hqk,qhc->khc",
        soft_weights.astype(jnp.bfloat16),
        context_grad,
        preferred_element_type=jnp.float32,
    )
    return ((running[0] + key_grad, running[1] + value_grad), query_grad)


def feed_term(upper_grad, up_full):
    return jnp.einsum("rf,df->rd", upper_grad, up_full, preferred_element_type=jnp.float32)


def heads_term_rows(heads_grad, heads_full):
    return jnp.einsum("rtc,dtc->rd", heads_grad, heads_full, preferred_element_type=jnp.float32)


def add_tuples(left, right):
    return jax.tree.map(jnp.add, left, right)


def body(
    tokens,
    image_lengths,
    heads_weight,
    heads_bias,
    out_weight,
    out_bias,
    up_weight,
    up_bias,
    down_weight,
    down_bias,
    first_gain,
    first_shift,
    second_gain,
    second_shift,
    mixer_scale,
    feed_scale,
    cotangent,
):
    micro_count, row_count, width = tokens.shape
    quarter = row_count // lax.axis_size("narrow")
    quarter_start = lax.axis_index("narrow") * quarter
    attention_scale = HEAD_DIM ** (-0.5)
    head_local = heads_weight.shape[2] // HEAD_DIM
    block_count = row_count // QUERY_BLOCK

    def quarter_rows(values_in):
        return lax.dynamic_slice_in_dim(values_in, quarter_start, quarter, 0)

    zero_row = jnp.zeros((width,), jnp.float32)
    out_bias_sum, down_bias_sum = (zero_row, zero_row)
    first_gain_sum, first_shift_sum = (zero_row, zero_row)
    second_gain_sum, second_shift_sum = (zero_row, zero_row)
    mixer_scale_sum, feed_scale_sum = (zero_row, zero_row)
    head_bias_sum = jnp.zeros(heads_bias.shape, jnp.float32)
    up_bias_sum = jnp.zeros(up_bias.shape, jnp.float32)
    term_list = []
    outputs = []
    input_grads = []
    for micro_index in range(micro_count):
        gathered = (
            lax.all_gather(heads_weight, "wide", axis=0, tiled=True),
            lax.all_gather(out_weight, "wide", axis=1, tiled=True),
            lax.all_gather(up_weight, "wide", axis=0, tiled=True),
            lax.all_gather(down_weight, "wide", axis=1, tiled=True),
        )
        heads_full, out_full, up_full, down_full = gathered
        token_rows = tokens[micro_index].astype(jnp.float32)
        index_row = image_index(image_lengths[micro_index, 0], row_count)
        same_image = index_row[:, None] == index_row[None, :]
        first_unit, first_inverse = norm_parts(token_rows)
        first_normed = (first_unit * first_gain + first_shift).astype(jnp.bfloat16)
        projected = jnp.einsum(
            "rd,dtc->rtc", first_normed, heads_full, preferred_element_type=jnp.float32
        )
        query_heads = (
            (projected[:, 0] + heads_bias[0])
            .astype(jnp.bfloat16)
            .reshape(row_count, head_local, HEAD_DIM)
        )
        key_heads = projected[:, 1].astype(jnp.bfloat16).reshape(row_count, head_local, HEAD_DIM)
        value_heads = (
            (projected[:, 2] + heads_bias[1])
            .astype(jnp.bfloat16)
            .reshape(row_count, head_local, HEAD_DIM)
        )
        query_blocks = query_heads.reshape(block_count, QUERY_BLOCK, head_local, HEAD_DIM)
        same_blocks = same_image.reshape(block_count, QUERY_BLOCK, row_count)
        context_blocks, log_total = lax.map(
            partial(attend_forward, key_heads, value_heads, attention_scale),
            (query_blocks, same_blocks),
        )
        context = context_blocks.reshape(row_count, head_local * HEAD_DIM).astype(jnp.bfloat16)
        mixed = lax.psum(
            jnp.dot(context, out_full, preferred_element_type=jnp.float32).astype(jnp.bfloat16),
            "narrow",
        ).astype(jnp.float32)
        middle = token_rows + mixer_scale * (mixed + out_bias)
        second_unit, second_inverse = norm_parts(middle)
        second_normed = (second_unit * second_gain + second_shift).astype(jnp.bfloat16)
        upper = jnp.dot(second_normed, up_full, preferred_element_type=jnp.float32) + up_bias
        active, gelu_slope = jax.vjp(exact_gelu, upper)
        active = active.astype(jnp.bfloat16)
        feed = lax.psum(
            jnp.dot(active, down_full, preferred_element_type=jnp.float32).astype(jnp.bfloat16),
            "narrow",
        ).astype(jnp.float32)
        outputs.append((middle + feed_scale * (feed + down_bias)).astype(jnp.bfloat16))
        output_grad = cotangent[micro_index].astype(jnp.float32)
        feed_grad = (feed_scale * output_grad).astype(jnp.bfloat16)
        active_grad = jnp.einsum(
            "rd,fd->rf", feed_grad, down_full, preferred_element_type=jnp.float32
        )
        down_term = jnp.einsum("rf,rd->fd", active, feed_grad, preferred_element_type=jnp.float32)
        upper_grad = gelu_slope(active_grad)[0].astype(jnp.bfloat16)
        up_term = jnp.einsum(
            "rd,rf->df", second_normed, upper_grad, preferred_element_type=jnp.float32
        )
        up_bias_sum = up_bias_sum + jnp.sum(upper_grad.astype(jnp.float32), axis=0)
        second_normed_grad = lax.psum_scatter(
            feed_term(upper_grad, up_full).astype(jnp.bfloat16),
            "narrow",
            scatter_dimension=0,
            tiled=True,
        ).astype(jnp.float32)
        out_quarter = quarter_rows(output_grad)
        second_unit_part = quarter_rows(second_unit)
        second_gain_sum = second_gain_sum + jnp.sum(second_normed_grad * second_unit_part, axis=0)
        second_shift_sum = second_shift_sum + jnp.sum(second_normed_grad, axis=0)
        feed_scale_sum = feed_scale_sum + jnp.sum(
            out_quarter * (quarter_rows(feed) + down_bias), axis=0
        )
        down_bias_sum = down_bias_sum + feed_scale * jnp.sum(out_quarter, axis=0)
        middle_grad = out_quarter + norm_back(
            second_normed_grad, second_unit_part, quarter_rows(second_inverse), second_gain
        )
        mixer_scale_sum = mixer_scale_sum + jnp.sum(
            middle_grad * (quarter_rows(mixed) + out_bias), axis=0
        )
        out_bias_sum = out_bias_sum + mixer_scale * jnp.sum(middle_grad, axis=0)
        mixed_grad = lax.all_gather(
            (mixer_scale * middle_grad).astype(jnp.bfloat16), "narrow", axis=0, tiled=True
        )
        out_term = jnp.einsum("rc,rd->cd", context, mixed_grad, preferred_element_type=jnp.float32)
        context_grad = jnp.einsum(
            "rd,cd->rc", mixed_grad, out_full, preferred_element_type=jnp.float32
        )
        context_grad = context_grad.astype(jnp.bfloat16).reshape(
            block_count, QUERY_BLOCK, head_local, HEAD_DIM
        )
        zero_heads = jnp.zeros((row_count, head_local, HEAD_DIM), jnp.float32)
        (key_total, value_total), query_total = lax.scan(
            partial(attend_back, key_heads, value_heads, attention_scale),
            (zero_heads, zero_heads),
            (query_blocks, context_grad, same_blocks, log_total),
        )
        heads_grad = jnp.stack(
            [
                query_total.reshape(row_count, head_local * HEAD_DIM),
                key_total.reshape(row_count, head_local * HEAD_DIM),
                value_total.reshape(row_count, head_local * HEAD_DIM),
            ],
            axis=1,
        ).astype(jnp.bfloat16)
        head_bias_sum = head_bias_sum + jnp.stack(
            [
                jnp.sum(heads_grad[:, 0].astype(jnp.float32), axis=0),
                jnp.sum(heads_grad[:, 2].astype(jnp.float32), axis=0),
            ]
        )
        heads_term = jnp.einsum(
            "rd,rtc->dtc", first_normed, heads_grad, preferred_element_type=jnp.float32
        )
        first_normed_grad = lax.psum_scatter(
            heads_term_rows(heads_grad, heads_full).astype(jnp.bfloat16),
            "narrow",
            scatter_dimension=0,
            tiled=True,
        ).astype(jnp.float32)
        first_unit_part = quarter_rows(first_unit)
        first_gain_sum = first_gain_sum + jnp.sum(first_normed_grad * first_unit_part, axis=0)
        first_shift_sum = first_shift_sum + jnp.sum(first_normed_grad, axis=0)
        input_grads.append(
            (
                middle_grad
                + norm_back(
                    first_normed_grad, first_unit_part, quarter_rows(first_inverse), first_gain
                )
            ).astype(jnp.bfloat16)
        )
        term_list.append((heads_term, out_term, up_term, down_term))
    summed_terms = reduce(add_tuples, term_list)
    heads_total, out_total, up_total, down_total, head_bias_total, up_bias_total = lax.psum(
        (
            summed_terms[0],
            summed_terms[1],
            summed_terms[2],
            summed_terms[3],
            head_bias_sum,
            up_bias_sum,
        ),
        "wide",
    )
    (
        out_bias_total,
        down_bias_total,
        first_gain_total,
        first_shift_total,
        second_gain_total,
        second_shift_total,
        mixer_scale_total,
        feed_scale_total,
    ) = lax.psum(
        (
            out_bias_sum,
            down_bias_sum,
            first_gain_sum,
            first_shift_sum,
            second_gain_sum,
            second_shift_sum,
            mixer_scale_sum,
            feed_scale_sum,
        ),
        ("wide", "narrow"),
    )
    return (
        jnp.stack(outputs),
        jnp.stack(input_grads),
        heads_total,
        head_bias_total,
        out_total,
        out_bias_total,
        up_total,
        up_bias_total,
        down_total,
        down_bias_total,
        first_gain_total,
        first_shift_total,
        second_gain_total,
        second_shift_total,
        mixer_scale_total,
        feed_scale_total,
    )


def solution(mesh):
    return jax.shard_map(
        body,
        mesh=mesh,
        in_specs=(
            P(None, "wide", None),
            P(None, "wide", None),
            P("wide", None, "narrow"),
            P(None, "narrow"),
            P("narrow", "wide"),
            P(),
            P("wide", "narrow"),
            P("narrow"),
            P("narrow", "wide"),
            P(),
            P(),
            P(),
            P(),
            P(),
            P(),
            P(),
            P(None, "wide", None),
        ),
        out_specs=(
            P(None, "wide", None),
            P(None, ("wide", "narrow"), None),
            P(None, None, "narrow"),
            P(None, "narrow"),
            P("narrow", None),
            P(),
            P(None, "narrow"),
            P("narrow"),
            P("narrow", None),
            P(),
            P(),
            P(),
            P(),
            P(),
            P(),
            P(),
        ),
        check_vma=False,
    )
```

profile of v0, /device:TPU:0, one launch (start us, length us, event | category | flops | bytes accessed | tf_op | source)
XLA Modules:
  0.0 991.3 jit_solution(16991604911997666892)
XLA Ops:
  15.0 38.7 %all_gather.14 = bf16[768,3,192]{2,1,0:T(4,128)(2,1)S(1)} all-gather(bf16[96,3,192]{2,1,0:T(4,128)(2,1)S(1)} %copy.82), channel_id=1, replica_groups=mesh['wide'=8,'narrow'=4] {'wide'}, dimensions={0}, use_global_device_ids=true | all-gather | bytes 995328 | tf_op jit(solution)/shard_map/all_gather | solution.py:142
  68.0 33.1 %all_gather.30 = bf16[192,768]{0,1:T(8,128)(2,1)} all-gather(bf16[192,96]{0,1:T(8,128)(2,1)S(1)} %copy.86), channel_id=1, replica_groups=mesh['wide'=8,'narrow'=4] {'wide'}, dimensions={1}, use_global_device_ids=true | all-gather | bytes 331776 | tf_op jit(solution)/shard_map/all_gather | solution.py:143
  119.8 23.0 %while.83 = (s32[]{:T(128)}, bf16[2,640,3,64]{1,3,2,0:T(8,128)(2,1)}, f32[2,3,640,1]{2,1,3,0:T(4,128)S(1)}, pred[2,640,1280]{2,1,0:T(8,128)(4,1)}, bf16[2,640,3,...) while((s32[]{:T(128)}, ...), condition=%wide.region_31.32_spmd, body=%wide.region_28.31_spmd.sunk | while | flops 658634880 | bytes 41280192 | solution.py:169
  143.9 18.9 %while.82 = (s32[]{:T(128)}, bf16[2,640,3,64]{1,3,2,0:T(8,128)(2,1)}, f32[2,3,640,1]{2,1,3,0:T(4,128)S(1)}, pred[2,640,1280]{2,1,0:T(8,128)(4,1)S(1)}, bf16[2,64...) while((s32[]{:T(128)}, ...), condition=%wide.region_19.20_spmd, body=%wide.region_16.19_spmd.sunk | while | flops 658634880 | bytes 41280192 | solution.py:169
  164.4 23.2 %while.81 = (s32[]{:T(128)}, bf16[2,640,3,64]{1,3,2,0:T(8,128)(2,1)}, f32[2,3,640,1]{2,1,3,0:T(4,128)S(1)}, pred[2,640,1280]{2,1,0:T(8,128)(4,1)}, bf16[2,640,3,...) while((s32[]{:T(128)}, ...), condition=%wide.region_7.8_spmd, body=%wide.region_4.7_spmd.sunk | while | flops 658634880 | bytes 41280192 | solution.py:169
  199.1 111.8 %all-reduce.13.cloned.1.call-done = (bf16[1280,768]{1,0:T(8,128)(2,1)}, bf16[1280,768]{1,0:T(8,128)(2,1)}, bf16[1280,768]{1,0:T(8,128)(2,1)}) async-done(((bf16[1280,768]{1,0:T(8,128)(2,1)}, bf16[1280,768]{1,0:T(8,128)(2,1)}, bf16[1280,768]{1,0:T(8,128)(2,1)}), (bf16[1280,768]{1,0:T(8,128)(2,1)}, bf16[1280,768]{1,0:T(8,128)(2,1)}, bf16[1280,768]{1,0:T(8,128)(2,1)})) %all-reduce.13.cloned.1.call-update) | async-done | bytes 5898256 | tf_op jit(solution)/shard_map/psum | solution.py:174
  311.0 8.6 fusion.206
  325.7 6.9 subtract_multiply_fusion.2
  332.6 14.0 %multiply_convert_fusion.5 = (bf16[1280,768]{1,0:T(8,128)(2,1)}, f32[1280,768]{1,0:T(8,128)}, f32[1280,768]{1,0:T(8,128)}) fusion(f32[768]{0:T(1024)S(1)} %copy-done.172, bf16[768,768]{1,0:T(8,128)(2,1)} %all-gather.6.cloned.1.call-done, f32[1280,768]{1,0:T(8,128)} %get-tuple-element.723, f32[768]{0:T(1024)S(1)} %copy-done.173, f32[768]{0:T(1024)S(1)} %copy-done.143), kind=kOutput, calls=%fused_computation.210 | convolution fusion | flops 1577779200 | bytes 14951424 | tf_op jit(solution)/shard_map/dot_general | solution.py:181
  346.6 7.7 convert_reduce_fusion.5
  358.8 12.5 %multiply_convert_fusion.4 = (bf16[1280,768]{1,0:T(8,128)(2,1)}, f32[1280,768]{1,0:T(8,128)S(1)}, f32[1280,768]{1,0:T(8,128)S(1)}) fusion(f32[768]{0:T(1024)S(1)} %copy-done.172, bf16[768,768]{1,0:T(8,128)(2,1)} %all-gather.6.cloned.1.call-done, f32[1280,768]{1,0:T(8,128)} %get-tuple-element.724, f32[768]{0:T(1024)S(1)} %copy-done.173, f32[768]{0:T(1024)S(1)} %copy-done.143), kind=kOutput, calls=%fused_computation.193 | convolution fusion | flops 1577779200 | bytes 14951424 | tf_op jit(solution)/shard_map/dot_general | solution.py:181
  371.2 5.2 convert_reduce_fusion.4
  380.8 12.9 %multiply_convert_fusion.3 = (bf16[1280,768]{1,0:T(8,128)(2,1)}, f32[1280,768]{1,0:T(8,128)S(1)}, f32[1280,768]{1,0:T(8,128)S(1)}) fusion(f32[768]{0:T(1024)S(1)} %copy-done.172, bf16[768,768]{1,0:T(8,128)(2,1)} %all-gather.6.cloned.1.call-done, f32[1280,768]{1,0:T(8,128)} %get-tuple-element.725, f32[768]{0:T(1024)S(1)} %copy-done.173, f32[768]{0:T(1024)S(1)} %copy-done.143), kind=kOutput, calls=%fused_computation.176 | convolution fusion | flops 1577779200 | bytes 14951424 | tf_op jit(solution)/shard_map/dot_general | solution.py:181
  393.7 5.2 convert_reduce_fusion.3
  403.3 7.5 slice_convert_fusion
  417.8 4.6 reduce-scatter.11.cloned.1.call-done
  422.4 33.4 %reduce-scatter.15.cloned.1.call-done = bf16[320,768]{1,0:T(8,128)(2,1)} async-done(((bf16[1280,768]{1,0:T(8,128)(2,1)}), bf16[320,768]{1,0:T(8,128)(2,1)}) %reduce-scatter.15.cloned.1.call-update) | async-done | bytes 491536 | tf_op jit(solution)/shard_map/reduce_scatter | solution.py:200
  459.7 5.0 multiply_reduce_fusion.7
  473.3 4.8 convolution_convert_fusion.8
  484.6 4.7 convolution_convert_fusion.7
  492.3 4.7 fusion.226
  499.9 5.0 add_add_fusion
  517.1 57.6 %while.86 = (s32[]{:T(128)}, f32[1280,3,64]{0,2,1:T(8,128)}, f32[1280,3,64]{0,2,1:T(8,128)}, bf16[2,640,3,64]{1,3,2,0:T(8,128)(2,1)}, bf16[2,640,3,64]{1,3,2,0:T...) while((s32[]{:T(128)}, f32[1280,3,64]{0,2,1:T(8,128)}, ...), condition=%wide.region_59.60_spmd.clone, body=%wide.region_57.59_spmd.clone.sunk | while | flops 1596332160 | bytes 153887056 | solution.py:232
  519.7 6.7 multiply_reduce_fusion.14
  526.5 9.8 multiply_convert_fusion.14
  536.3 5.8 fusion.430
  548.3 6.7 multiply_reduce_fusion.14
  555.0 10.0 %multiply_convert_fusion.14 = bf16[3,640,1280]{2,1,0:T(8,128)(2,1)} fusion(f32[3,640,1280]{2,1,0:T(8,128)} %get-tuple-element.1107, f32[3,640,1280]{2,1,0:T(8,128)} %copy-done, f32[3,640]{1,0:T(4,128)S(1)} %get-tuple-element.1108), kind=kLoop, calls=%fused_computation.104.clone.1 | loop fusion | flops 7372800 | bytes 24583680 | tf_op jit(solution)/shard_map/while/body/eval_jaxpr/convert_element_type | solution.py:71
  565.0 6.1 fusion.430
  588.5 58.6 %while.84 = (s32[]{:T(128)}, f32[1280,3,64]{0,2,1:T(8,128)}, f32[1280,3,64]{0,2,1:T(8,128)}, bf16[2,640,3,64]{1,3,2,0:T(8,128)(2,1)}, bf16[2,640,3,64]{1,3,2,0:T...) while((s32[]{:T(128)}, f32[1280,3,64]{0,2,1:T(8,128)}, ...), condition=%wide.region_41.42_spmd.clone, body=%wide.region_39.41_spmd.clone.sunk | while | flops 1596332160 | bytes 153887056 | solution.py:232
  591.1 6.6 multiply_reduce_fusion.12
  597.7 11.1 %multiply_convert_fusion.12 = bf16[3,640,1280]{2,1,0:T(8,128)(2,1)} fusion(f32[3,640,1280]{2,1,0:T(8,128)} %get-tuple-element.1083, f32[3,640,1280]{2,1,0:T(8,128)} %copy-done.1, f32[3,640]{1,0:T(4,128)S(1)} %get-tuple-element.1084), kind=kLoop, calls=%fused_computation.48.clone.1 | loop fusion | flops 7372800 | bytes 24583680 | tf_op jit(solution)/shard_map/while/body/eval_jaxpr/convert_element_type | solution.py:71
  608.8 5.9 fusion.404
  620.9 6.6 multiply_reduce_fusion.12
  627.5 10.0 %multiply_convert_fusion.12 = bf16[3,640,1280]{2,1,0:T(8,128)(2,1)} fusion(f32[3,640,1280]{2,1,0:T(8,128)} %get-tuple-element.1083, f32[3,640,1280]{2,1,0:T(8,128)} %copy-done.1, f32[3,640]{1,0:T(4,128)S(1)} %get-tuple-element.1084), kind=kLoop, calls=%fused_computation.48.clone.1 | loop fusion | flops 7372800 | bytes 24583680 | tf_op jit(solution)/shard_map/while/body/eval_jaxpr/convert_element_type | solution.py:71
  637.5 6.0 fusion.404
  653.3 4.6 bitcast_convert_fusion.2
  658.9 58.0 %while.85 = (s32[]{:T(128)}, f32[1280,3,64]{0,2,1:T(8,128)}, f32[1280,3,64]{0,2,1:T(8,128)}, bf16[2,640,3,64]{1,3,2,0:T(8,128)(2,1)}, bf16[2,640,3,64]{1,3,2,0:T...) while((s32[]{:T(128)}, f32[1280,3,64]{0,2,1:T(8,128)}, ...), condition=%wide.region_50.51_spmd.clone, body=%wide.region_48.50_spmd.clone.sunk | while | flops 1596332160 | bytes 153887056 | solution.py:232
  661.5 6.6 multiply_reduce_fusion.13
  668.2 10.1 %multiply_convert_fusion.13 = bf16[3,640,1280]{2,1,0:T(8,128)(2,1)} fusion(f32[3,640,1280]{2,1,0:T(8,128)} %get-tuple-element.1095, f32[3,640,1280]{2,1,0:T(8,128)} %copy-done.2, f32[3,640]{1,0:T(4,128)S(1)} %get-tuple-element.1096), kind=kLoop, calls=%fused_computation.76.clone.1 | loop fusion | flops 7372800 | bytes 24583680 | tf_op jit(solution)/shard_map/while/body/eval_jaxpr/convert_element_type | solution.py:71
  678.3 5.9 fusion.417
  690.3 6.8 multiply_reduce_fusion.13
  697.5 9.8 multiply_convert_fusion.13
  707.3 6.1 fusion.417
  745.6 8.3 fusion.144
  758.1 23.9 %all-reduce.1 = (f32[2,192]{1,0:T(2,128)}, f32[768]{0:T(1024)}) all-reduce(f32[2,192]{1,0:T(2,128)S(1)} %fusion.235, f32[768]{0:T(1024)S(1)} %add_add_fusion.9), channel_id=1, replica_groups=mesh['wide'=8,'narrow'=4] {'wide'}, use_global_device_ids=true, to_apply=%region_70.71 | all-reduce | flops 1152 | bytes 9216 | tf_op jit(solution)/shard_map/psum | solution.py:273
  790.3 41.7 %all-reduce = (f32[768]{0:T(1024)}, f32[768]{0:T(1024)}, f32[768]{0:T(1024)}, f32[768]{0:T(1024)}, f32[768]{0:T(1024)}, /*index=5*/f32[768]{0:T(1024)}, f32[768]{0:T(1024)}, f32[768]{0:T(1024)}) all-reduce(f32[768]{0:T(1024)S(1)} %add_multiply_fusion.1, ...), channel_id=1, replica_groups=mesh['wide'=8,'narrow'=4] {'wide','narrow'}, use_global_device_ids=true, to_apply=%region_75.76 | all-reduce | flops 6144 | bytes 49152 | tf_op jit(solution)/shard_map/psum | solution.py:293
  835.8 141.4 %all-reduce.9.cloned.1.call-done = (f32[768,3,192]{0,2,1:T(8,128)}, f32[192,768]{1,0:T(8,128)}, f32[768,768]{1,0:T(8,128)}, f32[768,768]{1,0:T(8,128)}) async-done(((f32[768,3,192]{0,2,1:T(8,128)}, f32[192,768]{1,0:T(8,128)}, f32[768,768]{1,0:T(8,128)}, f32[768,768]{1,0:T(8,128)}), (f32[768,3,192]{0,2,1:T(8,128)}, f32[192,768]{1,0:T(8,128)}, f32[768,768]{1,0:T(8,128)}, ...) | async-done | bytes 7077904 | tf_op jit(solution)/shard_map/psum | solution.py:273
  (711 shorter events, 289.3 us)
Async XLA Ops:
  8.0 302.9 %all-reduce.13.cloned.1.call-start = ((), (), s32[]{:S(2)}) async-start(), calls=%async_computation.19 | async-start | bytes 11796480 | tf_op jit(solution)/shard_map/psum | solution.py:174
  11.8 51.1 %copy-start.122 = (f32[1280]{0:T(1024)}, f32[1280]{0:T(1024)S(1)}, u32[]{:S(2)}) copy-start(f32[1280]{0:T(1024)S(1)} %broadcast_multiply_fusion.5) | copy-start | bytes 15364
  11.8 42.7 %copy-start.125 = (f32[1280]{0:T(1024)}, f32[1280]{0:T(1024)S(1)}, u32[]{:S(2)}) copy-start(f32[1280]{0:T(1024)S(1)} %get-tuple-element.769) | copy-start | bytes 15364
  11.9 48.0 %copy-start.128 = (f32[1280]{0:T(1024)}, f32[1280]{0:T(1024)S(1)}, u32[]{:S(2)}) copy-start(f32[1280]{0:T(1024)S(1)} %get-tuple-element.770) | copy-start | bytes 15364
  12.5 42.1 %copy-start.131 = (f32[768]{0:T(1024)S(1)}, f32[768]{0:T(1024)}, u32[]{:S(2)}) copy-start(f32[768]{0:T(1024)} %param.39) | copy-start | bytes 9220
  12.5 42.1 %copy-start.174 = (f32[768]{0:T(1024)S(1)}, f32[768]{0:T(1024)}, u32[]{:S(2)}) copy-start(f32[768]{0:T(1024)} %param.40) | copy-start | bytes 9220
  14.8 43.5 %copy-start.134 = (f32[1280]{0:T(1024)}, f32[1280]{0:T(1024)S(1)}, u32[]{:S(2)}) copy-start(f32[1280]{0:T(1024)S(1)} %add_rsqrt_fusion.1) | copy-start | bytes 15364
  143.9 19.8 %copy-start.9 = (bf16[1280,1,192]{0,2,1:T(8,128)(2,1)S(1)}, bf16[1280,1,192]{0,2,1:T(8,128)(2,1)}, u32[]{:S(2)}) copy-start(bf16[1280,1,192]{0,2,1:T(8,128)(2,1)} %slice.187) | copy-start | bytes 1474564
  195.8 115.2 %copy-start.117 = (f32[768]{0:T(1024)S(1)}, f32[768]{0:T(1024)}, u32[]{:S(2)}) copy-start(f32[768]{0:T(1024)} %param.43) | copy-start | bytes 9220
  195.8 115.2 %copy-start.120 = (f32[768]{0:T(1024)S(1)}, f32[768]{0:T(1024)}, u32[]{:S(2)}) copy-start(f32[768]{0:T(1024)} %param.34) | copy-start | bytes 9220
  195.8 115.1 %copy-start.126 = (f32[1280]{0:T(1024)S(1)}, f32[1280]{0:T(1024)}, u32[]{:S(2)}) copy-start(f32[1280]{0:T(1024)} %copy-done.125) | copy-start | bytes 15364
  195.8 115.1 %copy-start.129 = (f32[1280]{0:T(1024)S(1)}, f32[1280]{0:T(1024)}, u32[]{:S(2)}) copy-start(f32[1280]{0:T(1024)} %copy-done.128) | copy-start | bytes 15364
  195.8 115.1 %copy-start.135 = (f32[1280]{0:T(1024)S(1)}, f32[1280]{0:T(1024)}, u32[]{:S(2)}) copy-start(f32[1280]{0:T(1024)} %copy-done.134) | copy-start | bytes 15364
  195.8 115.1 %copy-start.138 = (f32[1280]{0:T(1024)S(1)}, f32[1280]{0:T(1024)}, u32[]{:S(2)}) copy-start(f32[1280]{0:T(1024)} %copy-done.137) | copy-start | bytes 15364
  197.8 134.7 %all-gather.6.cloned.1.call-start = ((), (), s32[]{:S(2)}) async-start(), calls=%async_computation.6 | async-start | bytes 1327104 | tf_op jit(solution)/shard_map/all_gather | solution.py:144
  198.4 148.2 %all-gather.8.cloned.1.call-start = ((), (), s32[]{:S(2)}) async-start(), calls=%async_computation.7 | async-start | bytes 1327104 | tf_op jit(solution)/shard_map/all_gather | solution.py:145
  199.0 218.8 %reduce-scatter.7.cloned.1.call-start = ((), (), s32[]{:S(2)}) async-start(), calls=%async_computation.8 | async-start | bytes 2457600 | tf_op jit(solution)/shard_map/reduce_scatter | solution.py:200
  311.0 9.4 copy-start.17
  311.0 10.1 %copy-start.19 = (bf16[1280,768]{1,0:T(8,128)(2,1)S(1)}, bf16[1280,768]{1,0:T(8,128)(2,1)}, u32[]{:S(2)}) copy-start(bf16[1280,768]{1,0:T(8,128)(2,1)} %get-tuple-element.697) | copy-start | bytes 5898244
  311.0 10.7 %copy-start.21 = (bf16[1280,768]{1,0:T(8,128)(2,1)S(1)}, bf16[1280,768]{1,0:T(8,128)(2,1)}, u32[]{:S(2)}) copy-start(bf16[1280,768]{1,0:T(8,128)(2,1)} %get-tuple-element.698) | copy-start | bytes 5898244
  332.6 14.0 %copy-start.145 = (f32[768]{0:T(1024)S(1)}, f32[768]{0:T(1024)}, u32[]{:S(2)}) copy-start(f32[768]{0:T(1024)} %param.44) | copy-start | bytes 9220
  346.6 9.0 copy-start.169
  358.7 63.7 %reduce-scatter.11.cloned.1.call-start = ((), (), s32[]{:S(2)}) async-start(), calls=%async_computation.11 | async-start | bytes 2457600 | tf_op jit(solution)/shard_map/reduce_scatter | solution.py:200
  358.8 12.5 %copy-start.168 = (bf16[768,768]{0,1:T(8,128)(2,1)S(1)}, bf16[768,768]{0,1:T(8,128)(2,1)}, u32[]{:S(2)}) copy-start(bf16[768,768]{0,1:T(8,128)(2,1)} %all-gather.8.cloned.1.call-done) | copy-start | bytes 3538948
  380.8 75.0 %reduce-scatter.15.cloned.1.call-start = ((), (), s32[]{:S(2)}) async-start(), calls=%async_computation.14 | async-start | bytes 2457600 | tf_op jit(solution)/shard_map/reduce_scatter | solution.py:200
  403.2 105.3 %all-gather.14.cloned.1.call-start = ((), (), s32[]{:S(2)}) async-start(), calls=%async_computation.15 | async-start | bytes 2457600 | tf_op jit(solution)/shard_map/all_gather | solution.py:221
  417.8 41.9 %copy-start.87 = (bf16[320,768]{1,0:T(8,128)(2,1)S(1)}, bf16[320,768]{1,0:T(8,128)(2,1)}, u32[]{:S(2)}) copy-start(bf16[320,768]{1,0:T(8,128)(2,1)} %reduce-scatter.7.cloned.1.call-done) | copy-start | bytes 1474564
  422.4 37.3 %copy-start.88 = (bf16[320,768]{1,0:T(8,128)(2,1)S(1)}, bf16[320,768]{1,0:T(8,128)(2,1)}, u32[]{:S(2)}) copy-start(bf16[320,768]{1,0:T(8,128)(2,1)} %reduce-scatter.11.cloned.1.call-done) | copy-start | bytes 1474564
  465.7 12.3 %slice-start.6 = ((s8[5898240]{0:T(1024)(128)(4,1)}), s8[1703936]{0:T(1024)(128)(4,1)S(1)}, s32[]{:S(2)}) async-start(s8[5898240]{0:T(1024)(128)(4,1)} %bitcast.559), calls=%async_computation.26 | async-start | bytes 3407872
  467.0 107.7 %all-gather.10.cloned.1.call-start = ((), (), s32[]{:S(2)}) async-start(), calls=%async_computation.9 | async-start | bytes 2457600 | tf_op jit(solution)/shard_map/all_gather | solution.py:221
  467.5 179.6 %all-gather.12.cloned.1.call-start = ((), (), s32[]{:S(2)}) async-start(), calls=%async_computation.12 | async-start | bytes 2457600 | tf_op jit(solution)/shard_map/all_gather | solution.py:221
  484.5 240.1 %all-reduce.11.cloned.1.call-start = ((), (), s32[]{:S(2)}) async-start(), calls=%async_computation.18 | async-start | bytes 11796480 | tf_op jit(solution)/shard_map/psum | solution.py:184
  508.2 8.9 copy-start.12
  508.3 8.8 copy-start.16
  508.3 273.7 %reduce-scatter.17.cloned.1.call-start = ((), (), s32[]{:S(2)}) async-start(), calls=%async_computation.16 | async-start | bytes 2457600 | tf_op jit(solution)/shard_map/reduce_scatter | solution.py:254
  587.2 196.5 %reduce-scatter.9.cloned.1.call-start = ((), (), s32[]{:S(2)}) async-start(), calls=%async_computation.10 | async-start | bytes 2457600 | tf_op jit(solution)/shard_map/reduce_scatter | solution.py:254
  657.8 129.3 %reduce-scatter.13.cloned.1.call-start = ((), (), s32[]{:S(2)}) async-start(), calls=%async_computation.13 | async-start | bytes 2457600 | tf_op jit(solution)/shard_map/reduce_scatter | solution.py:254
  718.9 12.8 %copy-start.74 = (bf16[1280,1,192]{0,2,1:T(8,128)(2,1)}, bf16[1280,1,192]{0,2,1:T(8,128)(2,1)S(1)}, u32[]{:S(2)}) copy-start(bf16[1280,1,192]{0,2,1:T(8,128)(2,1)S(1)} %stack_reshape.39) | copy-start | bytes 1474564
  720.4 11.4 %copy-start.72 = (bf16[1280,3,64]{0,2,1:T(8,128)(2,1)}, bf16[1280,3,64]{0,2,1:T(8,128)(2,1)S(1)}, u32[]{:S(2)}) copy-start(bf16[1280,3,64]{0,2,1:T(8,128)(2,1)S(1)} %convert.53) | copy-start | bytes 1474564
  724.4 252.8 %all-reduce.9.cloned.1.call-start = ((), (), s32[]{:S(2)}) async-start(), calls=%async_computation.17 | async-start | bytes 14155776 | tf_op jit(solution)/shard_map/psum | solution.py:273
  757.0 26.8 %copy-start.51 = (f32[320,768]{1,0:T(8,128)S(1)}, f32[320,768]{1,0:T(8,128)}, u32[]{:S(2)}) copy-start(f32[320,768]{1,0:T(8,128)} %copy-done.50) | copy-start | bytes 2949124
  757.0 26.8 %copy-start.161 = (f32[320]{0:T(512)S(1)}, f32[320]{0:T(512)}, u32[]{:S(2)}) copy-start(f32[320]{0:T(512)} %dynamic-slice.26) | copy-start | bytes 3844
  757.5 29.6 %copy-start.49 = (f32[320,768]{1,0:T(8,128)S(1)}, f32[320,768]{1,0:T(8,128)}, u32[]{:S(2)}) copy-start(f32[320,768]{1,0:T(8,128)} %copy-done.48) | copy-start | bytes 2949124
  757.5 29.6 %copy-start.160 = (f32[320]{0:T(512)S(1)}, f32[320]{0:T(512)}, u32[]{:S(2)}) copy-start(f32[320]{0:T(512)} %dynamic-slice.22) | copy-start | bytes 3844
  783.8 48.1 %copy-start.53 = (f32[320,768]{1,0:T(8,128)S(1)}, f32[320,768]{1,0:T(8,128)}, u32[]{:S(2)}) copy-start(f32[320,768]{1,0:T(8,128)} %copy-done.52) | copy-start | bytes 2949124
  783.8 48.1 %copy-start.162 = (f32[320]{0:T(512)S(1)}, f32[320]{0:T(512)}, u32[]{:S(2)}) copy-start(f32[320]{0:T(512)} %dynamic-slice.24) | copy-start | bytes 3844
  787.1 46.4 %copy-start.90 = (bf16[1,320,768]{2,1,0:T(8,128)(2,1)S(1)}, bf16[1,320,768]{2,1,0:T(8,128)(2,1)}, u32[]{:S(2)}) copy-start(bf16[1,320,768]{2,1,0:T(8,128)(2,1)} %get-tuple-element.739) | copy-start | bytes 1474564
  787.1 44.8 %copy-start.84 = (bf16[320,768]{1,0:T(8,128)(2,1)S(1)}, bf16[320,768]{1,0:T(8,128)(2,1)}, u32[]{:S(2)}) copy-start(bf16[320,768]{1,0:T(8,128)(2,1)} %reduce-scatter.13.cloned.1.call-done) | copy-start | bytes 1474564
  (187 other events, 659.8 us)
Sparse Core Ops, SparseCore 0:
  198.0 112.8 all-reduce.12
  358.8 30.5 reduce-scatter.6
  392.0 30.3 reduce-scatter.10
  425.4 30.3 reduce-scatter.14
  467.1 21.8 all-gather.13
  491.0 21.8 all-gather.9
  514.4 21.8 all-gather.11
  538.8 113.2 all-reduce.10
  654.7 30.5 reduce-scatter.16
  687.7 30.3 reduce-scatter.8
  724.5 30.3 reduce-scatter.12
Sparse Core Ops, SparseCore 1:
  200.5 40.8 all-gather.5
  243.4 39.8 all-gather.7
  744.1 232.9 all-reduce.8
where the time goes:
time: 998 us; the launch traced here: 991 us
  waiting for transfers between devices  293 us (29%)
  matrix products  284 us (28%)
  other arithmetic  175 us (18%)
  blocking collectives  137 us (14%)
  local copies, waits for them, and re-layouts  79.8 us (8%)
  between operations  17.9 us (2%)
    psum x1, waiting for transfers between devices, body(): lax.psum((summed_terms[0], summed_terms[1], summed_terms[2], summed_terms...  141 us
    psum x1, waiting for transfers between devices, body(): lax.psum(jnp.dot(context, out_full, preferred_element_type=jnp.float32).a...  112 us
    convert_element_type x6, other arithmetic, attend_back(): score_grad = (soft_weights * (weight_grad - row_delta)).astype(jnp.bfloat16)  60.8 us
    psum x1, blocking collectives, body(): lax.psum((out_bias_sum, down_bias_sum, first_gain_sum, first_shift_sum, s...  41.7 us
    dot_general x6, matrix products, attend_back(): jnp.einsum('qhc,khc->hqk', query_heads, key_heads, preferred_element_type...  40 us
    dot_general x3, matrix products, body(): jnp.dot(second_normed, up_full, preferred_element_type=jnp.float32)  39.3 us
    all_gather x1, blocking collectives, body(): lax.all_gather(heads_weight, 'wide', axis=0, tiled=True)  38.7 us
    reduce_scatter x3, waiting for transfers between devices, body(): lax.psum_scatter(feed_term(upper_grad, up_full).astype(jnp.bfloat16), 'na...  38 us
  transfers between devices with their start and end apart: 14, of which 4 were waited for; matrix products, arithmetic and copies ran while one was open for 38% of the time, Pallas kernels for 0%

commit v1 on v0

v1 whole, which is shorter than its diff:
```python
import math
from functools import partial

import jax
import jax.numpy as jnp
from jax import lax
from jax.experimental import pallas as pl
from jax.experimental.pallas import tpu as pltpu
from jax.sharding import PartitionSpec as P

HEAD_DIM = 64
MOST = 196
epsilon = 1e-06
bf16 = jnp.bfloat16
f32 = jnp.float32
LOG2E = math.log2(math.e)
VMEM_LIMIT = 60 * 1024 * 1024


def round_up(value, step):
    return -(-value // step) * step


def nt(left, right):
    return lax.dot_general(left, right, (((1,), (1,)), ((), ())), preferred_element_type=f32)


def tn(left, right):
    return lax.dot_general(left, right, (((0,), (0,)), ((), ())), preferred_element_type=f32)


def nn(left, right):
    return jnp.dot(left, right, preferred_element_type=f32)


def params():
    return pltpu.CompilerParams(
        dimension_semantics=("arbitrary",), vmem_limit_bytes=VMEM_LIMIT
    )


def cost(flops, transcendentals, moved):
    return pl.CostEstimate(
        flops=int(flops), transcendentals=int(transcendentals), bytes_accessed=int(moved)
    )


def full(shape):
    return pl.BlockSpec(shape, lambda *a: (0,) * len(shape))


def per_micro(shape):
    return pl.BlockSpec((1,) + shape, lambda m, *a: (m,) + (0,) * len(shape))


def stack_heads(rows, heads):
    lane = lax.broadcasted_iota(jnp.int32, rows.shape, 1) // HEAD_DIM
    zero = jnp.zeros_like(rows)
    return jnp.concatenate([jnp.where(lane == h, rows, zero) for h in range(heads)], axis=0)


def unstack_heads(stacked, heads):
    rows = stacked.shape[0] // heads
    lane = lax.broadcasted_iota(jnp.int32, (rows, stacked.shape[1]), 1) // HEAD_DIM
    out = stacked[:rows]
    for h in range(1, heads):
        out = jnp.where(lane == h, stacked[h * rows : (h + 1) * rows], out)
    return out


def attend_kernel(own, heads, groups, first, off_ref, *refs):
    count = len(groups)
    x_ref, b_ref, bnd_ref = refs[:3]
    w_refs = refs[3 : 3 + count]
    rest = refs[3 + count + (0 if first else 1) :]
    mixed_ref = rest[0]
    off = pl.multiple_of(off_ref[0], 16)
    win = x_ref.shape[1]
    cols = heads * HEAD_DIM
    xw = x_ref[0]
    xo = x_ref[0, pl.ds(off, own), :]
    place = lax.broadcasted_iota(jnp.int32, (win, heads * own), 0)
    keep = (place >= bnd_ref[0, 0:1]) & (place < bnd_ref[0, 1:2])
    mixed = None if first else refs[3 + count][0]
    for i in range(count):
        q_ref, k_ref, v_ref, o_ref, l_ref = rest[1 + 5 * i : 6 + 5 * i]
        w = w_refs[i]
        both = nn(xw, w[:, : 2 * cols])
        k = both[:, :cols].astype(bf16)
        v = (both[:, cols:] + b_ref[groups[i], 1:2]).astype(bf16)
        q = (nn(xo, w[:, 2 * cols : 3 * cols]) + b_ref[groups[i], 0:1]).astype(bf16)
        q_ref[0] = q
        k_ref[0] = k
        v_ref[0] = v
        qs = stack_heads(q, heads)
        scores = nt(k, qs) * (HEAD_DIM**-0.5 * LOG2E)
        scores = jnp.where(keep, scores, -1e30)
        top = jnp.max(scores, axis=0, keepdims=True)
        weights = jnp.exp2(scores - top)
        total = jnp.sum(weights, axis=0, keepdims=True)
        out = tn(v, weights.astype(bf16)) * (1.0 / total)
        out = unstack_heads(out.T, heads).astype(bf16)
        o_ref[0] = out
        l_ref[0] = top + jnp.log2(total)
        part = nt(out, w[:, 3 * cols :])
        mixed = part if mixed is None else mixed + part
    mixed_ref[0] = mixed


def attend(off, x_win, pieces, bias, bounds, own, groups, mixed):
    micro, win, width = x_win.shape
    cols = pieces[0].shape[1] // 4
    heads = cols // HEAD_DIM
    stacked = heads * own
    count = len(groups)
    first = mixed is None
    shapes = [jax.ShapeDtypeStruct((micro, own, width), f32)]
    specs = [per_micro((own, width))]
    for _ in groups:
        for rows in (own, win, win, own):
            shapes.append(jax.ShapeDtypeStruct((micro, rows, cols), bf16))
            specs.append(per_micro((rows, cols)))
        shapes.append(jax.ShapeDtypeStruct((micro, 1, stacked), f32))
        specs.append(per_micro((1, stacked)))
    args = [x_win, bias, bounds] + list(pieces)
    in_specs = [per_micro((win, width)), full(bias.shape), per_micro((2, stacked))]
    in_specs += [full((width, 4 * cols))] * count
    if not first:
        args.append(mixed)
        in_specs.append(per_micro((own, width)))
    result = pl.pallas_call(
        partial(attend_kernel, own, heads, groups, first),
        grid_spec=pltpu.PrefetchScalarGridSpec(
            num_scalar_prefetch=1, grid=(micro,), in_specs=in_specs, out_specs=specs
        ),
        out_shape=shapes,
        compiler_params=params(),
        cost_estimate=cost(
            count * micro * 2 * (win * width * cols * 3 + 8 * stacked * win * HEAD_DIM),
            count * micro * stacked * win,
            micro * win * width * 2 + count * 4 * width * cols * 2,
        ),
        name="attend",
    )(off, *args)
    return result[0], [tuple(result[1 + 5 * i : 6 + 5 * i]) for i in range(count)]


def attend_back_kernel(own, heads, count, first, off_ref, *refs):
    x_ref, mg_ref, bnd_ref = refs[:3]
    w_refs = refs[3 : 3 + count]
    saved = refs[3 + count : 3 + 6 * count]
    at = 3 + 6 * count
    in_ref = None if first else refs[at]
    rest = refs[at + (0 if first else 1) :]
    dn_ref = rest[0]
    acc_refs = rest[1 + 2 * count :]
    off = pl.multiple_of(off_ref[0], 16)
    win = x_ref.shape[1]
    cols = heads * HEAD_DIM
    scale = HEAD_DIM**-0.5
    step = pl.program_id(0)
    mg = mg_ref[0]
    xw = x_ref[0]
    xt = xw.T
    xot = x_ref[0, pl.ds(off, own), :].T
    mgt = mg.T
    place = lax.broadcasted_iota(jnp.int32, (win, heads * own), 0)
    keep = (place >= bnd_ref[0, 0:1]) & (place < bnd_ref[0, 1:2])
    dn = None if first else in_ref[0]
    dn_own = None
    for i in range(count):
        w = w_refs[i]
        q_ref, k_ref, v_ref, o_ref, l_ref = saved[5 * i : 5 * i + 5]
        dw_ref, db_ref = rest[1 + 2 * i : 3 + 2 * i]
        acc_ref = acc_refs[i]
        k, v, o = k_ref[0], v_ref[0], o_ref[0]
        g = nn(mg, w[:, 3 * cols :]).astype(bf16)
        qs = stack_heads(q_ref[0], heads)
        gs = stack_heads(g, heads)
        both = gs.astype(f32) * jnp.concatenate([o.astype(f32)] * heads, axis=0)
        delta = lax.dot_general(
            jnp.ones((8, both.shape[1]), f32), both, (((1,), (1,)), ((), ())),
            precision=lax.Precision.HIGHEST, preferred_element_type=f32,
        )[0:1]
        scores = nt(k, qs) * (scale * LOG2E) - l_ref[0]
        weights = jnp.exp2(jnp.where(keep, scores, -1e30))
        slope = (weights * (nt(v, gs) - delta)).astype(bf16)
        low = weights.astype(bf16)
        dq = (unstack_heads(tn(k, slope).T, heads) * scale).astype(bf16)
        dkv = jnp.concatenate([nn(slope, qs) * scale, nn(low, gs)], axis=1).astype(bf16)
        part = nt(dkv, w[:, : 2 * cols])
        dn = part if dn is None else dn + part
        part = nt(dq, w[:, 2 * cols : 3 * cols])
        dn_own = part if dn_own is None else dn_own + part
        left = nn(xt, dkv)
        right = jnp.concatenate([nn(xot, dq), nn(mgt, o)], axis=1)
        sums = jnp.concatenate(
            [
                jnp.sum(dkv.astype(f32), axis=0, keepdims=True),
                jnp.sum(jnp.concatenate([dq, dq], axis=1).astype(f32), axis=0, keepdims=True),
            ],
            axis=1,
        )

        @pl.when(step == 0)
        def _():
            acc_ref[:, : 2 * cols] = left
            acc_ref[:, 2 * cols :] = right
            db_ref[...] = sums

        @pl.when(step > 0)
        def _():
            acc_ref[:, : 2 * cols] += left
            acc_ref[:, 2 * cols :] += right
            db_ref[...] += sums

        @pl.when(step == pl.num_programs(0) - 1)
        def _():
            dw_ref[...] = acc_ref[...].astype(bf16)

    dn_ref[0] = dn
    dn_ref[0, pl.ds(off, own), :] += dn_own


def attend_back(off, x_win, mixed_grad, pieces, saved, bounds, grad_in):
    micro, win, width = x_win.shape
    own = mixed_grad.shape[1]
    cols = pieces[0].shape[1] // 4
    heads = cols // HEAD_DIM
    stacked = heads * own
    count = len(pieces)
    first = grad_in is None
    args = [x_win, mixed_grad, bounds] + list(pieces)
    in_specs = [per_micro((win, width)), per_micro((own, width)), per_micro((2, stacked))]
    in_specs += [full((width, 4 * cols))] * count
    for one in saved:
        args += list(one)
        in_specs += [per_micro((rows, cols)) for rows in (own, win, win, own)]
        in_specs.append(per_micro((1, stacked)))
    if not first:
        args.append(grad_in)
        in_specs.append(per_micro((win, width)))
    shapes = [jax.ShapeDtypeStruct((micro, win, width), f32)]
    specs = [per_micro((win, width))]
    for _ in pieces:
        shapes += [
            jax.ShapeDtypeStruct((width, 4 * cols), bf16),
            jax.ShapeDtypeStruct((1, 4 * cols), f32),
        ]
        specs += [full((width, 4 * cols)), full((1, 4 * cols))]
    result = pl.pallas_call(
        partial(attend_back_kernel, own, heads, count, first),
        grid_spec=pltpu.PrefetchScalarGridSpec(
            num_scalar_prefetch=1,
            grid=(micro,),
            in_specs=in_specs,
            out_specs=specs,
            scratch_shapes=[pltpu.VMEM((width, 4 * cols), f32)] * count,
        ),
        out_shape=shapes,
        compiler_params=params(),
        cost_estimate=cost(
            count * micro * (40 * stacked * win * HEAD_DIM + 12 * win * width * cols),
            count * micro * stacked * win,
            micro * (10 * win) * width + count * 4 * width * cols * 4,
        ),
        name="attend_back",
    )(off, *args)
    return result[0], list(result[1::2]), list(result[2::2])


def feed_kernel(chunks, count, first, *refs):
    x_ref, g_ref = refs[:2]
    u_refs = refs[2 : 2 + count]
    d_refs = refs[2 + count : 2 + 2 * count]
    b_refs = refs[2 + 2 * count : 2 + 3 * count]
    at = 2 + 3 * count
    if not first:
        fi_ref, ni_ref = refs[at : at + 2]
        at = at + 2
    f_ref, n_ref = refs[at : at + 2]
    outs = refs[at + 2 : at + 2 + 3 * count]
    act_ref, ug_ref, xt_ref, gt_ref = refs[at + 2 + 3 * count :]
    rows = x_ref.shape[0]
    step = rows // chunks
    xt_ref[...] = x_ref[...].T
    gt_ref[...] = g_ref[...].T
    for i in range(count):
        u_ref, d_ref, b_ref = u_refs[i], d_refs[i], b_refs[i]
        du_ref, dd_ref, db_ref = outs[3 * i : 3 * i + 3]
        total = jnp.zeros((1, b_ref.shape[1]), f32)
        for c in range(chunks):
            rows_at = pl.ds(c * step, step)
            upper = nn(x_ref[rows_at, :], u_ref[...]) + b_ref[...]
            phi = 0.5 + 0.5 * lax.erf(upper * math.sqrt(0.5))
            active = (upper * phi).astype(bf16)
            bell = jnp.exp2(upper * upper * (-0.5 * LOG2E)) * (1.0 / math.sqrt(2.0 * math.pi))
            slope = phi + upper * bell
            grad = (nn(g_ref[rows_at, :], d_ref[...]) * slope).astype(bf16)
            act_ref[rows_at, :] = active
            ug_ref[rows_at, :] = grad
            total = total + jnp.sum(grad.astype(f32), axis=0, keepdims=True)
            feed = nt(active, d_ref[...])
            back = nt(grad, u_ref[...])
            if i > 0:
                feed = feed + f_ref[rows_at, :]
                back = back + n_ref[rows_at, :]
            elif not first:
                feed = feed + fi_ref[rows_at, :]
                back = back + ni_ref[rows_at, :]
            f_ref[rows_at, :] = feed
            n_ref[rows_at, :] = back
        db_ref[...] = total
        dd_ref[...] = nn(gt_ref[...], act_ref[...]).astype(bf16)
        du_ref[...] = nn(xt_ref[...], ug_ref[...]).astype(bf16)


def feed_part(x2, grad, ups, downs, biases, before):
    rows, width = x2.shape
    hidden = ups[0].shape[1]
    count = len(ups)
    first = before is None
    args = [x2, grad] + list(ups) + list(downs) + list(biases)
    aliases = {}
    if not first:
        aliases = {len(args): 0, len(args) + 1: 1}
        args += list(before)
    whole = pl.BlockSpec(memory_space=pltpu.VMEM)
    shapes = [jax.ShapeDtypeStruct((rows, width), f32)] * 2
    for _ in ups:
        shapes += [
            jax.ShapeDtypeStruct((width, hidden), bf16),
            jax.ShapeDtypeStruct((width, hidden), bf16),
            jax.ShapeDtypeStruct((1, hidden), f32),
        ]
    result = pl.pallas_call(
        partial(feed_kernel, 4, count, first),
        in_specs=[whole] * len(args),
        out_specs=[whole] * len(shapes),
        out_shape=shapes,
        scratch_shapes=[
            pltpu.VMEM((rows, hidden), bf16),
            pltpu.VMEM((rows, hidden), bf16),
            pltpu.VMEM((width, rows), bf16),
            pltpu.VMEM((width, rows), bf16),
        ],
        input_output_aliases=aliases,
        compiler_params=pltpu.CompilerParams(vmem_limit_bytes=VMEM_LIMIT),
        cost_estimate=cost(
            count * 12 * rows * width * hidden,
            count * 2 * rows * hidden,
            16 * rows * width + count * 8 * width * hidden,
        ),
        name="feed_part",
    )(*args)
    return tuple(result[:2]), list(result[2::3]), list(result[3::3]), list(result[4::3])


def norm_parts(values_in):
    center = jnp.mean(values_in, axis=-1, keepdims=True)
    shifted = values_in - center
    inverse = lax.rsqrt(jnp.mean(shifted * shifted, axis=-1, keepdims=True) + epsilon)
    return (shifted * inverse, inverse)


def norm_back(grad_in, unit_rows, inverse, gain_row):
    scaled = grad_in * gain_row
    return inverse * (
        scaled
        - jnp.mean(scaled, axis=-1, keepdims=True)
        - unit_rows * jnp.mean(scaled * unit_rows, axis=-1, keepdims=True)
    )


def swap(values_in, axis, bit):
    size = lax.axis_size(axis)
    return lax.ppermute(values_in, axis, [(i, i ^ bit) for i in range(size)])


def shift(values_in, axis, step):
    size = lax.axis_size(axis)
    pairs = [(i, i + step) for i in range(size) if 0 <= i + step < size]
    return lax.ppermute(values_in, axis, pairs)


def wide_bits(size):
    bits = []
    bit = size // 2
    while bit:
        bits.append(bit)
        bit //= 2
    return bits


def bit_of(axis, bit):
    return (lax.axis_index(axis) & bit) != 0


def join(mine, other, is_high, axis):
    low = jnp.where(is_high, other, mine)
    high = jnp.where(is_high, mine, other)
    return jnp.stack([low, high], axis=axis)


def widen(blocks, other, bit):
    pair = join(blocks, other, bit_of("wide", bit), 1)
    return pair.reshape((-1,) + blocks.shape[1:])


def gather_pieces(shard, far_first):
    bits = wide_bits(lax.axis_size("wide"))
    blocks = shard[None]
    for bit in bits[:-1]:
        blocks = widen(blocks, swap(blocks, "wide", bit), bit)
    last = bits[-1]
    if far_first:
        far = swap(blocks, "narrow", 2)
        mine = widen(blocks, swap(blocks, "wide", last), last)
        far = widen(far, swap(far, "wide", last), last)
    else:
        mine = widen(blocks, swap(blocks, "wide", last), last)
        far = swap(mine, "narrow", 2)
    mine = mine.reshape(-1, shard.shape[1])
    far = far.reshape(-1, shard.shape[1])
    return [mine, swap(mine, "narrow", 1), far, swap(far, "narrow", 1)]


def gather_narrow(piece):
    far = swap(piece, "narrow", 2)
    return [piece, swap(piece, "narrow", 1), far, swap(far, "narrow", 1)]


def add_low(left, right):
    return (left.astype(f32) + right.astype(f32)).astype(bf16)


def halve(values_in, axis, bit):
    half = values_in.shape[0] // 2
    high = bit_of(axis, bit).astype(jnp.int32)
    keep = lax.dynamic_slice_in_dim(values_in, high * half, half, 0)
    give = lax.dynamic_slice_in_dim(values_in, (1 - high) * half, half, 0)
    return keep, swap(give, axis, bit)


def spread(part):
    for bit in wide_bits(lax.axis_size("wide")):
        other = swap(part, "wide", bit)
        part = join(part, other, bit_of("wide", bit), 0).reshape((-1,) + part.shape[1:])
    return part


def reduce_pair(near_part, given_part):
    return add_low(near_part, swap(given_part, "narrow", 1))


def reduce_rest(near, far, narrow_last):
    bits = list(reversed(wide_bits(lax.axis_size("wide"))))
    if narrow_last:
        keep, other = halve(near, "wide", bits[0])
        far_keep, far_other = halve(far, "wide", bits[0])
        far = add_low(far_keep, far_other)
        near = add_low(keep, other)
        bits = bits[1:]
    mine = add_low(near, swap(far, "narrow", 2))
    if narrow_last:
        bits = list(bits)
    for bit in bits:
        keep, other = halve(mine, "wide", bit)
        mine = add_low(keep, other)
    return spread(mine)


def reduce_everywhere(values_in):
    for bit in wide_bits(lax.axis_size("wide")):
        values_in = values_in + swap(values_in, "wide", bit)
    for bit in wide_bits(lax.axis_size("narrow")):
        values_in = values_in + swap(values_in, "narrow", bit)
    return values_in


def body(
    tokens, image_lengths, heads_weight, heads_bias, out_weight, out_bias, up_weight, up_bias,
    down_weight, down_bias, first_gain, first_shift, second_gain, second_shift, mixer_scale,
    feed_scale, cotangent,
):
    micro, row_count, width = tokens.shape
    narrow_size = lax.axis_size("narrow")
    narrow_at = lax.axis_index("narrow")
    own = row_count // narrow_size
    cols = heads_weight.shape[2]
    heads = cols // HEAD_DIM
    rows = micro * own
    halo = round_up(MOST - 1, 16)
    window = min(row_count, round_up(own + 2 * halo, 128))
    lead = round_up((window - own) // 2, 16)
    start = jnp.clip(narrow_at * own - lead, 0, row_count - window)
    off = narrow_at * own - start
    offset = off.reshape(1).astype(jnp.int32)

    shard_heads = jnp.concatenate(
        [heads_weight[:, 1], heads_weight[:, 2], heads_weight[:, 0], out_weight.T], axis=1
    )
    heads_pieces = gather_pieces(shard_heads, False)
    bias_pieces = gather_narrow(
        jnp.concatenate([heads_bias.reshape(-1), up_bias]).reshape(1, -1)
    )
    up_pieces = gather_pieces(up_weight, True)
    down_pieces = gather_pieces(down_weight.T, False)
    qv_bias = jnp.stack([b[0, : 2 * cols].reshape(2, cols) for b in bias_pieces])
    up_biases = [b[:, 2 * cols :] for b in bias_pieces]

    ends = jnp.cumsum(image_lengths[:, 0], axis=1)
    places = narrow_at * own + jnp.arange(own, dtype=jnp.int32)
    passed = ends[:, :, None] <= places[None, None, :]
    first_key = jnp.max(jnp.where(passed, ends[:, :, None], 0), axis=1) - start
    last_key = jnp.min(jnp.where(passed, row_count, ends[:, :, None]), axis=1) - start
    bounds = jnp.tile(jnp.stack([first_key, last_key], axis=1), (1, 1, heads)).astype(jnp.int32)

    token_window = lax.dynamic_slice_in_dim(tokens, start, window, 1).astype(f32)
    window_normed = (norm_parts(token_window)[0] * first_gain + first_shift).astype(bf16)
    output_grad = lax.dynamic_slice_in_dim(cotangent, narrow_at * own, own, 1)
    output_grad = output_grad.reshape(rows, width).astype(f32)
    feed_grad = (feed_scale * output_grad).astype(bf16)
    token_rows = lax.dynamic_slice_in_dim(tokens, narrow_at * own, own, 1)
    token_rows = token_rows.reshape(rows, width).astype(f32)

    mixed, near_saved = attend(
        offset, window_normed, heads_pieces[:2], qv_bias, bounds, own, (0, 1), None
    )
    mixed, far_saved = attend(
        offset, window_normed, heads_pieces[2:], qv_bias, bounds, own, (2, 3), mixed
    )
    branch = mixed.reshape(rows, width) + out_bias
    middle = token_rows + mixer_scale * branch
    second_unit, second_inverse = norm_parts(middle)
    second_normed = (second_unit * second_gain + second_shift).astype(bf16)

    sums, far_up, far_down, far_bias = feed_part(
        second_normed, feed_grad, up_pieces[2:], down_pieces[2:], up_biases[2:], None
    )
    far_down_sum = reduce_pair(*far_down)
    far_up_sum = reduce_pair(*far_up)
    sums, near_up, near_down, near_bias = feed_part(
        second_normed, feed_grad, up_pieces[:2], down_pieces[:2], up_biases[:2], sums
    )
    feed, second_normed_grad = sums
    up_bias_parts = near_bias + far_bias
    down_total = reduce_rest(reduce_pair(*near_down), far_down_sum, False)
    up_total = reduce_rest(reduce_pair(*near_up), far_up_sum, True)

    feed_branch = feed + down_bias
    layer_own = (middle + feed_scale * feed_branch).astype(bf16).reshape(micro, own, width)
    y_high, core_high = bit_of("narrow", 2), bit_of("narrow", 1)
    layer_far = swap(layer_own, "narrow", 2)
    layer_near = join(layer_own, swap(layer_own, "narrow", 1), core_high, 1)
    layer_far = join(layer_far, swap(layer_far, "narrow", 1), core_high, 1)
    layer_out = join(layer_near, layer_far, y_high, 1).reshape(micro, row_count, width)

    feed_scale_sum = jnp.sum(output_grad * feed_branch, axis=0)
    down_bias_sum = feed_scale * jnp.sum(output_grad, axis=0)
    second_gain_sum = jnp.sum(second_normed_grad * second_unit, axis=0)
    second_shift_sum = jnp.sum(second_normed_grad, axis=0)
    middle_grad = output_grad + norm_back(second_normed_grad, second_unit, second_inverse, second_gain)
    mixer_scale_sum = jnp.sum(middle_grad * branch, axis=0)
    out_bias_sum = mixer_scale * jnp.sum(middle_grad, axis=0)
    mixed_grad = (mixer_scale * middle_grad).astype(bf16).reshape(micro, own, width)

    window_grad, far_heads, far_sums = attend_back(
        offset, window_normed, mixed_grad, heads_pieces[2:], far_saved, bounds, None
    )
    far_heads_sum = reduce_pair(*far_heads)
    window_grad, near_heads, near_sums = attend_back(
        offset, window_normed, mixed_grad, heads_pieces[:2], near_saved, bounds, window_grad
    )
    heads_total = reduce_rest(reduce_pair(*near_heads), far_heads_sum, False)
    head_bias_parts = [
        jnp.concatenate([s[0, 2 * cols : 3 * cols], s[0, cols : 2 * cols]])
        for s in near_sums + far_sums
    ]

    before = lax.dynamic_slice_in_dim(window_grad, jnp.maximum(off - halo, 0), halo, 1)
    after = lax.dynamic_slice_in_dim(
        window_grad, jnp.minimum(off + own, window - halo), halo, 1
    )
    from_left = shift(after.astype(bf16), "narrow", 1).astype(f32)
    from_right = shift(before.astype(bf16), "narrow", -1).astype(f32)
    first_normed_grad = lax.dynamic_slice_in_dim(window_grad, off, own, 1)
    first_normed_grad = (
        first_normed_grad
        + jnp.pad(from_left, ((0, 0), (0, own - halo), (0, 0)))
        + jnp.pad(from_right, ((0, 0), (own - halo, 0), (0, 0)))
    ).reshape(rows, width)

    first_unit, first_inverse = norm_parts(token_rows)
    first_gain_sum = jnp.sum(first_normed_grad * first_unit, axis=0)
    first_shift_sum = jnp.sum(first_normed_grad, axis=0)
    token_grad = (
        middle_grad + norm_back(first_normed_grad, first_unit, first_inverse, first_gain)
    ).astype(bf16).reshape(micro, own, width)

    sums = jnp.stack(
        [out_bias_sum, down_bias_sum, first_gain_sum, first_shift_sum, second_gain_sum,
         second_shift_sum, mixer_scale_sum, feed_scale_sum]
    )
    group_sums = jnp.stack(
        [jnp.concatenate([head_bias_parts[r], up_bias_parts[r][0]]) for r in range(narrow_size)]
    )
    group_sums = jnp.stack([group_sums[r ^ narrow_at] for r in range(narrow_size)])
    packed = jnp.concatenate([sums.reshape(-1), group_sums.reshape(-1)]).reshape(-1, 128)
    packed = reduce_everywhere(packed).reshape(-1)
    sums = packed[: 8 * width].reshape(8, width)
    group_sums = packed[8 * width :].reshape(narrow_size, -1)
    mine = lax.dynamic_slice_in_dim(group_sums, narrow_at, 1, 0)[0]

    heads_grad = jnp.stack(
        [heads_total[:, 2 * cols : 3 * cols], heads_total[:, :cols], heads_total[:, cols : 2 * cols]],
        axis=1,
    ).astype(f32)
    out_grad = heads_total[:, 3 * cols :].T.astype(f32)
    return (
        layer_out, token_grad, heads_grad, mine[: 2 * cols].reshape(2, cols), out_grad, sums[0],
        up_total.astype(f32), mine[2 * cols :], down_total.T.astype(f32), sums[1], sums[2],
        sums[3], sums[4], sums[5], sums[6], sums[7],
    )


def solution(mesh):
    return jax.shard_map(
        body,
        mesh=mesh,
        in_specs=(
            P(None, "wide", None),
            P(None, "wide", None),
            P("wide", None, "narrow"),
            P(None, "narrow"),
            P("narrow", "wide"),
            P(),
            P("wide", "narrow"),
            P("narrow"),
            P("narrow", "wide"),
            P(),
            P(),
            P(),
            P(),
            P(),
            P(),
            P(),
            P(None, "wide", None),
        ),
        out_specs=(
            P(None, "wide", None),
            P(None, ("wide", "narrow"), None),
            P(None, None, "narrow"),
            P(None, "narrow"),
            P("narrow", None),
            P(),
            P(None, "narrow"),
            P("narrow"),
            P("narrow", None),
            P(),
            P(),
            P(),
            P(),
            P(),
            P(),
            P(),
        ),
        check_vma=False,
    )
```

time: 998 us -> 570 us (0.57)
  matrix products: 284 us -> 0 us
  Pallas kernels: 0 us -> 174 us
  blocking collectives: 137 us -> 0 us
  other arithmetic: 175 us -> 72.1 us
  waiting for transfers between devices: 293 us -> 220 us
  starting transfers between devices: 1.92 us -> 61.4 us
  local copies, waits for them, and re-layouts: 79.8 us -> 36.1 us
  between operations: 17.9 us -> 2.11 us
    dot_general x72 -> x0, matrix products: 273 us -> none  [the longest x6 40 us: attend_back(): jnp.einsum('qhc,khc->hqk', query_heads, key_heads, preferred_element_type...]
    psum x3 -> x0, waiting for transfers between devices: 253 us -> none  [the longest x1 141 us: body(): lax.psum((summed_terms[0], summed_terms[1], summed_terms[2], summed_terms...]
    ppermute x0 -> x60, waiting for transfers between devices: none -> 220 us  [the longest x58 218 us: swap(): return lax.ppermute(values_in, axis, [(i, i ^ bit) for i in range(size)])]
    pallas_call x0 -> x6, Pallas kernels: none -> 174 us  [the longest x2 88.2 us: attend_back(): pl.pallas_call(partial(attend_back_kernel, own, heads, count, first), gri...]
    all_gather x2 -> x0, blocking collectives: 71.8 us -> none  [the longest x1 38.7 us: body(): lax.all_gather(heads_weight, 'wide', axis=0, tiled=True)]
    psum x2 -> x0, blocking collectives: 65.5 us -> none  [the longest x1 41.7 us: body(): lax.psum((out_bias_sum, down_bias_sum, first_gain_sum, first_shift_sum, s...]
    ppermute x0 -> x60, starting transfers between devices: none -> 61.4 us  [the longest x58 58.1 us: swap(): return lax.ppermute(values_in, axis, [(i, i ^ bit) for i in range(size)])]
    convert_element_type x16 -> x25, other arithmetic: 83.3 us -> 33.1 us  [the longest x16 11.2 us: add_low(): return (left.astype(f32) + right.astype(f32)).astype(bf16)]
  transfers between devices with their start and end apart: 14 -> 60, of which waited for: 4 -> 26; matrix products, arithmetic and copies ran while one was open for 38% -> 17% of each run, Pallas kernels for 0% -> 31%
where the time goes in v1:
time: 570 us; the launch traced here: 565 us
  waiting for transfers between devices  220 us (39%)
  Pallas kernels  174 us (31%)
  other arithmetic  72.1 us (13%)
  starting transfers between devices  61.4 us (11%)
  local copies, waits for them, and re-layouts  36.1 us (6%)
    ppermute x58, waiting for transfers between devices, swap(): return lax.ppermute(values_in, axis, [(i, i ^ bit) for i in range(size)])  218 us
    pallas_call x2, Pallas kernels, attend_back(): pl.pallas_call(partial(attend_back_kernel, own, heads, count, first), gri...  88.2 us
    ppermute x58, starting transfers between devices, swap(): return lax.ppermute(values_in, axis, [(i, i ^ bit) for i in range(size)])  58.1 us
    pallas_call x2, Pallas kernels, attend(): pl.pallas_call(partial(attend_kernel, own, heads, groups, first), grid_sp...  43.3 us
    pallas_call x2, Pallas kernels, feed_part(): pl.pallas_call(partial(feed_kernel, 4, count, first), in_specs=[whole] *...  42 us
  transfers between devices with their start and end apart: 60, of which 26 were waited for; matrix products, arithmetic and copies ran while one was open for 17% of the time, Pallas kernels for 31%

profile of v1, /device:TPU:0, one launch (start us, length us, event | category | flops | bytes accessed | tf_op | source)
XLA Modules:
  0.0 565.1 jit_solution(15250023934514356130)
XLA Ops:
  2.7 2.6 collective-permute-start.1
  7.1 2.7 collective-permute-start.3
  10.1 2.6 collective-permute-start.9
  13.6 3.0 convert_reduce_fusion
  16.6 3.7 fusion.2
  22.3 2.8 fusion.11.refs_1_
  25.1 5.1 fusion.5.refs_0_
  39.3 6.0 %collective-permute-done.4 = bf16[2,96,768]{2,1,0:T(8,128)(2,1)S(1)} collective-permute-done((bf16[2,96,768]{2,1,0:T(8,128)(2,1)S(1)}, bf16[2,96,768]{2,1,0:T(8,128)(2,1)S(1)}, u32[]{:S(2)}, u32[]{:S(2)}) %collective-permute-start.4) | collective-permute-done | bytes 294944 | tf_op jit(solution)/shard_map/ppermute | solution.py:377
  47.0 10.5 %collective-permute-done.14 = bf16[2,96,768]{2,1,0:T(8,128)(2,1)S(1)} collective-permute-done((bf16[2,96,768]{2,1,0:T(8,128)(2,1)S(1)}, bf16[2,96,768]{2,1,0:T(8,128)(2,1)S(1)}, u32[]{:S(2)}, u32[]{:S(2)}) %collective-permute-start.14) | collective-permute-done | bytes 294944 | tf_op jit(solution)/shard_map/ppermute | solution.py:377
  60.9 13.0 %collective-permute-done.15 = bf16[4,96,768]{2,1,0:T(8,128)(2,1)S(1)} collective-permute-done((bf16[4,96,768]{2,1,0:T(8,128)(2,1)S(1)}, bf16[4,96,768]{2,1,0:T(8,128)(2,1)S(1)}, u32[]{:S(2)}, u32[]{:S(2)}) %collective-permute-start.15) | collective-permute-done | bytes 589856 | tf_op jit(solution)/shard_map/ppermute | solution.py:377
  83.9 2.7 collective-permute-done.11
  87.9 10.0 %collective-permute-done.18 = bf16[4,96,768]{2,1,0:T(8,128)(2,1)S(1)} collective-permute-done((bf16[4,96,768]{2,1,0:T(8,128)(2,1)S(1)}, bf16[4,96,768]{2,1,0:T(8,128)(2,1)S(1)}, u32[]{:S(2)}, u32[]{:S(2)}) %collective-permute-start.18) | collective-permute-done | bytes 589856 | tf_op jit(solution)/shard_map/ppermute | solution.py:377
  97.9 5.0 collective-permute-done.6
  104.7 20.0 %collective-permute-done.20 = bf16[8,96,768]{2,1,0:T(8,128)(2,1)} collective-permute-done((bf16[8,96,768]{2,1,0:T(8,128)(2,1)}, bf16[8,96,768]{2,1,0:T(8,128)(2,1)}, u32[]{:S(2)}, u32[]{:S(2)}) %collective-permute-start.20) | collective-permute-done | bytes 1179680 | tf_op jit(solution)/shard_map/ppermute | solution.py:377
  124.7 20.8 %attend.2 = (f32[3,320,768]{2,1,0:T(8,128)}, bf16[3,320,192]{2,1,0:T(8,128)(2,1)}, bf16[3,768,192]{2,1,0:T(8,128)(2,1)}, bf16[3,768,192]{2,1,0:T(8,128)(2,1)}, b...) custom-call(s32[1]{0:T(128)} %bitcast.1.off_ref, ...), custom_call_target="tpu_custom_call" | custom-call | flops 8606711808 | bytes 5898240 | tf_op jit(solution)/shard_map/attend/pallas_call | solution.py:131
  145.6 22.5 %attend.3 = (f32[3,320,768]{2,1,0:T(8,128)}, bf16[3,320,192]{2,1,0:T(8,128)(2,1)}, bf16[3,768,192]{2,1,0:T(8,128)(2,1)}, bf16[3,768,192]{2,1,0:T(8,128)(2,1)}, b...) custom-call(s32[1]{0:T(128)} %bitcast.1.off_ref, ...), custom_call_target="tpu_custom_call" | custom-call | flops 8606711808 | bytes 5898240 | tf_op jit(solution)/shard_map/attend/pallas_call | solution.py:131
  168.1 3.6 fusion.19
  171.8 2.2 multiply_reduce_fusion.3
  174.1 4.7 add_convert_fusion.1
  178.8 20.1 %feed_part.2 = (f32[960,768]{1,0:T(8,128)}, f32[960,768]{1,0:T(8,128)}, bf16[768,768]{1,0:T(8,128)(2,1)}, bf16[768,768]{1,0:T(8,128)(2,1)}, f32[1,768]{1,0:T(1,1...) custom-call(bf16[960,768]{1,0:T(8,128)(2,1)} %get-tuple-element.128.refs_0_, ...), custom_call_target="tpu_custom_call" | custom-call | flops 13589544960 | bytes 21233664 | tf_op jit(solution)/shard_map/feed_part/pallas_call | solution.py:336
  199.4 22.0 %feed_part.3 = (f32[960,768]{1,0:T(8,128)}, f32[960,768]{1,0:T(8,128)}, bf16[768,768]{1,0:T(8,128)(2,1)}, bf16[768,768]{1,0:T(8,128)(2,1)}, f32[1,768]{1,0:T(1,1...) custom-call(bf16[960,768]{1,0:T(8,128)(2,1)} %get-tuple-element.128., ...), custom_call_target="tpu_custom_call", output_to_operand_aliasing={{0}: (8, {}), {1}: (9, {})} | custom-call | flops 13589544960 | bytes 21233664 | tf_op jit(solution)/shard_map/feed_part/pallas_call | solution.py:336
  221.4 4.1 multiply_reduce_fusion.1
  225.8 5.2 multiply_reduce_fusion
  234.0 43.5 %attend_back.2 = (f32[3,768,768]{2,1,0:T(8,128)}, bf16[768,768]{1,0:T(8,128)(2,1)}, f32[1,768]{1,0:T(1,128)}, bf16[768,768]{1,0:T(8,128)(2,1)}, f32[1,768]{1,0:T(1,128)}) custom-call(s32[1]{0:T(128)} %bitcast.1.off_ref, bf16[3,768,768]{2,1,0:T(8,128)(2,1)} %fusion.5.refs_0_, bf16[3,320,768]{2,1,0:T(8,128)(2,1)} %bitcast.261, s32[3,2,960]{2,1,0:T(2,128)} %tile.10.refs_2_, ...), custom_call_target="tpu_custom_call" | custom-call | flops 19478347776 | bytes 22413312 | tf_op jit(solution)/shard_map/attend_back/pallas_call | solution.py:251
  277.5 44.7 %attend_back.3 = (f32[3,768,768]{2,1,0:T(8,128)}, bf16[768,768]{1,0:T(8,128)(2,1)}, f32[1,768]{1,0:T(1,128)}, bf16[768,768]{1,0:T(8,128)(2,1)}, f32[1,768]{1,0:T(1,128)}) custom-call(s32[1]{0:T(128)} %bitcast.1.off_ref, bf16[3,768,768]{2,1,0:T(8,128)(2,1)} %fusion.5.refs_0_, bf16[3,320,768]{2,1,0:T(8,128)(2,1)} %bitcast.262, s32[3,2,960]{2,1,0:T(2,128)} %tile.10.refs_2_, ...), custom_call_target="tpu_custom_call" | custom-call | flops 19478347776 | bytes 22413312 | tf_op jit(solution)/shard_map/attend_back/pallas_call | solution.py:251
  322.3 2.5 dynamic-slice_convert_fusion.1
  331.4 4.8 fusion.18
  336.7 4.6 collective-permute-done.36
  343.2 9.8 %collective-permute-start.52 = (bf16[768,768]{1,0:T(8,128)(2,1)}, bf16[768,768]{1,0:T(8,128)(2,1)}, u32[]{:S(2)}, u32[]{:S(2)}) collective-permute-start(bf16[768,768]{1,0:T(8,128)(2,1)} %get-tuple-element.111), channel_id=1, source_target_pairs={{0,1},{1,0},{2,3},{3,2},{4,5},{5,4},{6,7},{7,6},{8,9},{9,8},{10,11... | collective-permute-start | bytes 3538952 | tf_op jit(solution)/shard_map/ppermute | solution.py:377
  356.0 2.6 collective-permute-done.38
  360.6 28.2 %collective-permute-done.39 = f32[84,128]{1,0:T(8,128)S(1)} collective-permute-done((f32[84,128]{1,0:T(8,128)S(1)}, f32[84,128]{1,0:T(8,128)S(1)}, u32[]{:S(2)}, u32[]{:S(2)}) %collective-permute-start.39) | collective-permute-done | bytes 43040 | tf_op jit(solution)/shard_map/ppermute | solution.py:377
  393.5 3.9 fusion.10
  400.6 7.2 %collective-permute-done.44 = bf16[384,768]{1,0:T(8,128)(2,1)S(1)} collective-permute-done((bf16[384,768]{1,0:T(8,128)(2,1)S(1)}, bf16[384,768]{1,0:T(8,128)(2,1)S(1)}, u32[]{:S(2)}, u32[]{:S(2)}) %collective-permute-start.44) | collective-permute-done | bytes 589856 | tf_op jit(solution)/shard_map/ppermute | solution.py:377
  419.6 4.2 collective-permute-done.42
  426.5 6.5 %collective-permute-done.45 = bf16[384,768]{1,0:T(8,128)(2,1)S(1)} collective-permute-done((bf16[384,768]{1,0:T(8,128)(2,1)S(1)}, bf16[384,768]{1,0:T(8,128)(2,1)S(1)}, u32[]{:S(2)}, u32[]{:S(2)}) %collective-permute-start.45) | collective-permute-done | bytes 589856 | tf_op jit(solution)/shard_map/ppermute | solution.py:377
  438.0 6.7 %collective-permute-done.46 = bf16[192,768]{1,0:T(8,128)(2,1)S(1)} collective-permute-done((bf16[192,768]{1,0:T(8,128)(2,1)S(1)}, bf16[192,768]{1,0:T(8,128)(2,1)S(1)}, u32[]{:S(2)}, u32[]{:S(2)}) %collective-permute-start.46) | collective-permute-done | bytes 294944 | tf_op jit(solution)/shard_map/ppermute | solution.py:377
  445.6 12.7 %collective-permute-done.53 = bf16[768,768]{1,0:T(8,128)(2,1)S(1)} collective-permute-done((bf16[768,768]{1,0:T(8,128)(2,1)S(1)}, bf16[768,768]{1,0:T(8,128)(2,1)S(1)}, u32[]{:S(2)}, u32[]{:S(2)}) %collective-permute-start.53) | collective-permute-done | bytes 1179680 | tf_op jit(solution)/shard_map/ppermute | solution.py:377
  460.3 21.7 %collective-permute-done.29 = bf16[768,768]{1,0:T(8,128)(2,1)S(1)} collective-permute-done((bf16[768,768]{1,0:T(8,128)(2,1)S(1)}, bf16[768,768]{1,0:T(8,128)(2,1)S(1)}, u32[]{:S(2)}, u32[]{:S(2)}) %collective-permute-start.29) | collective-permute-done | bytes 1179680 | tf_op jit(solution)/shard_map/ppermute | solution.py:377
  485.6 10.6 %collective-permute-done.30 = bf16[384,768]{1,0:T(8,128)(2,1)S(1)} collective-permute-done((bf16[384,768]{1,0:T(8,128)(2,1)S(1)}, bf16[384,768]{1,0:T(8,128)(2,1)S(1)}, u32[]{:S(2)}, u32[]{:S(2)}) %collective-permute-start.30) | collective-permute-done | bytes 589856 | tf_op jit(solution)/shard_map/ppermute | solution.py:377
  499.9 3.0 copy.98
  504.6 2.4 collective-permute-start.32
  507.0 8.1 %collective-permute-done.56 = bf16[96,768]{1,0:T(8,128)(2,1)S(1)} collective-permute-done((bf16[96,768]{1,0:T(8,128)(2,1)S(1)}, bf16[96,768]{1,0:T(8,128)(2,1)S(1)}, u32[]{:S(2)}, u32[]{:S(2)}) %collective-permute-start.56) | collective-permute-done | bytes 147488 | tf_op jit(solution)/shard_map/ppermute | solution.py:377
  515.2 7.8 %collective-permute-done.32 = bf16[96,768]{1,0:T(8,128)(2,1)S(1)} collective-permute-done((bf16[96,768]{1,0:T(8,128)(2,1)S(1)}, bf16[96,768]{1,0:T(8,128)(2,1)S(1)}, u32[]{:S(2)}, u32[]{:S(2)}) %collective-permute-start.32) | collective-permute-done | bytes 147488 | tf_op jit(solution)/shard_map/ppermute | solution.py:377
  523.1 4.4 collective-permute-done.57
  530.0 7.5 %collective-permute-done.58 = bf16[192,768]{1,0:T(8,128)(2,1)S(1)} collective-permute-done((bf16[192,768]{1,0:T(8,128)(2,1)S(1)}, bf16[192,768]{1,0:T(8,128)(2,1)S(1)}, u32[]{:S(2)}, u32[]{:S(2)}) %collective-permute-start.58) | collective-permute-done | bytes 294944 | tf_op jit(solution)/shard_map/ppermute | solution.py:377
  539.2 2.5 collective-permute-done.34
  545.2 8.7 %collective-permute-done.59 = bf16[384,768]{1,0:T(8,128)(2,1)S(1)} collective-permute-done((bf16[384,768]{1,0:T(8,128)(2,1)S(1)}, bf16[384,768]{1,0:T(8,128)(2,1)S(1)}, u32[]{:S(2)}, u32[]{:S(2)}) %collective-permute-start.59) | collective-permute-done | bytes 589856 | tf_op jit(solution)/shard_map/ppermute | solution.py:377
  556.4 5.0 collective-permute-done.35
  (344 shorter events, 104.6 us)
Async XLA Ops:
  2.1 31.7 %collective-permute-start = (f32[1,1152]{1,0:T(1,128)S(1)}, f32[1,1152]{1,0:T(1,128)S(1)}, u32[]{:S(2)}, u32[]{:S(2)}) collective-permute-start(f32[1,1152]{1,0:T(1,128)S(1)} %reshape.469), channel_id=1, source_target_pairs={{0,1},{1,0},{2,3},{3,2},{4,5},{5,4},{6,7},{7,6},{8,9},{9,8},{10,11... | collective-permute-start | bytes 13832 | tf_op jit(solution)/shard_map/ppermute | solution.py:377
  2.7 31.2 %collective-permute-start.1 = (f32[1,1152]{1,0:T(1,128)S(1)}, f32[1,1152]{1,0:T(1,128)S(1)}, u32[]{:S(2)}, u32[]{:S(2)}) collective-permute-start(f32[1,1152]{1,0:T(1,128)S(1)} %reshape.469), channel_id=1, source_target_pairs={{0,2},{1,3},{2,0},{3,1},{4,6},{5,7},{6,4},{7,5},{8,10},{9,11},{10,... | collective-permute-start | bytes 13832 | tf_op jit(solution)/shard_map/ppermute | solution.py:377
  7.1 28.1 %collective-permute-start.3 = (bf16[1,96,768]{2,1,0:T(8,128)(2,1)S(1)}, bf16[1,96,768]{2,1,0:T(8,128)(2,1)S(1)}, u32[]{:S(2)}, u32[]{:S(2)}) collective-permute-start(bf16[1,96,768]{2,1,0:T(8,128)(2,1)S(1)} %maximum_bitcast_fusion.3), channel_id=1, source_target_pairs={{0,16},{4,20},{8,24},{12,28},{16,0},{20,4},{24,8},{28,12},{1,17},{... | collective-permute-start | bytes 442376 | tf_op jit(solution)/shard_map/ppermute | solution.py:377
  9.8 27.3 %collective-permute-start.13 = (bf16[1,96,768]{2,1,0:T(8,128)(2,1)}, bf16[1,96,768]{2,1,0:T(8,128)(2,1)S(1)}, u32[]{:S(2)}, u32[]{:S(2)}) collective-permute-start(bf16[1,96,768]{2,1,0:T(8,128)(2,1)} %bitcast.276), channel_id=1, source_target_pairs={{0,16},{4,20},{8,24},{12,28},{16,0},{20,4},{24,8},{28,12},{1,17},{... | collective-permute-start | bytes 442376 | tf_op jit(solution)/shard_map/ppermute | solution.py:377
  10.1 26.9 %collective-permute-start.9 = (bf16[1,96,768]{2,1,0:T(8,128)(2,1)}, bf16[1,96,768]{2,1,0:T(8,128)(2,1)S(1)}, u32[]{:S(2)}, u32[]{:S(2)}) collective-permute-start(bf16[1,96,768]{2,1,0:T(8,128)(2,1)} %bitcast.277), channel_id=1, source_target_pairs={{0,16},{4,20},{8,24},{12,28},{16,0},{20,4},{24,8},{28,12},{1,17},{... | collective-permute-start | bytes 442376 | tf_op jit(solution)/shard_map/ppermute | solution.py:377
  34.0 41.8 %collective-permute-start.2 = (f32[1,1152]{1,0:T(1,128)S(1)}, f32[1,1152]{1,0:T(1,128)S(1)}, u32[]{:S(2)}, u32[]{:S(2)}) collective-permute-start(f32[1,1152]{1,0:T(1,128)S(1)} %collective-permute-done.1), channel_id=1, source_target_pairs={{0,1},{1,0},{2,3},{3,2},{4,5},{5,4},{6,7},{7,6},{8,9},{9,8},{10,11... | collective-permute-start | bytes 13832 | tf_op jit(solution)/shard_map/ppermute | solution.py:377
  37.1 22.1 %collective-permute-start.10 = (bf16[2,96,768]{2,1,0:T(8,128)(2,1)S(1)}, bf16[2,96,768]{2,1,0:T(8,128)(2,1)S(1)}, u32[]{:S(2)}, u32[]{:S(2)}) collective-permute-start(bf16[2,96,768]{2,1,0:T(8,128)(2,1)S(1)} %maximum_bitcast_fusion.1), channel_id=1, source_target_pairs={{0,8},{4,12},{8,0},{12,4},{16,24},{20,28},{24,16},{28,20},{1,9},{5... | collective-permute-start | bytes 884744 | tf_op jit(solution)/shard_map/ppermute | solution.py:377
  37.7 19.8 %collective-permute-start.14 = (bf16[2,96,768]{2,1,0:T(8,128)(2,1)S(1)}, bf16[2,96,768]{2,1,0:T(8,128)(2,1)S(1)}, u32[]{:S(2)}, u32[]{:S(2)}) collective-permute-start(bf16[2,96,768]{2,1,0:T(8,128)(2,1)S(1)} %maximum_bitcast_fusion.2), channel_id=1, source_target_pairs={{0,8},{4,12},{8,0},{12,4},{16,24},{20,28},{24,16},{28,20},{1,9},{5... | collective-permute-start | bytes 884744 | tf_op jit(solution)/shard_map/ppermute | solution.py:377
  45.4 15.1 %collective-permute-start.5 = (bf16[4,96,768]{2,1,0:T(8,128)(2,1)S(1)}, bf16[4,96,768]{2,1,0:T(8,128)(2,1)S(1)}, u32[]{:S(2)}, u32[]{:S(2)}) collective-permute-start(bf16[4,96,768]{2,1,0:T(8,128)(2,1)S(1)} %bitcast.257), channel_id=1, source_target_pairs={{0,4},{4,0},{8,12},{12,8},{16,20},{20,16},{24,28},{28,24},{1,5},{5... | collective-permute-start | bytes 1769480 | tf_op jit(solution)/shard_map/ppermute | solution.py:377
  57.7 16.3 %collective-permute-start.15 = (bf16[4,96,768]{2,1,0:T(8,128)(2,1)S(1)}, bf16[4,96,768]{2,1,0:T(8,128)(2,1)S(1)}, u32[]{:S(2)}, u32[]{:S(2)}) collective-permute-start(bf16[4,96,768]{2,1,0:T(8,128)(2,1)S(1)} %bitcast.256), channel_id=1, source_target_pairs={{0,4},{4,0},{8,12},{12,8},{16,20},{20,16},{24,28},{28,24},{1,5},{5... | collective-permute-start | bytes 1769480 | tf_op jit(solution)/shard_map/ppermute | solution.py:377
  59.4 18.6 %collective-permute-start.17 = (bf16[4,96,768]{2,1,0:T(8,128)(2,1)S(1)}, bf16[4,96,768]{2,1,0:T(8,128)(2,1)S(1)}, u32[]{:S(2)}, u32[]{:S(2)}) collective-permute-start(bf16[4,96,768]{2,1,0:T(8,128)(2,1)S(1)} %bitcast.254), channel_id=1, source_target_pairs={{0,2},{1,3},{2,0},{3,1},{4,6},{5,7},{6,4},{7,5},{8,10},{9,11},{10,... | collective-permute-start | bytes 1769480 | tf_op jit(solution)/shard_map/ppermute | solution.py:377
  60.0 26.6 %collective-permute-start.11 = (bf16[4,96,768]{2,1,0:T(8,128)(2,1)S(1)}, bf16[4,96,768]{2,1,0:T(8,128)(2,1)S(1)}, u32[]{:S(2)}, u32[]{:S(2)}) collective-permute-start(bf16[4,96,768]{2,1,0:T(8,128)(2,1)S(1)} %bitcast.255), channel_id=1, source_target_pairs={{0,4},{4,0},{8,12},{12,8},{16,20},{20,16},{24,28},{28,24},{1,5},{5... | collective-permute-start | bytes 1769480 | tf_op jit(solution)/shard_map/ppermute | solution.py:377
  60.8 43.4 %collective-permute-start.8 = (bf16[768,768]{1,0:T(8,128)(2,1)S(1)}, bf16[768,768]{1,0:T(8,128)(2,1)}, u32[]{:S(2)}, u32[]{:S(2)}) collective-permute-start(bf16[768,768]{1,0:T(8,128)(2,1)S(1)} %bitcast.264), channel_id=1, source_target_pairs={{0,1},{1,0},{2,3},{3,2},{4,5},{5,4},{6,7},{7,6},{8,9},{9,8},{10,11... | collective-permute-start | bytes 3538952 | tf_op jit(solution)/shard_map/ppermute | solution.py:377
  73.9 28.9 %collective-permute-start.6 = (bf16[8,96,768]{2,1,0:T(8,128)(2,1)S(1)}, bf16[8,96,768]{2,1,0:T(8,128)(2,1)}, u32[]{:S(2)}, u32[]{:S(2)}) collective-permute-start(bf16[8,96,768]{2,1,0:T(8,128)(2,1)S(1)} %bitcast.265), channel_id=1, source_target_pairs={{0,2},{1,3},{2,0},{3,1},{4,6},{5,7},{6,4},{7,5},{8,10},{9,11},{10,... | collective-permute-start | bytes 3538952 | tf_op jit(solution)/shard_map/ppermute | solution.py:377
  75.8 48.9 %collective-permute-start.20 = (bf16[8,96,768]{2,1,0:T(8,128)(2,1)}, bf16[8,96,768]{2,1,0:T(8,128)(2,1)}, u32[]{:S(2)}, u32[]{:S(2)}) collective-permute-start(bf16[8,96,768]{2,1,0:T(8,128)(2,1)} %bitcast.48), channel_id=1, source_target_pairs={{0,2},{1,3},{2,0},{3,1},{4,6},{5,7},{6,4},{7,5},{8,10},{9,11},{10,... | collective-permute-start | bytes 3538952 | tf_op jit(solution)/shard_map/ppermute | solution.py:377
  77.9 19.9 %collective-permute-start.18 = (bf16[4,96,768]{2,1,0:T(8,128)(2,1)S(1)}, bf16[4,96,768]{2,1,0:T(8,128)(2,1)S(1)}, u32[]{:S(2)}, u32[]{:S(2)}) collective-permute-start(bf16[4,96,768]{2,1,0:T(8,128)(2,1)S(1)} %collective-permute-done.17), channel_id=1, source_target_pairs={{0,4},{4,0},{8,12},{12,8},{16,20},{20,16},{24,28},{28,24},{1,5},{5... | collective-permute-start | bytes 1769480 | tf_op jit(solution)/shard_map/ppermute | solution.py:377
  87.9 111.5 %collective-permute-start.12 = (bf16[768,768]{1,0:T(8,128)(2,1)}, bf16[768,768]{1,0:T(8,128)(2,1)}, u32[]{:S(2)}, u32[]{:S(2)}) collective-permute-start(bf16[768,768]{1,0:T(8,128)(2,1)} %bitcast.32.refs_2_), channel_id=1, source_target_pairs={{0,1},{1,0},{2,3},{3,2},{4,5},{5,4},{6,7},{7,6},{8,9},{9,8},{10,11... | collective-permute-start | bytes 3538952 | tf_op jit(solution)/shard_map/ppermute | solution.py:377
  97.9 101.5 %collective-permute-start.16 = (bf16[768,768]{1,0:T(8,128)(2,1)}, bf16[768,768]{1,0:T(8,128)(2,1)}, u32[]{:S(2)}, u32[]{:S(2)}) collective-permute-start(bf16[768,768]{1,0:T(8,128)(2,1)} %bitcast.44.refs_4_), channel_id=1, source_target_pairs={{0,1},{1,0},{2,3},{3,2},{4,5},{5,4},{6,7},{7,6},{8,9},{9,8},{10,11... | collective-permute-start | bytes 3538952 | tf_op jit(solution)/shard_map/ppermute | solution.py:377
  102.9 42.6 %collective-permute-start.7 = (bf16[768,768]{1,0:T(8,128)(2,1)}, bf16[768,768]{1,0:T(8,128)(2,1)}, u32[]{:S(2)}, u32[]{:S(2)}) collective-permute-start(bf16[768,768]{1,0:T(8,128)(2,1)} %bitcast.19.refs_3_), channel_id=1, source_target_pairs={{0,1},{1,0},{2,3},{3,2},{4,5},{5,4},{6,7},{7,6},{8,9},{9,8},{10,11... | collective-permute-start | bytes 3538952 | tf_op jit(solution)/shard_map/ppermute | solution.py:377
  104.2 74.6 %collective-permute-start.19 = (bf16[768,768]{1,0:T(8,128)(2,1)}, bf16[768,768]{1,0:T(8,128)(2,1)}, u32[]{:S(2)}, u32[]{:S(2)}) collective-permute-start(bf16[768,768]{1,0:T(8,128)(2,1)} %bitcast.47.refs_2_), channel_id=1, source_target_pairs={{0,1},{1,0},{2,3},{3,2},{4,5},{5,4},{6,7},{7,6},{8,9},{9,8},{10,11... | collective-permute-start | bytes 3538952 | tf_op jit(solution)/shard_map/ppermute | solution.py:377
  124.7 54.1 %collective-permute-start.21 = (bf16[768,768]{1,0:T(8,128)(2,1)}, bf16[768,768]{1,0:T(8,128)(2,1)}, u32[]{:S(2)}, u32[]{:S(2)}) collective-permute-start(bf16[768,768]{1,0:T(8,128)(2,1)} %bitcast.49.refs_4_), channel_id=1, source_target_pairs={{0,1},{1,0},{2,3},{3,2},{4,5},{5,4},{6,7},{7,6},{8,9},{9,8},{10,11... | collective-permute-start | bytes 3538952 | tf_op jit(solution)/shard_map/ppermute | solution.py:377
  198.9 190.0 %collective-permute-start.43 = (bf16[768,768]{1,0:T(8,128)(2,1)}, bf16[768,768]{1,0:T(8,128)(2,1)}, u32[]{:S(2)}, u32[]{:S(2)}) collective-permute-start(bf16[768,768]{1,0:T(8,128)(2,1)} %get-tuple-element.107), channel_id=1, source_target_pairs={{0,1},{1,0},{2,3},{3,2},{4,5},{5,4},{6,7},{7,6},{8,9},{9,8},{10,11... | collective-permute-start | bytes 3538952 | tf_op jit(solution)/shard_map/ppermute | solution.py:377
  341.3 13.1 %collective-permute-start.37 = (f32[84,128]{1,0:T(8,128)S(1)}, f32[84,128]{1,0:T(8,128)S(1)}, u32[]{:S(2)}, u32[]{:S(2)}) collective-permute-start(f32[84,128]{1,0:T(8,128)S(1)} %fusion.26), channel_id=1, source_target_pairs={{0,8},{4,12},{8,0},{12,4},{16,24},{20,28},{24,16},{28,20},{1,9},{5... | collective-permute-start | bytes 129032 | tf_op jit(solution)/shard_map/ppermute | solution.py:377
  343.2 73.6 %collective-permute-start.52 = (bf16[768,768]{1,0:T(8,128)(2,1)}, bf16[768,768]{1,0:T(8,128)(2,1)}, u32[]{:S(2)}, u32[]{:S(2)}) collective-permute-start(bf16[768,768]{1,0:T(8,128)(2,1)} %get-tuple-element.111), channel_id=1, source_target_pairs={{0,1},{1,0},{2,3},{3,2},{4,5},{5,4},{6,7},{7,6},{8,9},{9,8},{10,11... | collective-permute-start | bytes 3538952 | tf_op jit(solution)/shard_map/ppermute | solution.py:377
  352.9 44.7 %collective-permute-start.41 = (bf16[768,768]{1,0:T(8,128)(2,1)}, bf16[768,768]{1,0:T(8,128)(2,1)}, u32[]{:S(2)}, u32[]{:S(2)}) collective-permute-start(bf16[768,768]{1,0:T(8,128)(2,1)} %get-tuple-element.105), channel_id=1, source_target_pairs={{0,1},{1,0},{2,3},{3,2},{4,5},{5,4},{6,7},{7,6},{8,9},{9,8},{10,11... | collective-permute-start | bytes 3538952 | tf_op jit(solution)/shard_map/ppermute | solution.py:377
  353.0 81.4 %collective-permute-start.22 = (bf16[3,320,768]{2,1,0:T(8,128)(2,1)}, bf16[3,320,768]{2,1,0:T(8,128)(2,1)}, u32[]{:S(2)}, u32[]{:S(2)}) collective-permute-start(bf16[3,320,768]{2,1,0:T(8,128)(2,1)} %bitcast.50), channel_id=1, source_target_pairs={{0,2},{1,3},{2,0},{3,1},{4,6},{5,7},{6,4},{7,5},{8,10},{9,11},{10,... | collective-permute-start | bytes 4423688 | tf_op jit(solution)/shard_map/ppermute | solution.py:377
  358.6 30.2 %collective-permute-start.39 = (f32[84,128]{1,0:T(8,128)S(1)}, f32[84,128]{1,0:T(8,128)S(1)}, u32[]{:S(2)}, u32[]{:S(2)}) collective-permute-start(f32[84,128]{1,0:T(8,128)S(1)} %add.274), channel_id=1, source_target_pairs={{0,2},{1,3},{2,0},{3,1},{4,6},{5,7},{6,4},{7,5},{8,10},{9,11},{10,... | collective-permute-start | bytes 129032 | tf_op jit(solution)/shard_map/ppermute | solution.py:377
  392.0 15.8 %collective-permute-start.44 = (bf16[384,768]{1,0:T(8,128)(2,1)S(1)}, bf16[384,768]{1,0:T(8,128)(2,1)S(1)}, u32[]{:S(2)}, u32[]{:S(2)}) collective-permute-start(bf16[384,768]{1,0:T(8,128)(2,1)S(1)} %constant_dynamic-slice_fusion.6), channel_id=1, source_target_pairs={{0,4},{4,0},{8,12},{12,8},{16,20},{20,16},{24,28},{28,24},{1,5},{5... | collective-permute-start | bytes 1769480 | tf_op jit(solution)/shard_map/ppermute | solution.py:377
  397.4 38.2 %collective-permute-start.24 = (bf16[3,320,768]{2,1,0:T(8,128)(2,1)}, bf16[3,320,768]{2,1,0:T(8,128)(2,1)}, u32[]{:S(2)}, u32[]{:S(2)}) collective-permute-start(bf16[3,320,768]{2,1,0:T(8,128)(2,1)} %bitcast.50), channel_id=1, source_target_pairs={{0,1},{1,0},{2,3},{3,2},{4,5},{5,4},{6,7},{7,6},{8,9},{9,8},{10,11... | collective-permute-start | bytes 4423688 | tf_op jit(solution)/shard_map/ppermute | solution.py:377
  397.6 21.9 %collective-permute-start.28 = (bf16[768,768]{1,0:T(8,128)(2,1)}, bf16[768,768]{1,0:T(8,128)(2,1)}, u32[]{:S(2)}, u32[]{:S(2)}) collective-permute-start(bf16[768,768]{1,0:T(8,128)(2,1)} %get-tuple-element.95), channel_id=1, source_target_pairs={{0,1},{1,0},{2,3},{3,2},{4,5},{5,4},{6,7},{7,6},{8,9},{9,8},{10,11... | collective-permute-start | bytes 3538952 | tf_op jit(solution)/shard_map/ppermute | solution.py:377
  408.6 15.2 %collective-permute-start.42 = (bf16[384,768]{1,0:T(8,128)(2,1)}, bf16[384,768]{1,0:T(8,128)(2,1)}, u32[]{:S(2)}, u32[]{:S(2)}) collective-permute-start(bf16[384,768]{1,0:T(8,128)(2,1)} %constant_dynamic-slice_fusion.7), channel_id=1, source_target_pairs={{0,4},{4,0},{8,12},{12,8},{16,20},{20,16},{24,28},{28,24},{1,5},{5... | collective-permute-start | bytes 1769480 | tf_op jit(solution)/shard_map/ppermute | solution.py:377
  416.7 16.3 %collective-permute-start.45 = (bf16[384,768]{1,0:T(8,128)(2,1)S(1)}, bf16[384,768]{1,0:T(8,128)(2,1)S(1)}, u32[]{:S(2)}, u32[]{:S(2)}) collective-permute-start(bf16[384,768]{1,0:T(8,128)(2,1)S(1)} %add_convert_fusion.12), channel_id=1, source_target_pairs={{0,2},{1,3},{2,0},{3,1},{4,6},{5,7},{6,4},{7,5},{8,10},{9,11},{10,... | collective-permute-start | bytes 1769480 | tf_op jit(solution)/shard_map/ppermute | solution.py:377
  419.5 25.3 %collective-permute-start.51 = (bf16[768,768]{1,0:T(8,128)(2,1)S(1)}, bf16[768,768]{1,0:T(8,128)(2,1)S(1)}, u32[]{:S(2)}, u32[]{:S(2)}) collective-permute-start(bf16[768,768]{1,0:T(8,128)(2,1)S(1)} %copy-done.36), channel_id=1, source_target_pairs={{0,1},{1,0},{2,3},{3,2},{4,5},{5,4},{6,7},{7,6},{8,9},{9,8},{10,11... | collective-permute-start | bytes 3538952 | tf_op jit(solution)/shard_map/ppermute | solution.py:377
  423.8 34.5 %collective-permute-start.53 = (bf16[768,768]{1,0:T(8,128)(2,1)S(1)}, bf16[768,768]{1,0:T(8,128)(2,1)S(1)}, u32[]{:S(2)}, u32[]{:S(2)}) collective-permute-start(bf16[768,768]{1,0:T(8,128)(2,1)S(1)} %add_convert_fusion.3), channel_id=1, source_target_pairs={{0,2},{1,3},{2,0},{3,1},{4,6},{5,7},{6,4},{7,5},{8,10},{9,11},{10,... | collective-permute-start | bytes 3538952 | tf_op jit(solution)/shard_map/ppermute | solution.py:377
  433.0 27.3 %collective-permute-start.27 = (bf16[768,768]{1,0:T(8,128)(2,1)S(1)}, bf16[768,768]{1,0:T(8,128)(2,1)S(1)}, u32[]{:S(2)}, u32[]{:S(2)}) collective-permute-start(bf16[768,768]{1,0:T(8,128)(2,1)S(1)} %copy-done.37), channel_id=1, source_target_pairs={{0,1},{1,0},{2,3},{3,2},{4,5},{5,4},{6,7},{7,6},{8,9},{9,8},{10,11... | collective-permute-start | bytes 3538952 | tf_op jit(solution)/shard_map/ppermute | solution.py:377
  434.4 47.6 %collective-permute-start.29 = (bf16[768,768]{1,0:T(8,128)(2,1)S(1)}, bf16[768,768]{1,0:T(8,128)(2,1)S(1)}, u32[]{:S(2)}, u32[]{:S(2)}) collective-permute-start(bf16[768,768]{1,0:T(8,128)(2,1)S(1)} %add_convert_fusion.8), channel_id=1, source_target_pairs={{0,2},{1,3},{2,0},{3,1},{4,6},{5,7},{6,4},{7,5},{8,10},{9,11},{10,... | collective-permute-start | bytes 3538952 | tf_op jit(solution)/shard_map/ppermute | solution.py:377
  444.7 52.3 %collective-permute-start.23 = (bf16[3,320,768]{2,1,0:T(8,128)(2,1)}, bf16[3,320,768]{2,1,0:T(8,128)(2,1)S(1)}, u32[]{:S(2)}, u32[]{:S(2)}) collective-permute-start(bf16[3,320,768]{2,1,0:T(8,128)(2,1)} %collective-permute-done.22), channel_id=1, source_target_pairs={{0,1},{1,0},{2,3},{3,2},{4,5},{5,4},{6,7},{7,6},{8,9},{9,8},{10,11... | collective-permute-start | bytes 4423688 | tf_op jit(solution)/shard_map/ppermute | solution.py:377
  444.8 14.6 %collective-permute-start.47 = (bf16[96,768]{1,0:T(8,128)(2,1)S(1)}, bf16[96,768]{1,0:T(8,128)(2,1)S(1)}, u32[]{:S(2)}, u32[]{:S(2)}) collective-permute-start(bf16[96,768]{1,0:T(8,128)(2,1)S(1)} %constant_dynamic-slice_fusion.4), channel_id=1, source_target_pairs={{0,16},{4,20},{8,24},{12,28},{16,0},{20,4},{24,8},{28,12},{1,17},{... | collective-permute-start | bytes 442376 | tf_op jit(solution)/shard_map/ppermute | solution.py:377
  458.8 24.9 %collective-permute-start.54 = (bf16[384,768]{1,0:T(8,128)(2,1)S(1)}, bf16[384,768]{1,0:T(8,128)(2,1)S(1)}, u32[]{:S(2)}, u32[]{:S(2)}) collective-permute-start(bf16[384,768]{1,0:T(8,128)(2,1)S(1)} %constant_dynamic-slice_fusion.3), channel_id=1, source_target_pairs={{0,4},{4,0},{8,12},{12,8},{16,20},{20,16},{24,28},{28,24},{1,5},{5... | collective-permute-start | bytes 1769480 | tf_op jit(solution)/shard_map/ppermute | solution.py:377
  459.5 23.6 %collective-permute-start.48 = (bf16[96,768]{1,0:T(8,128)(2,1)S(1)}, bf16[96,768]{1,0:T(8,128)(2,1)S(1)}, u32[]{:S(2)}, u32[]{:S(2)}) collective-permute-start(bf16[96,768]{1,0:T(8,128)(2,1)S(1)} %add_convert_fusion.19), channel_id=1, source_target_pairs={{0,16},{4,20},{8,24},{12,28},{16,0},{20,4},{24,8},{28,12},{1,17},{... | collective-permute-start | bytes 442376 | tf_op jit(solution)/shard_map/ppermute | solution.py:377
  482.5 13.8 %collective-permute-start.30 = (bf16[384,768]{1,0:T(8,128)(2,1)S(1)}, bf16[384,768]{1,0:T(8,128)(2,1)S(1)}, u32[]{:S(2)}, u32[]{:S(2)}) collective-permute-start(bf16[384,768]{1,0:T(8,128)(2,1)S(1)} %constant_dynamic-slice_fusion.14), channel_id=1, source_target_pairs={{0,4},{4,0},{8,12},{12,8},{16,20},{20,16},{24,28},{28,24},{1,5},{5... | collective-permute-start | bytes 1769480 | tf_op jit(solution)/shard_map/ppermute | solution.py:377
  483.2 19.7 %collective-permute-start.49 = (bf16[192,768]{1,0:T(8,128)(2,1)S(1)}, bf16[192,768]{1,0:T(8,128)(2,1)S(1)}, u32[]{:S(2)}, u32[]{:S(2)}) collective-permute-start(bf16[192,768]{1,0:T(8,128)(2,1)S(1)} %bitcast.268), channel_id=1, source_target_pairs={{0,8},{4,12},{8,0},{12,4},{16,24},{20,28},{24,16},{28,20},{1,9},{5... | collective-permute-start | bytes 884744 | tf_op jit(solution)/shard_map/ppermute | solution.py:377
  483.9 19.8 %collective-permute-start.55 = (bf16[192,768]{1,0:T(8,128)(2,1)S(1)}, bf16[192,768]{1,0:T(8,128)(2,1)S(1)}, u32[]{:S(2)}, u32[]{:S(2)}) collective-permute-start(bf16[192,768]{1,0:T(8,128)(2,1)S(1)} %constant_dynamic-slice_fusion.2), channel_id=1, source_target_pairs={{0,8},{4,12},{8,0},{12,4},{16,24},{20,28},{24,16},{28,20},{1,9},{5... | collective-permute-start | bytes 884744 | tf_op jit(solution)/shard_map/ppermute | solution.py:377
  503.1 40.3 %collective-permute-start.50 = (bf16[384,768]{1,0:T(8,128)(2,1)S(1)}, bf16[384,768]{1,0:T(8,128)(2,1)S(1)}, u32[]{:S(2)}, u32[]{:S(2)}) collective-permute-start(bf16[384,768]{1,0:T(8,128)(2,1)S(1)} %bitcast.253), channel_id=1, source_target_pairs={{0,4},{4,0},{8,12},{12,8},{16,20},{20,16},{24,28},{28,24},{1,5},{5... | collective-permute-start | bytes 1769480 | tf_op jit(solution)/shard_map/ppermute | solution.py:377
  504.6 18.4 %collective-permute-start.32 = (bf16[96,768]{1,0:T(8,128)(2,1)S(1)}, bf16[96,768]{1,0:T(8,128)(2,1)S(1)}, u32[]{:S(2)}, u32[]{:S(2)}) collective-permute-start(bf16[96,768]{1,0:T(8,128)(2,1)S(1)} %constant_dynamic-slice_fusion.12), channel_id=1, source_target_pairs={{0,16},{4,20},{8,24},{12,28},{16,0},{20,4},{24,8},{28,12},{1,17},{... | collective-permute-start | bytes 442376 | tf_op jit(solution)/shard_map/ppermute | solution.py:377
  515.1 12.4 %collective-permute-start.57 = (bf16[96,768]{1,0:T(8,128)(2,1)S(1)}, bf16[96,768]{1,0:T(8,128)(2,1)S(1)}, u32[]{:S(2)}, u32[]{:S(2)}) collective-permute-start(bf16[96,768]{1,0:T(8,128)(2,1)S(1)} %add_convert_fusion.18), channel_id=1, source_target_pairs={{0,16},{4,20},{8,24},{12,28},{16,0},{20,4},{24,8},{28,12},{1,17},{... | collective-permute-start | bytes 442376 | tf_op jit(solution)/shard_map/ppermute | solution.py:377
  537.7 16.3 %collective-permute-start.59 = (bf16[384,768]{1,0:T(8,128)(2,1)S(1)}, bf16[384,768]{1,0:T(8,128)(2,1)S(1)}, u32[]{:S(2)}, u32[]{:S(2)}) collective-permute-start(bf16[384,768]{1,0:T(8,128)(2,1)S(1)} %bitcast.258), channel_id=1, source_target_pairs={{0,4},{4,0},{8,12},{12,8},{16,20},{20,16},{24,28},{28,24},{1,5},{5... | collective-permute-start | bytes 1769480 | tf_op jit(solution)/shard_map/ppermute | solution.py:377
  541.8 19.6 %collective-permute-start.35 = (bf16[384,768]{1,0:T(8,128)(2,1)S(1)}, bf16[384,768]{1,0:T(8,128)(2,1)S(1)}, u32[]{:S(2)}, u32[]{:S(2)}) collective-permute-start(bf16[384,768]{1,0:T(8,128)(2,1)S(1)} %bitcast.259), channel_id=1, source_target_pairs={{0,4},{4,0},{8,12},{12,8},{16,20},{20,16},{24,28},{28,24},{1,5},{5... | collective-permute-start | bytes 1769480 | tf_op jit(solution)/shard_map/ppermute | solution.py:377
  (50 other events, 387.9 us)

commit v2 on v1

--- a/solution.py
+++ b/solution.py
@@ -68,8 +68,7 @@
     return out
 
 
-def attend_kernel(own, heads, groups, first, off_ref, *refs):
-    count = len(groups)
+def attend_kernel(own, heads, count, first, off_ref, *refs):
     x_ref, b_ref, bnd_ref = refs[:3]
     w_refs = refs[3 : 3 + count]
     rest = refs[3 + count + (0 if first else 1) :]
@@ -87,8 +86,8 @@
         w = w_refs[i]
         both = nn(xw, w[:, : 2 * cols])
         k = both[:, :cols].astype(bf16)
-        v = (both[:, cols:] + b_ref[groups[i], 1:2]).astype(bf16)
-        q = (nn(xo, w[:, 2 * cols : 3 * cols]) + b_ref[groups[i], 0:1]).astype(bf16)
+        v = (both[:, cols:] + b_ref[i, 1:2]).astype(bf16)
+        q = (nn(xo, w[:, 2 * cols : 3 * cols]) + b_ref[i, 0:1]).astype(bf16)
         q_ref[0] = q
         k_ref[0] = k
         v_ref[0] = v
@@ -107,16 +106,16 @@
     mixed_ref[0] = mixed
 
 
-def attend(off, x_win, pieces, bias, bounds, own, groups, mixed):
+def attend(off, x_win, pieces, bias, bounds, own, mixed):
     micro, win, width = x_win.shape
     cols = pieces[0].shape[1] // 4
     heads = cols // HEAD_DIM
     stacked = heads * own
-    count = len(groups)
+    count = len(pieces)
     first = mixed is None
     shapes = [jax.ShapeDtypeStruct((micro, own, width), f32)]
     specs = [per_micro((own, width))]
-    for _ in groups:
+    for _ in pieces:
         for rows in (own, win, win, own):
             shapes.append(jax.ShapeDtypeStruct((micro, rows, cols), bf16))
             specs.append(per_micro((rows, cols)))
@@ -129,7 +128,7 @@
         args.append(mixed)
         in_specs.append(per_micro((own, width)))
     result = pl.pallas_call(
-        partial(attend_kernel, own, heads, groups, first),
+        partial(attend_kernel, own, heads, count, first),
         grid_spec=pltpu.PrefetchScalarGridSpec(
             num_scalar_prefetch=1, grid=(micro,), in_specs=in_specs, out_specs=specs
         ),
@@ -146,24 +145,20 @@
 
 
 def attend_back_kernel(own, heads, count, first, off_ref, *refs):
-    x_ref, mg_ref, bnd_ref = refs[:3]
-    w_refs = refs[3 : 3 + count]
-    saved = refs[3 + count : 3 + 6 * count]
-    at = 3 + 6 * count
+    xt_ref, xot_ref, mg_ref, mgt_ref, bnd_ref = refs[:5]
+    w_refs = refs[5 : 5 + count]
+    saved = refs[5 + count : 5 + 6 * count]
+    at = 5 + 6 * count
     in_ref = None if first else refs[at]
     rest = refs[at + (0 if first else 1) :]
     dn_ref = rest[0]
     acc_refs = rest[1 + 2 * count :]
     off = pl.multiple_of(off_ref[0], 16)
-    win = x_ref.shape[1]
+    win = xt_ref.shape[2]
     cols = heads * HEAD_DIM
     scale = HEAD_DIM**-0.5
     step = pl.program_id(0)
     mg = mg_ref[0]
-    xw = x_ref[0]
-    xt = xw.T
-    xot = x_ref[0, pl.ds(off, own), :].T
-    mgt = mg.T
     place = lax.broadcasted_iota(jnp.int32, (win, heads * own), 0)
     keep = (place >= bnd_ref[0, 0:1]) & (place < bnd_ref[0, 1:2])
     dn = None if first else in_ref[0]
@@ -192,8 +187,8 @@
         dn = part if dn is None else dn + part
         part = nt(dq, w[:, 2 * cols : 3 * cols])
         dn_own = part if dn_own is None else dn_own + part
-        left = nn(xt, dkv)
-        right = jnp.concatenate([nn(xot, dq), nn(mgt, o)], axis=1)
+        left = nn(xt_ref[0], dkv)
+        right = jnp.concatenate([nn(xot_ref[0], dq), nn(mgt_ref[0], o)], axis=1)
         sums = jnp.concatenate(
             [
                 jnp.sum(dkv.astype(f32), axis=0, keepdims=True),
@@ -222,16 +217,19 @@
     dn_ref[0, pl.ds(off, own), :] += dn_own
 
 
-def attend_back(off, x_win, mixed_grad, pieces, saved, bounds, grad_in):
-    micro, win, width = x_win.shape
+def attend_back(off, xt, xot, mixed_grad, mgt, pieces, saved, bounds, grad_in):
+    micro, width, win = xt.shape
     own = mixed_grad.shape[1]
     cols = pieces[0].shape[1] // 4
     heads = cols // HEAD_DIM
     stacked = heads * own
     count = len(pieces)
     first = grad_in is None
-    args = [x_win, mixed_grad, bounds] + list(pieces)
-    in_specs = [per_micro((win, width)), per_micro((own, width)), per_micro((2, stacked))]
+    args = [xt, xot, mixed_grad, mgt, bounds] + list(pieces)
+    in_specs = [
+        per_micro((width, win)), per_micro((width, own)), per_micro((own, width)),
+        per_micro((width, own)), per_micro((2, stacked)),
+    ]
     in_specs += [full((width, 4 * cols))] * count
     for one in saved:
         args += list(one)
@@ -270,38 +268,36 @@
 
 
 def feed_kernel(chunks, count, first, *refs):
-    x_ref, g_ref = refs[:2]
-    u_refs = refs[2 : 2 + count]
-    d_refs = refs[2 + count : 2 + 2 * count]
-    b_refs = refs[2 + 2 * count : 2 + 3 * count]
-    at = 2 + 3 * count
+    x_ref, g_ref, xt_ref, gt_ref = refs[:4]
+    w_refs = refs[4 : 4 + count]
+    b_refs = refs[4 + count : 4 + 2 * count]
+    at = 4 + 2 * count
     if not first:
         fi_ref, ni_ref = refs[at : at + 2]
         at = at + 2
     f_ref, n_ref = refs[at : at + 2]
-    outs = refs[at + 2 : at + 2 + 3 * count]
-    act_ref, ug_ref, xt_ref, gt_ref = refs[at + 2 + 3 * count :]
+    outs = refs[at + 2 : at + 2 + 2 * count]
+    act_ref, ug_ref = refs[at + 2 + 2 * count :]
     rows = x_ref.shape[0]
     step = rows // chunks
-    xt_ref[...] = x_ref[...].T
-    gt_ref[...] = g_ref[...].T
     for i in range(count):
-        u_ref, d_ref, b_ref = u_refs[i], d_refs[i], b_refs[i]
-        du_ref, dd_ref, db_ref = outs[3 * i : 3 * i + 3]
-        total = jnp.zeros((1, b_ref.shape[1]), f32)
+        w_ref, b_ref = w_refs[i], b_refs[i]
+        dw_ref, db_ref = outs[2 * i : 2 * i + 2]
+        hidden = b_ref.shape[1]
+        total = jnp.zeros((1, hidden), f32)
         for c in range(chunks):
             rows_at = pl.ds(c * step, step)
-            upper = nn(x_ref[rows_at, :], u_ref[...]) + b_ref[...]
+            upper = nn(x_ref[rows_at, :], w_ref[:, :hidden]) + b_ref[...]
             phi = 0.5 + 0.5 * lax.erf(upper * math.sqrt(0.5))
             active = (upper * phi).astype(bf16)
             bell = jnp.exp2(upper * upper * (-0.5 * LOG2E)) * (1.0 / math.sqrt(2.0 * math.pi))
             slope = phi + upper * bell
-            grad = (nn(g_ref[rows_at, :], d_ref[...]) * slope).astype(bf16)
+            grad = (nn(g_ref[rows_at, :], w_ref[:, hidden:]) * slope).astype(bf16)
             act_ref[rows_at, :] = active
             ug_ref[rows_at, :] = grad
             total = total + jnp.sum(grad.astype(f32), axis=0, keepdims=True)
-            feed = nt(active, d_ref[...])
-            back = nt(grad, u_ref[...])
+            feed = nt(active, w_ref[:, hidden:])
+            back = nt(grad, w_ref[:, :hidden])
             if i > 0:
                 feed = feed + f_ref[rows_at, :]
                 back = back + n_ref[rows_at, :]
@@ -311,26 +307,25 @@
             f_ref[rows_at, :] = feed
             n_ref[rows_at, :] = back
         db_ref[...] = total
-        dd_ref[...] = nn(gt_ref[...], act_ref[...]).astype(bf16)
-        du_ref[...] = nn(xt_ref[...], ug_ref[...]).astype(bf16)
-
-
-def feed_part(x2, grad, ups, downs, biases, before):
+        dw_ref[:, :hidden] = nn(xt_ref[...], ug_ref[...]).astype(bf16)
+        dw_ref[:, hidden:] = nn(gt_ref[...], act_ref[...]).astype(bf16)
+
+
+def feed_part(x2, grad, x2t, gradt, pieces, biases, before):
     rows, width = x2.shape
-    hidden = ups[0].shape[1]
-    count = len(ups)
+    hidden = biases[0].shape[1]
+    count = len(pieces)
     first = before is None
-    args = [x2, grad] + list(ups) + list(downs) + list(biases)
+    args = [x2, grad, x2t, gradt] + list(pieces) + list(biases)
     aliases = {}
     if not first:
         aliases = {len(args): 0, len(args) + 1: 1}
         args += list(before)
     whole = pl.BlockSpec(memory_space=pltpu.VMEM)
     shapes = [jax.ShapeDtypeStruct((rows, width), f32)] * 2
-    for _ in ups:
+    for _ in pieces:
         shapes += [
-            jax.ShapeDtypeStruct((width, hidden), bf16),
-            jax.ShapeDtypeStruct((width, hidden), bf16),
+            jax.ShapeDtypeStruct((width, 2 * hidden), bf16),
             jax.ShapeDtypeStruct((1, hidden), f32),
         ]
     result = pl.pallas_call(
@@ -338,12 +333,7 @@
         in_specs=[whole] * len(args),
         out_specs=[whole] * len(shapes),
         out_shape=shapes,
-        scratch_shapes=[
-            pltpu.VMEM((rows, hidden), bf16),
-            pltpu.VMEM((rows, hidden), bf16),
-            pltpu.VMEM((width, rows), bf16),
-            pltpu.VMEM((width, rows), bf16),
-        ],
+        scratch_shapes=[pltpu.VMEM((rows, hidden), bf16), pltpu.VMEM((rows, hidden), bf16)],
         input_output_aliases=aliases,
         compiler_params=pltpu.CompilerParams(vmem_limit_bytes=VMEM_LIMIT),
         cost_estimate=cost(
@@ -353,7 +343,7 @@
         ),
         name="feed_part",
     )(*args)
-    return tuple(result[:2]), list(result[2::3]), list(result[3::3]), list(result[4::3])
+    return tuple(result[:2]), list(result[2::2]), list(result[3::2])
 
 
 def norm_parts(values_in):
@@ -402,27 +392,44 @@
     return jnp.stack([low, high], axis=axis)
 
 
-def widen(blocks, other, bit):
-    pair = join(blocks, other, bit_of("wide", bit), 1)
-    return pair.reshape((-1,) + blocks.shape[1:])
-
-
-def gather_pieces(shard, far_first):
-    bits = wide_bits(lax.axis_size("wide"))
-    blocks = shard[None]
-    for bit in bits[:-1]:
-        blocks = widen(blocks, swap(blocks, "wide", bit), bit)
-    last = bits[-1]
-    if far_first:
-        far = swap(blocks, "narrow", 2)
-        mine = widen(blocks, swap(blocks, "wide", last), last)
-        far = widen(far, swap(far, "wide", last), last)
-    else:
-        mine = widen(blocks, swap(blocks, "wide", last), last)
-        far = swap(mine, "narrow", 2)
-    mine = mine.reshape(-1, shard.shape[1])
-    far = far.reshape(-1, shard.shape[1])
-    return [mine, swap(mine, "narrow", 1), far, swap(far, "narrow", 1)]
+def tie(*values_in):
+    return lax.optimization_barrier(values_in)
+
+
+def far_groups():
+    bits = wide_bits(lax.axis_size("wide"))[:-1]
+    return [bits[i : i + 2] for i in range(0, len(bits), 2)]
+
+
+def offsets(bits):
+    return [
+        sum(bit for i, bit in enumerate(reversed(bits)) if (k >> i) & 1)
+        for k in range(2 ** len(bits))
+    ]
+
+
+def exchange(values_in, bits):
+    return [values_in] + [swap(values_in, "wide", o) for o in offsets(bits)[1:]]
+
+
+def arrange(parts, bits, axis):
+    if not bits:
+        return jnp.expand_dims(parts[0], axis)
+    half = len(parts) // 2
+    low = arrange(parts[:half], bits[1:], axis)
+    high = arrange(parts[half:], bits[1:], axis)
+    is_high = bit_of("wide", bits[0])
+    return jnp.concatenate(
+        [jnp.where(is_high, high, low), jnp.where(is_high, low, high)], axis=axis
+    )
+
+
+def arrange_blocks(parts, bits):
+    return arrange(parts, bits, 1).reshape((-1,) + parts[0].shape[1:])
+
+
+def last_bit():
+    return wide_bits(lax.axis_size("wide"))[-1]
 
 
 def gather_narrow(piece):
@@ -430,44 +437,52 @@
     return [piece, swap(piece, "narrow", 1), far, swap(far, "narrow", 1)]
 
 
-def add_low(left, right):
-    return (left.astype(f32) + right.astype(f32)).astype(bf16)
-
-
-def halve(values_in, axis, bit):
-    half = values_in.shape[0] // 2
-    high = bit_of(axis, bit).astype(jnp.int32)
-    keep = lax.dynamic_slice_in_dim(values_in, high * half, half, 0)
-    give = lax.dynamic_slice_in_dim(values_in, (1 - high) * half, half, 0)
-    return keep, swap(give, axis, bit)
-
-
-def spread(part):
-    for bit in wide_bits(lax.axis_size("wide")):
-        other = swap(part, "wide", bit)
-        part = join(part, other, bit_of("wide", bit), 0).reshape((-1,) + part.shape[1:])
+def add_low(*parts):
+    total = parts[0].astype(f32)
+    for part in parts[1:]:
+        total = total + part.astype(f32)
+    return total.astype(bf16)
+
+
+def cut(values_in, axis, bits):
+    count = 2 ** len(bits)
+    size = values_in.shape[0] // count
+    at = lax.axis_index(axis)
+    places = []
+    for o in offsets(bits):
+        other = at ^ o
+        place = 0
+        for bit in bits:
+            place = 2 * place + ((other & bit) != 0).astype(jnp.int32)
+        places.append(place)
+    return [lax.dynamic_slice_in_dim(values_in, p * size, size, 0) for p in places]
+
+
+def send_cut(parts, bits):
+    return [swap(part, "wide", o) for part, o in zip(parts[1:], offsets(bits)[1:])]
+
+
+def reduce_far(part):
+    for bits in far_groups():
+        parts = cut(part, "wide", bits)
+        part = add_low(parts[0], *send_cut(parts, bits))
     return part
 
 
-def reduce_pair(near_part, given_part):
-    return add_low(near_part, swap(given_part, "narrow", 1))
-
-
-def reduce_rest(near, far, narrow_last):
-    bits = list(reversed(wide_bits(lax.axis_size("wide"))))
-    if narrow_last:
-        keep, other = halve(near, "wide", bits[0])
-        far_keep, far_other = halve(far, "wide", bits[0])
-        far = add_low(far_keep, far_other)
-        near = add_low(keep, other)
-        bits = bits[1:]
-    mine = add_low(near, swap(far, "narrow", 2))
-    if narrow_last:
-        bits = list(bits)
-    for bit in bits:
-        keep, other = halve(mine, "wide", bit)
-        mine = add_low(keep, other)
-    return spread(mine)
+def spread_far(part):
+    for bits in reversed(far_groups()):
+        part = arrange(exchange(part, bits), bits, 0).reshape((-1,) + part.shape[1:])
+    return part
+
+
+def reduce_last(part):
+    parts = cut(part, "wide", [last_bit()])
+    return add_low(parts[0], *send_cut(parts, [last_bit()]))
+
+
+def spread_last(part):
+    bits = [last_bit()]
+    return arrange(exchange(part, bits), bits, 0).reshape((-1,) + part.shape[1:])
 
 
 def reduce_everywhere(values_in):
@@ -497,17 +512,27 @@
     off = narrow_at * own - start
     offset = off.reshape(1).astype(jnp.int32)
 
-    shard_heads = jnp.concatenate(
-        [heads_weight[:, 1], heads_weight[:, 2], heads_weight[:, 0], out_weight.T], axis=1
-    )
-    heads_pieces = gather_pieces(shard_heads, False)
+    hidden = up_weight.shape[1]
+    groups = far_groups()
+
     bias_pieces = gather_narrow(
         jnp.concatenate([heads_bias.reshape(-1), up_bias]).reshape(1, -1)
     )
-    up_pieces = gather_pieces(up_weight, True)
-    down_pieces = gather_pieces(down_weight.T, False)
-    qv_bias = jnp.stack([b[0, : 2 * cols].reshape(2, cols) for b in bias_pieces])
-    up_biases = [b[:, 2 * cols :] for b in bias_pieces]
+    qv_biases = [heads_bias[None]]
+    qv_biases += [b[:, : 2 * cols].reshape(1, 2, cols) for b in bias_pieces[1:]]
+    up_biases = [up_bias.reshape(1, hidden)] + [b[:, 2 * cols :] for b in bias_pieces[1:]]
+    heads_blocks = jnp.concatenate(
+        [heads_weight[:, 1], heads_weight[:, 2], heads_weight[:, 0], out_weight.T], axis=1
+    )[None]
+    for bits in groups:
+        heads_blocks = arrange_blocks(exchange(heads_blocks, bits), bits)
+    feed_blocks = jnp.concatenate([up_weight, down_weight.T], axis=1)[None]
+    heads_blocks, feed_blocks = tie(heads_blocks, feed_blocks)
+    for bits in groups[:-1]:
+        feed_blocks = arrange_blocks(exchange(feed_blocks, bits), bits)
+    feed_parts = exchange(feed_blocks, groups[-1])
+    last = [last_bit()]
+    heads_own = arrange_blocks(exchange(heads_blocks, last), last).reshape(width, -1)
 
     ends = jnp.cumsum(image_lengths[:, 0], axis=1)
     places = narrow_at * own + jnp.arange(own, dtype=jnp.int32)
@@ -524,29 +549,60 @@
     token_rows = lax.dynamic_slice_in_dim(tokens, narrow_at * own, own, 1)
     token_rows = token_rows.reshape(rows, width).astype(f32)
 
-    mixed, near_saved = attend(
-        offset, window_normed, heads_pieces[:2], qv_bias, bounds, own, (0, 1), None
-    )
-    mixed, far_saved = attend(
-        offset, window_normed, heads_pieces[2:], qv_bias, bounds, own, (2, 3), mixed
+    normed_t = window_normed.transpose(0, 2, 1)
+    own_normed = (norm_parts(token_rows)[0] * first_gain + first_shift).astype(bf16)
+    own_normed_t = own_normed.reshape(micro, own, width).transpose(0, 2, 1)
+    feed_grad_t = feed_grad.T
+
+    heads_near = swap(heads_own, "narrow", 1)
+    heads_far = swap(heads_own, "narrow", 2)
+    mixed, saved0 = attend(
+        offset, window_normed, [heads_own], qv_biases[0], bounds, own, None
+    )
+    mixed, *feed_parts = tie(mixed, *feed_parts)
+    feed_blocks = arrange_blocks(feed_parts, groups[-1])
+    mixed, feed_blocks = tie(mixed, feed_blocks)
+    feed_other = exchange(feed_blocks, last)[1]
+    mixed, saved1 = attend(
+        offset, window_normed, [heads_near], qv_biases[1], bounds, own, mixed
+    )
+    mixed, feed_other = tie(mixed, feed_other)
+    feed_own = arrange_blocks([feed_blocks, feed_other], last).reshape(width, -1)
+    mixed, feed_own, heads_far = tie(mixed, feed_own, heads_far)
+    feed_near = swap(feed_own, "narrow", 1)
+    feed_far = swap(feed_own, "narrow", 2)
+    heads_cross = swap(heads_far, "narrow", 1)
+    mixed, saved2 = attend(
+        offset, window_normed, [heads_far], qv_biases[2], bounds, own, mixed
+    )
+    mixed, saved3 = attend(
+        offset, window_normed, [heads_cross], qv_biases[3], bounds, own, mixed
     )
     branch = mixed.reshape(rows, width) + out_bias
     middle = token_rows + mixer_scale * branch
     second_unit, second_inverse = norm_parts(middle)
     second_normed = (second_unit * second_gain + second_shift).astype(bf16)
 
-    sums, far_up, far_down, far_bias = feed_part(
-        second_normed, feed_grad, up_pieces[2:], down_pieces[2:], up_biases[2:], None
-    )
-    far_down_sum = reduce_pair(*far_down)
-    far_up_sum = reduce_pair(*far_up)
-    sums, near_up, near_down, near_bias = feed_part(
-        second_normed, feed_grad, up_pieces[:2], down_pieces[:2], up_biases[:2], sums
-    )
+    second_normed_t = second_normed.T
+
+    def feed_on(pieces, biases, before):
+        return feed_part(
+            second_normed, feed_grad, second_normed_t, feed_grad_t, pieces, biases, before
+        )
+
+    sums, (part1,), bias1 = feed_on([feed_near], up_biases[1:2], None)
+    given = swap(part1, "narrow", 1)
+    sums, (part0,), bias0 = feed_on([feed_own], up_biases[:1], sums)
+    near = add_low(part0, given)
+    near_cut = cut(near, "wide", last)
+    feed, back, *near_cut = tie(*sums, *near_cut)
+    near_sent = send_cut(near_cut, last)
+    feed_far, near_keep = tie(feed_far, near_cut[0])
+    feed_cross = swap(feed_far, "narrow", 1)
+    sums, (part2, part3), bias23 = feed_on([feed_far, feed_cross], up_biases[2:], (feed, back))
+    given = swap(part3, "narrow", 1)
     feed, second_normed_grad = sums
-    up_bias_parts = near_bias + far_bias
-    down_total = reduce_rest(reduce_pair(*near_down), far_down_sum, False)
-    up_total = reduce_rest(reduce_pair(*near_up), far_up_sum, True)
+    up_bias_parts = bias0 + bias1 + bias23
 
     feed_branch = feed + down_bias
     layer_own = (middle + feed_scale * feed_branch).astype(bf16).reshape(micro, own, width)
@@ -565,17 +621,52 @@
     out_bias_sum = mixer_scale * jnp.sum(middle_grad, axis=0)
     mixed_grad = (mixer_scale * middle_grad).astype(bf16).reshape(micro, own, width)
 
-    window_grad, far_heads, far_sums = attend_back(
-        offset, window_normed, mixed_grad, heads_pieces[2:], far_saved, bounds, None
-    )
-    far_heads_sum = reduce_pair(*far_heads)
-    window_grad, near_heads, near_sums = attend_back(
-        offset, window_normed, mixed_grad, heads_pieces[:2], near_saved, bounds, window_grad
-    )
-    heads_total = reduce_rest(reduce_pair(*near_heads), far_heads_sum, False)
+    mgt = mixed_grad.transpose(0, 2, 1)
+
+    def back_on(pieces, saved, grad_in):
+        return attend_back(
+            offset, normed_t, own_normed_t, mixed_grad, mgt, pieces, saved, bounds, grad_in
+        )
+
+    near, far = add_low(near_keep, *near_sent), add_low(part2, given)
+    far_cut = cut(far, "wide", last)
+    mgt, near, *far_cut = tie(mgt, near, *far_cut)
+    far_sent = send_cut(far_cut, last)
+    window_grad, (heads3,), sums3 = back_on([heads_cross], saved3, None)
+    given3 = swap(heads3, "narrow", 1)
+    window_grad, *far_sent = tie(window_grad, *far_sent)
+    far = add_low(far_cut[0], *far_sent)
+    window_grad, far = tie(window_grad, far)
+    far_given = swap(far, "narrow", 2)
+    window_grad, (heads2,), sums2 = back_on([heads_far], saved2, window_grad)
+    window_grad, far_given, given3 = tie(window_grad, far_given, given3)
+    mine = add_low(near, far_given)
+    for bits in groups[:-1]:
+        parts = cut(mine, "wide", bits)
+        mine = add_low(parts[0], *send_cut(parts, bits))
+    mine_cut = cut(mine, "wide", groups[-1])
+    heads_sum = add_low(heads2, given3)
+    window_grad, heads_sum, *mine_cut = tie(window_grad, heads_sum, *mine_cut)
+    mine_sent = send_cut(mine_cut, groups[-1])
+    heads_given = swap(heads_sum, "narrow", 2)
+    window_grad, (heads1,), sums1 = back_on([heads_near], saved1, window_grad)
+    given1 = swap(heads1, "narrow", 1)
+    window_grad, heads_given, *mine_sent = tie(window_grad, heads_given, *mine_sent)
+    mine = add_low(mine_cut[0], *mine_sent)
+    window_grad, mine = tie(window_grad, mine)
+    mine_all = exchange(mine, groups[-1])
+    window_grad, (heads0,), sums0 = back_on([heads_own], saved0, window_grad)
+    window_grad, *mine_all = tie(window_grad, *mine_all)
+    mine = arrange(mine_all, groups[-1], 0).reshape((-1,) + mine.shape[1:])
+    for bits in reversed(groups[:-1]):
+        mine = arrange(exchange(mine, bits), bits, 0).reshape((-1,) + mine.shape[1:])
+    feed_total = spread_last(mine)
+    heads_total = spread_last(
+        spread_far(reduce_far(reduce_last(add_low(heads0, given1, heads_given))))
+    )
     head_bias_parts = [
         jnp.concatenate([s[0, 2 * cols : 3 * cols], s[0, cols : 2 * cols]])
-        for s in near_sums + far_sums
+        for s in sums0 + sums1 + sums2 + sums3
     ]
 
     before = lax.dynamic_slice_in_dim(window_grad, jnp.maximum(off - halo, 0), halo, 1)
@@ -619,7 +710,8 @@
     out_grad = heads_total[:, 3 * cols :].T.astype(f32)
     return (
         layer_out, token_grad, heads_grad, mine[: 2 * cols].reshape(2, cols), out_grad, sums[0],
-        up_total.astype(f32), mine[2 * cols :], down_total.T.astype(f32), sums[1], sums[2],
+        feed_total[:, :hidden].astype(f32), mine[2 * cols :],
+        feed_total[:, hidden:].T.astype(f32), sums[1], sums[2],
         sums[3], sums[4], sums[5], sums[6], sums[7],
     )
 

time: 570 us -> 621 us (1.089); the launches traced: 565 us -> 609 us
  waiting for transfers between devices: 220 us -> 101 us
  local copies, waits for them, and re-layouts: 36.1 us -> 140 us
  other arithmetic: 72.1 us -> 113 us
  Pallas kernels: 174 us -> 200 us
  starting transfers between devices: 61.4 us -> 52.4 us
    ppermute x58 -> x48, waiting for transfers between devices: 218 us -> 101 us  [swap(): return lax.ppermute(values_in, axis, [(i, i ^ bit) for i in range(size)])]
    convert_element_type x1 -> x9, local copies, waits for them, and re-layouts: 1.95 us -> 29.3 us  [the longest x2 7.43 us: body(): token_rows = token_rows.reshape(rows, width).astype(f32)]
    reshape x0 -> x7, local copies, waits for them, and re-layouts: none -> 15.5 us  [the longest x3 4.02 us: body(): qv_biases += [b[:, :2 * cols].reshape(1, 2, cols) for b in bias_pieces[1:]]]
    convert_element_type x18 -> x12, other arithmetic: 13.1 us -> 24.7 us  [the longest x10 18.9 us: add_low(): return total.astype(bf16)]
    pallas_call x2 -> x4, Pallas kernels: 88.2 us -> 99.2 us  [attend_back(): pl.pallas_call(partial(attend_back_kernel, own, heads, count, first), gri...]
    pallas_call x0 -> x3, local copies, waits for them, and re-layouts: none -> 10.9 us  [the longest x2 6.02 us: feed_part(): pl.pallas_call(partial(feed_kernel, 4, count, first), in_specs=[whole] *...]
    ppermute x58 -> x48, starting transfers between devices: 58.1 us -> 48.9 us  [swap(): return lax.ppermute(values_in, axis, [(i, i ^ bit) for i in range(size)])]
    select_n x0 -> x12, other arithmetic: none -> 8.78 us  [arrange(): jnp.where(is_high, high, low)]
  transfers between devices with their start and end apart: 60 -> 50, of which waited for: 26 -> 12; matrix products, arithmetic and copies ran while one was open for 17% -> 39% of each run, Pallas kernels for 31% -> 31%
where the time goes in v2:
time: 621 us; the launch traced here: 609 us
  Pallas kernels  200 us (32%)
  local copies, waits for them, and re-layouts  140 us (23%)
  other arithmetic  113 us (18%)
  waiting for transfers between devices  101 us (16%)
  starting transfers between devices  52.4 us (8%)
    ppermute x48, waiting for transfers between devices, swap(): return lax.ppermute(values_in, axis, [(i, i ^ bit) for i in range(size)])  101 us
    pallas_call x4, Pallas kernels, attend_back(): pl.pallas_call(partial(attend_back_kernel, own, heads, count, first), gri...  99.2 us
    pallas_call x4, Pallas kernels, attend(): pl.pallas_call(partial(attend_kernel, own, heads, count, first), grid_spe...  50.4 us
    pallas_call x3, Pallas kernels, feed_part(): pl.pallas_call(partial(feed_kernel, 4, count, first), in_specs=[whole] *...  50.1 us
    ppermute x48, starting transfers between devices, swap(): return lax.ppermute(values_in, axis, [(i, i ^ bit) for i in range(size)])  48.9 us
    convert_element_type x10, other arithmetic, add_low(): return total.astype(bf16)  18.9 us
    unnamed x115, local copies, waits for them, and re-layouts  14.6 us
  transfers between devices with their start and end apart: 50, of which 12 were waited for; matrix products, arithmetic and copies ran while one was open for 39% of the time, Pallas kernels for 31%

profile of v2, /device:TPU:0, one launch (start us, length us, event | category | flops | bytes accessed | tf_op | source)
XLA Modules:
  0.0 608.7 jit_solution(15877357850176050743)
XLA Ops:
  3.8 5.1 collective-permute-start.3
  11.2 4.7 constant_dynamic-slice_fusion.17
  15.9 4.3 copy.282
  31.0 6.0 copy.246.refs_0_
  37.0 3.6 collective-permute-start.10
  43.9 12.2 %attend.4 = (f32[3,320,768]{2,1,0:T(8,128)}, bf16[3,320,192]{2,1,0:T(8,128)(2,1)}, bf16[3,768,192]{2,1,0:T(8,128)(2,1)}, bf16[3,768,192]{2,1,0:T(8,128)(2,1)}, b...) custom-call(s32[1]{0:T(128)} %bitcast.1.off_ref, bf16[3,768,768]{2,1,0:T(8,128)(2,1)} %copy.246.refs_0_, ...), custom_call_target="tpu_custom_call" | custom-call | flops 4303355904 | bytes 4718592 | tf_op jit(solution)/shard_map/attend/pallas_call | solution.py:130
  56.2 8.7 %collective-permute-done.9 = bf16[1,96,1536]{2,1,0:T(8,128)(2,1)} collective-permute-done((bf16[1,96,1536]{2,1,0:T(8,128)(2,1)}, bf16[1,96,1536]{2,1,0:T(8,128)(2,1)}, u32[]{:S(2)}, u32[]{:S(2)}) %collective-permute-start.9) | collective-permute-done | bytes 294944 | tf_op jit(solution)/shard_map/ppermute | solution.py:367
  72.9 4.2 dynamic-slice_convert_fusion.2
  77.1 3.6 copy.251
  83.9 13.0 %attend.5 = (f32[3,320,768]{2,1,0:T(8,128)}, bf16[3,320,192]{2,1,0:T(8,128)(2,1)}, bf16[3,768,192]{2,1,0:T(8,128)(2,1)}, bf16[3,768,192]{2,1,0:T(8,128)(2,1)}, b...) custom-call(s32[1]{0:T(128)} %bitcast.1.off_ref, bf16[3,768,768]{2,1,0:T(8,128)(2,1)} %copy.246.refs_0_, ...), custom_call_target="tpu_custom_call" | custom-call | flops 4303355904 | bytes 4718592 | tf_op jit(solution)/shard_map/attend/pallas_call | solution.py:130
  100.5 11.3 %collective-permute-done.12.refs_3_.refs_5_ = bf16[768,768]{1,0:T(8,128)(2,1)} collective-permute-done((bf16[768,768]{1,0:T(8,128)(2,1)}, bf16[768,768]{1,0:T(8,128)(2,1)}, u32[]{:S(2)}, u32[]{:S(2)}) %collective-permute-start.12) | collective-permute-done | bytes 1179680 | tf_op jit(solution)/shard_map/ppermute | solution.py:367
  114.6 3.7 copy.281
  118.3 4.0 copy.237
  122.2 3.5 copy.249
  135.3 12.6 %attend.6 = (f32[3,320,768]{2,1,0:T(8,128)}, bf16[3,320,192]{2,1,0:T(8,128)(2,1)}, bf16[3,768,192]{2,1,0:T(8,128)(2,1)}, bf16[3,768,192]{2,1,0:T(8,128)(2,1)}, b...) custom-call(s32[1]{0:T(128)} %bitcast.1.off_ref, bf16[3,768,768]{2,1,0:T(8,128)(2,1)} %copy.246.refs_0_, ...), custom_call_target="tpu_custom_call" | custom-call | flops 4303355904 | bytes 4718592 | tf_op jit(solution)/shard_map/attend/pallas_call | solution.py:130
  147.9 12.6 %attend.7 = (f32[3,320,768]{2,1,0:T(8,128)}, bf16[3,320,192]{2,1,0:T(8,128)(2,1)}, bf16[3,768,192]{2,1,0:T(8,128)(2,1)}, bf16[3,768,192]{2,1,0:T(8,128)(2,1)}, b...) custom-call(s32[1]{0:T(128)} %bitcast.1.off_ref, bf16[3,768,768]{2,1,0:T(8,128)(2,1)} %copy.246.refs_0_, ...), custom_call_target="tpu_custom_call" | custom-call | flops 4303355904 | bytes 4718592 | tf_op jit(solution)/shard_map/attend/pallas_call | solution.py:130
  160.5 4.9 copy.250
  165.4 4.0 convert_reduce_fusion.1
  172.6 4.5 multiply_reduce_fusion.2
  179.1 3.5 copy.247
  182.6 4.9 add_convert_fusion.5
  190.2 12.5 %feed_part.3 = (f32[960,768]{1,0:T(8,128)}, f32[960,768]{1,0:T(8,128)}, bf16[768,1536]{1,0:T(8,128)(2,1)}, f32[1,768]{1,0:T(1,128)}) custom-call(bf16[960,768]{1,0:T(8,128)(2,1)} %copy.256.refs_0_, bf16[960,768]{1,0:T(8,128)(2,1)} %copy.257.refs_1_, bf16[768,960]{1,0:T(8,128)(2,1)} %bitcast.158, bf16[768,960]{1,0:T(8,128)(2,1)} %fusion.21.refs_3_, ...), custom_call_target="tpu_custom_call" | custom-call | flops 6794772480 | bytes 16515072 | tf_op jit(solution)/shard_map/feed_part/pallas_call | solution.py:331
  204.3 14.5 %feed_part.4 = (f32[960,768]{1,0:T(8,128)}, f32[960,768]{1,0:T(8,128)}, bf16[768,1536]{1,0:T(8,128)(2,1)}, f32[1,768]{1,0:T(1,128)}) custom-call(bf16[960,768]{1,0:T(8,128)(2,1)} %copy.256.refs_0_, bf16[960,768]{1,0:T(8,128)(2,1)} %copy.257.refs_1_, bf16[768,960]{1,0:T(8,128)(2,1)} %bitcast.159, ...), custom_call_target="tpu_custom_call", output_to_operand_aliasing={{0}: (6, {}), {1}: (7, {})} | custom-call | flops 6794772480 | bytes 16515072 | tf_op jit(solution)/shard_map/feed_part/pallas_call | solution.py:331
  223.4 33.4 %collective-permute-done.14.refs_4_ = bf16[768,1536]{1,0:T(8,128)(2,1)} collective-permute-done((bf16[768,1536]{1,0:T(8,128)(2,1)}, bf16[768,1536]{1,0:T(8,128)(2,1)}, u32[]{:S(2)}, u32[]{:S(2)}) %collective-permute-start.14) | collective-permute-done | bytes 2359328 | tf_op jit(solution)/shard_map/ppermute | solution.py:367
  256.7 3.8 fusion.20.refs_0_
  264.5 23.1 %feed_part.5 = (f32[960,768]{1,0:T(8,128)}, f32[960,768]{1,0:T(8,128)}, bf16[768,1536]{1,0:T(8,128)(2,1)}, f32[1,768]{1,0:T(1,128)}, bf16[768,1536]{1,0:T(8,128)(2,1)}, /*index=5*/f32[1,768]{1,0:T(1,128)}) custom-call(bf16[960,768]{1,0:T(8,128)(2,1)} %copy.256.refs_0_, ...), custom_call_target="tpu_custom_call", output_to_operand_aliasing={{0}: (8, {}), {1}: (9, {})} | custom-call | flops 13589544960 | bytes 21233664 | tf_op jit(solution)/shard_map/feed_part/pallas_call | solution.py:331
  290.3 4.0 multiply_reduce_fusion.7
  294.4 3.6 copy.258
  298.0 7.3 %multiply_reduce_fusion.5 = (f32[768]{0:T(1024)S(1)}, bf16[960,768]{0,1:T(8,128)(2,1)}, f32[768]{0:T(1024)S(1)}, f32[768]{0:T(1024)S(1)}, f32[960,768]{0,1:T(8,128)}) fusion(f32[960,768]{0,1:T(8,128)S(1)} %copy-done.2, f32[960,768]{0,1:T(8,128)} %copy.258, f32[768]{0:T(1024)S(1)} %copy-done.46, f32[960,768]{0,1:T(8,128)} %get-tuple-element.328, ...), kind=kLoop, calls=%fused_computation.21 | loop fusion | flops 13268736 | bytes 19206144 | tf_op jit(solution)/shard_map/reduce_sum | solution.py:615
  319.9 3.8 copy.265
  328.7 14.1 %collective-permute-done.18 = bf16[3,320,768]{2,1,0:T(8,128)(2,1)} collective-permute-done((bf16[3,320,768]{2,1,0:T(8,128)(2,1)}, bf16[3,320,768]{2,1,0:T(8,128)(2,1)}, u32[]{:S(2)}, u32[]{:S(2)}) %collective-permute-start.18) | collective-permute-done | bytes 1474592 | tf_op jit(solution)/shard_map/ppermute | solution.py:367
  350.4 24.2 %attend_back.4 = (f32[3,768,768]{2,1,0:T(8,128)}, bf16[768,768]{1,0:T(8,128)(2,1)}, f32[1,768]{1,0:T(1,128)}) custom-call(s32[1]{0:T(128)} %bitcast.1.off_ref, bf16[3,768,768]{2,1,0:T(8,128)(2,1)} %fusion.20.refs_0_, bf16[3,768,320]{2,1,0:T(8,128)(2,1)} %fusion.7.refs_1_, bf16[3,320,768]{2,1,0:T(8,128)(2,1)} %bitcast.163, bf16[3,768,320]{2,1,0:T(8,128)(2,1)} %bitcast.170, ...), custom_call_target="tpu_custom_call" | custom-call | flops 9739173888 | bytes 20054016 | tf_op jit(solution)/shard_map/attend_back/pallas_call | solution.py:249
  385.9 24.9 %attend_back.5 = (f32[3,768,768]{2,1,0:T(8,128)}, bf16[768,768]{1,0:T(8,128)(2,1)}, f32[1,768]{1,0:T(1,128)}) custom-call(s32[1]{0:T(128)} %bitcast.1.off_ref, bf16[3,768,768]{2,1,0:T(8,128)(2,1)} %fusion.20.refs_0_, bf16[3,768,320]{2,1,0:T(8,128)(2,1)} %fusion.7.refs_1_, bf16[3,320,768]{2,1,0:T(8,128)(2,1)} %bitcast.164, bf16[3,768,320]{2,1,0:T(8,128)(2,1)} %bitcast.171, ...), custom_call_target="tpu_custom_call" | custom-call | flops 9739173888 | bytes 20054016 | tf_op jit(solution)/shard_map/attend_back/pallas_call | solution.py:249
  424.2 25.0 %attend_back.6 = (f32[3,768,768]{2,1,0:T(8,128)}, bf16[768,768]{1,0:T(8,128)(2,1)}, f32[1,768]{1,0:T(1,128)}) custom-call(s32[1]{0:T(128)} %bitcast.1.off_ref, bf16[3,768,768]{2,1,0:T(8,128)(2,1)} %fusion.20.refs_0_, bf16[3,768,320]{2,1,0:T(8,128)(2,1)} %fusion.7.refs_1_, bf16[3,320,768]{2,1,0:T(8,128)(2,1)} %bitcast.165, bf16[3,768,320]{2,1,0:T(8,128)(2,1)} %bitcast.172, ...), custom_call_target="tpu_custom_call" | custom-call | flops 9739173888 | bytes 20054016 | tf_op jit(solution)/shard_map/attend_back/pallas_call | solution.py:249
  459.1 25.1 %attend_back.7 = (f32[3,768,768]{2,1,0:T(8,128)}, bf16[768,768]{1,0:T(8,128)(2,1)}, f32[1,768]{1,0:T(1,128)}) custom-call(s32[1]{0:T(128)} %bitcast.1.off_ref, bf16[3,768,768]{2,1,0:T(8,128)(2,1)} %fusion.20.refs_0_, bf16[3,768,320]{2,1,0:T(8,128)(2,1)} %fusion.7.refs_1_, bf16[3,320,768]{2,1,0:T(8,128)(2,1)} %bitcast.166, bf16[3,768,320]{2,1,0:T(8,128)(2,1)} %bitcast.173, ...), custom_call_target="tpu_custom_call" | custom-call | flops 9739173888 | bytes 20054016 | tf_op jit(solution)/shard_map/attend_back/pallas_call | solution.py:249
  492.0 3.9 dynamic-slice_convert_fusion.1
  499.2 8.1 %copy.266 = f32[3,768,768]{1,2,0:T(8,128)} copy(f32[3,768,768]{2,1,0:T(8,128)} %get-tuple-element.198) | data formatting | bytes 14155776 | tf_op jit(solution)/shard_map/optimization_barrier | solution.py:396
  515.5 4.6 collective-permute-done.37
  520.1 4.8 collective-permute-done.38
  525.0 3.8 collective-permute-start.42
  532.9 3.2 collective-permute-start.41
  539.0 5.9 collective-permute-done.41
  549.0 6.4 %multiply_reduce_fusion = (f32[768]{0:T(1024)S(1)}, f32[3,320]{1,0:T(4,128)}, f32[3,320]{1,0:T(4,128)}, f32[768]{0:T(1024)S(1)}, f32[3,320,768]{1,2,0:T(8,128)}) fusion(bf16[3,320,768]{1,2,0:T(8,128)(2,1)S(1)} %copy-done, f32[3,320]{1,0:T(4,128)} %copy-done.27, f32[3,320]{1,0:T(4,128)S(1)} %copy-done.21, f32[768]{0:T(1024)S(1)} %copy-done.25, ...), kind=kLoop, calls=%fused_computation.11 | loop fusion | flops 10318464 | bytes 9314308 | tf_op jit(solution)/shard_map/reduce_sum | solution.py:686
  557.0 4.9 collective-permute-done.44
  569.6 8.8 %collective-permute-done.46 = f32[84,128]{1,0:T(8,128)S(1)} collective-permute-done((f32[84,128]{1,0:T(8,128)S(1)}, f32[84,128]{1,0:T(8,128)S(1)}, u32[]{:S(2)}, u32[]{:S(2)}) %collective-permute-start.46) | collective-permute-done | bytes 43040 | tf_op jit(solution)/shard_map/ppermute | solution.py:367
  578.6 4.9 copy.269
  583.5 3.6 copy.270
  587.4 4.9 add_convert_fusion.3
  (352 shorter events, 185.0 us)
Async XLA Ops:
  3.8 18.7 %collective-permute-start.3 = (bf16[1,96,768]{2,1,0:T(8,128)(2,1)}, bf16[1,96,768]{2,1,0:T(8,128)(2,1)}, u32[]{:S(2)}, u32[]{:S(2)}) collective-permute-start(bf16[1,96,768]{2,1,0:T(8,128)(2,1)} %maximum_bitcast_fusion.3), channel_id=1, source_target_pairs={{0,24},{4,28},{8,16},{12,20},{16,8},{20,12},{24,0},{28,4},{1,25},{... | collective-permute-start | bytes 442376 | tf_op jit(solution)/shard_map/ppermute | solution.py:367
  8.9 13.6 %collective-permute-start.4 = (bf16[1,96,768]{2,1,0:T(8,128)(2,1)}, bf16[1,96,768]{2,1,0:T(8,128)(2,1)}, u32[]{:S(2)}, u32[]{:S(2)}) collective-permute-start(bf16[1,96,768]{2,1,0:T(8,128)(2,1)} %maximum_bitcast_fusion.3), channel_id=1, source_target_pairs={{0,16},{4,20},{8,24},{12,28},{16,0},{20,4},{24,8},{28,12},{1,17},{... | collective-permute-start | bytes 442376 | tf_op jit(solution)/shard_map/ppermute | solution.py:367
  8.9 14.6 %collective-permute-start.5 = (bf16[1,96,768]{2,1,0:T(8,128)(2,1)}, bf16[1,96,768]{2,1,0:T(8,128)(2,1)}, u32[]{:S(2)}, u32[]{:S(2)}) collective-permute-start(bf16[1,96,768]{2,1,0:T(8,128)(2,1)} %maximum_bitcast_fusion.3), channel_id=1, source_target_pairs={{0,8},{4,12},{8,0},{12,4},{16,24},{20,28},{24,16},{28,20},{1,9},{5... | collective-permute-start | bytes 442376 | tf_op jit(solution)/shard_map/ppermute | solution.py:367
  25.6 15.8 %collective-permute-start.6 = (bf16[4,96,768]{2,1,0:T(8,128)(2,1)}, bf16[4,96,768]{2,1,0:T(8,128)(2,1)}, u32[]{:S(2)}, u32[]{:S(2)}) collective-permute-start(bf16[4,96,768]{2,1,0:T(8,128)(2,1)} %maximum_bitcast_fusion.1), channel_id=1, source_target_pairs={{0,4},{4,0},{8,12},{12,8},{16,20},{20,16},{24,28},{28,24},{1,5},{5... | collective-permute-start | bytes 1769480 | tf_op jit(solution)/shard_map/ppermute | solution.py:367
  37.0 19.1 %collective-permute-start.10 = (bf16[1,96,1536]{2,1,0:T(8,128)(2,1)}, bf16[1,96,1536]{2,1,0:T(8,128)(2,1)}, u32[]{:S(2)}, u32[]{:S(2)}) collective-permute-start(bf16[1,96,1536]{2,1,0:T(8,128)(2,1)} %maximum_bitcast_fusion.2), channel_id=1, source_target_pairs={{0,24},{4,28},{8,16},{12,20},{16,8},{20,12},{24,0},{28,4},{1,25},{... | collective-permute-start | bytes 884744 | tf_op jit(solution)/shard_map/ppermute | solution.py:367
  40.6 15.5 %collective-permute-start.8 = (bf16[1,96,1536]{2,1,0:T(8,128)(2,1)}, bf16[1,96,1536]{2,1,0:T(8,128)(2,1)}, u32[]{:S(2)}, u32[]{:S(2)}) collective-permute-start(bf16[1,96,1536]{2,1,0:T(8,128)(2,1)} %maximum_bitcast_fusion.2), channel_id=1, source_target_pairs={{0,8},{4,12},{8,0},{12,4},{16,24},{20,28},{24,16},{28,20},{1,9},{5... | collective-permute-start | bytes 884744 | tf_op jit(solution)/shard_map/ppermute | solution.py:367
  40.6 24.3 %collective-permute-start.9 = (bf16[1,96,1536]{2,1,0:T(8,128)(2,1)}, bf16[1,96,1536]{2,1,0:T(8,128)(2,1)}, u32[]{:S(2)}, u32[]{:S(2)}) collective-permute-start(bf16[1,96,1536]{2,1,0:T(8,128)(2,1)} %maximum_bitcast_fusion.2), channel_id=1, source_target_pairs={{0,16},{4,20},{8,24},{12,28},{16,0},{20,4},{24,8},{28,12},{1,17},{... | collective-permute-start | bytes 884744 | tf_op jit(solution)/shard_map/ppermute | solution.py:367
  43.9 39.9 %collective-permute-start.7 = (bf16[768,768]{1,0:T(8,128)(2,1)}, bf16[768,768]{1,0:T(8,128)(2,1)}, u32[]{:S(2)}, u32[]{:S(2)}) collective-permute-start(bf16[768,768]{1,0:T(8,128)(2,1)} %bitcast.22.refs_3_.refs_5_), channel_id=1, source_target_pairs={{0,1},{1,0},{2,3},{3,2},{4,5},{5,4},{6,7},{7,6},{8,9},{9,8},{10,11... | collective-permute-start | bytes 3538952 | tf_op jit(solution)/shard_map/ppermute | solution.py:367
  68.2 28.7 %collective-permute-start.11 = (bf16[4,96,1536]{2,1,0:T(8,128)(2,1)}, bf16[4,96,1536]{2,1,0:T(8,128)(2,1)}, u32[]{:S(2)}, u32[]{:S(2)}) collective-permute-start(bf16[4,96,1536]{2,1,0:T(8,128)(2,1)} %maximum_bitcast_fusion), channel_id=1, source_target_pairs={{0,4},{4,0},{8,12},{12,8},{16,20},{20,16},{24,28},{28,24},{1,5},{5... | collective-permute-start | bytes 3538952 | tf_op jit(solution)/shard_map/ppermute | solution.py:367
  71.4 9.3 %collective-permute-start.2 = (f32[1,1152]{1,0:T(1,128)}, f32[1,1152]{1,0:T(1,128)}, u32[]{:S(2)}, u32[]{:S(2)}) collective-permute-start(f32[1,1152]{1,0:T(1,128)} %reshape.806), channel_id=1, source_target_pairs={{0,1},{1,0},{2,3},{3,2},{4,5},{5,4},{6,7},{7,6},{8,9},{9,8},{10,11... | collective-permute-start | bytes 13832 | tf_op jit(solution)/shard_map/ppermute | solution.py:367
  71.4 56.9 %collective-permute-start = (f32[1,1152]{1,0:T(1,128)}, f32[1,1152]{1,0:T(1,128)}, u32[]{:S(2)}, u32[]{:S(2)}) collective-permute-start(f32[1,1152]{1,0:T(1,128)} %reshape.806), channel_id=1, source_target_pairs={{0,2},{1,3},{2,0},{3,1},{4,6},{5,7},{6,4},{7,5},{8,10},{9,11},{10,... | collective-permute-start | bytes 13832 | tf_op jit(solution)/shard_map/ppermute | solution.py:367
  83.4 28.4 %collective-permute-start.12 = (bf16[768,768]{1,0:T(8,128)(2,1)}, bf16[768,768]{1,0:T(8,128)(2,1)}, u32[]{:S(2)}, u32[]{:S(2)}) collective-permute-start(bf16[768,768]{1,0:T(8,128)(2,1)} %bitcast.22.refs_3_.refs_5_), channel_id=1, source_target_pairs={{0,2},{1,3},{2,0},{3,1},{4,6},{5,7},{6,4},{7,5},{8,10},{9,11},{10,... | collective-permute-start | bytes 3538952 | tf_op jit(solution)/shard_map/ppermute | solution.py:367
  111.8 36.1 %collective-permute-start.13 = (bf16[768,768]{1,0:T(8,128)(2,1)}, bf16[768,768]{1,0:T(8,128)(2,1)}, u32[]{:S(2)}, u32[]{:S(2)}) collective-permute-start(bf16[768,768]{1,0:T(8,128)(2,1)} %collective-permute-done.12.refs_3_.refs_5_), channel_id=1, source_target_pairs={{0,1},{1,0},{2,3},{3,2},{4,5},{5,4},{6,7},{7,6},{8,9},{9,8},{10,11... | collective-permute-start | bytes 3538952 | tf_op jit(solution)/shard_map/ppermute | solution.py:367
  135.3 54.9 %collective-permute-start.15 = (bf16[768,1536]{1,0:T(8,128)(2,1)}, bf16[768,1536]{1,0:T(8,128)(2,1)}, u32[]{:S(2)}, u32[]{:S(2)}) collective-permute-start(bf16[768,1536]{1,0:T(8,128)(2,1)} %bitcast.167), channel_id=1, source_target_pairs={{0,1},{1,0},{2,3},{3,2},{4,5},{5,4},{6,7},{7,6},{8,9},{9,8},{10,11... | collective-permute-start | bytes 7077896 | tf_op jit(solution)/shard_map/ppermute | solution.py:367
  202.7 16.1 %collective-permute-start.16 = (bf16[768,1536]{1,0:T(8,128)(2,1)}, bf16[768,1536]{1,0:T(8,128)(2,1)}, u32[]{:S(2)}, u32[]{:S(2)}) collective-permute-start(bf16[768,1536]{1,0:T(8,128)(2,1)} %get-tuple-element.138), channel_id=1, source_target_pairs={{0,1},{1,0},{2,3},{3,2},{4,5},{5,4},{6,7},{7,6},{8,9},{9,8},{10,11... | collective-permute-start | bytes 7077896 | tf_op jit(solution)/shard_map/ppermute | solution.py:367
  203.2 53.5 %collective-permute-start.14 = (bf16[768,1536]{1,0:T(8,128)(2,1)}, bf16[768,1536]{1,0:T(8,128)(2,1)}, u32[]{:S(2)}, u32[]{:S(2)}) collective-permute-start(bf16[768,1536]{1,0:T(8,128)(2,1)} %bitcast.168), channel_id=1, source_target_pairs={{0,2},{1,3},{2,0},{3,1},{4,6},{5,7},{6,4},{7,5},{8,10},{9,11},{10,... | collective-permute-start | bytes 7077896 | tf_op jit(solution)/shard_map/ppermute | solution.py:367
  256.7 7.8 %collective-permute-start.17 = (bf16[768,1536]{1,0:T(8,128)(2,1)}, bf16[768,1536]{1,0:T(8,128)(2,1)}, u32[]{:S(2)}, u32[]{:S(2)}) collective-permute-start(bf16[768,1536]{1,0:T(8,128)(2,1)} %collective-permute-done.14.refs_4_), channel_id=1, source_target_pairs={{0,1},{1,0},{2,3},{3,2},{4,5},{5,4},{6,7},{7,6},{8,9},{9,8},{10,11... | collective-permute-start | bytes 7077896 | tf_op jit(solution)/shard_map/ppermute | solution.py:367
  263.0 52.3 %collective-permute-start.21 = (bf16[384,1536]{1,0:T(8,128)(2,1)}, bf16[384,1536]{1,0:T(8,128)(2,1)}, u32[]{:S(2)}, u32[]{:S(2)}) collective-permute-start(bf16[384,1536]{1,0:T(8,128)(2,1)} %get-tuple-element.146), channel_id=1, source_target_pairs={{0,4},{4,0},{8,12},{12,8},{16,20},{20,16},{24,28},{28,24},{1,5},{5... | collective-permute-start | bytes 3538952 | tf_op jit(solution)/shard_map/ppermute | solution.py:367
  287.6 58.4 %collective-permute-start.22 = (bf16[768,1536]{1,0:T(8,128)(2,1)}, bf16[768,1536]{1,0:T(8,128)(2,1)}, u32[]{:S(2)}, u32[]{:S(2)}) collective-permute-start(bf16[768,1536]{1,0:T(8,128)(2,1)} %get-tuple-element.148), channel_id=1, source_target_pairs={{0,1},{1,0},{2,3},{3,2},{4,5},{5,4},{6,7},{7,6},{8,9},{9,8},{10,11... | collective-permute-start | bytes 7077896 | tf_op jit(solution)/shard_map/ppermute | solution.py:367
  308.0 34.8 %collective-permute-start.18 = (bf16[3,320,768]{2,1,0:T(8,128)(2,1)}, bf16[3,320,768]{2,1,0:T(8,128)(2,1)}, u32[]{:S(2)}, u32[]{:S(2)}) collective-permute-start(bf16[3,320,768]{2,1,0:T(8,128)(2,1)} %bitcast.36), channel_id=1, source_target_pairs={{0,2},{1,3},{2,0},{3,1},{4,6},{5,7},{6,4},{7,5},{8,10},{9,11},{10,... | collective-permute-start | bytes 4423688 | tf_op jit(solution)/shard_map/ppermute | solution.py:367
  308.6 34.3 %collective-permute-start.20 = (bf16[3,320,768]{2,1,0:T(8,128)(2,1)}, bf16[3,320,768]{2,1,0:T(8,128)(2,1)}, u32[]{:S(2)}, u32[]{:S(2)}) collective-permute-start(bf16[3,320,768]{2,1,0:T(8,128)(2,1)} %bitcast.36), channel_id=1, source_target_pairs={{0,1},{1,0},{2,3},{3,2},{4,5},{5,4},{6,7},{7,6},{8,9},{9,8},{10,11... | collective-permute-start | bytes 4423688 | tf_op jit(solution)/shard_map/ppermute | solution.py:367
  342.9 33.5 %collective-permute-start.19 = (bf16[3,320,768]{2,1,0:T(8,128)(2,1)}, bf16[3,320,768]{2,1,0:T(8,128)(2,1)}, u32[]{:S(2)}, u32[]{:S(2)}) collective-permute-start(bf16[3,320,768]{2,1,0:T(8,128)(2,1)} %collective-permute-done.18), channel_id=1, source_target_pairs={{0,1},{1,0},{2,3},{3,2},{4,5},{5,4},{6,7},{7,6},{8,9},{9,8},{10,11... | collective-permute-start | bytes 4423688 | tf_op jit(solution)/shard_map/ppermute | solution.py:367
  349.9 28.7 %collective-permute-start.23 = (bf16[384,1536]{1,0:T(8,128)(2,1)}, bf16[384,1536]{1,0:T(8,128)(2,1)}, u32[]{:S(2)}, u32[]{:S(2)}) collective-permute-start(bf16[384,1536]{1,0:T(8,128)(2,1)} %get-tuple-element.171), channel_id=1, source_target_pairs={{0,4},{4,0},{8,12},{12,8},{16,20},{20,16},{24,28},{28,24},{1,5},{5... | collective-permute-start | bytes 3538952 | tf_op jit(solution)/shard_map/ppermute | solution.py:367
  374.6 36.2 %collective-permute-start.25 = (bf16[768,768]{1,0:T(8,128)(2,1)}, bf16[768,768]{1,0:T(8,128)(2,1)}, u32[]{:S(2)}, u32[]{:S(2)}) collective-permute-start(bf16[768,768]{1,0:T(8,128)(2,1)} %get-tuple-element.178), channel_id=1, source_target_pairs={{0,1},{1,0},{2,3},{3,2},{4,5},{5,4},{6,7},{7,6},{8,9},{9,8},{10,11... | collective-permute-start | bytes 3538952 | tf_op jit(solution)/shard_map/ppermute | solution.py:367
  381.2 29.6 %collective-permute-start.24 = (bf16[384,1536]{1,0:T(8,128)(2,1)}, bf16[384,1536]{1,0:T(8,128)(2,1)}, u32[]{:S(2)}, u32[]{:S(2)}) collective-permute-start(bf16[384,1536]{1,0:T(8,128)(2,1)} %add_convert_fusion.9), channel_id=1, source_target_pairs={{0,2},{1,3},{2,0},{3,1},{4,6},{5,7},{6,4},{7,5},{8,10},{9,11},{10,... | collective-permute-start | bytes 3538952 | tf_op jit(solution)/shard_map/ppermute | solution.py:367
  415.0 38.2 %collective-permute-start.26 = (bf16[768,768]{1,0:T(8,128)(2,1)S(1)}, bf16[768,768]{1,0:T(8,128)(2,1)}, u32[]{:S(2)}, u32[]{:S(2)}) collective-permute-start(bf16[768,768]{1,0:T(8,128)(2,1)S(1)} %add_convert_fusion.8), channel_id=1, source_target_pairs={{0,2},{1,3},{2,0},{3,1},{4,6},{5,7},{6,4},{7,5},{8,10},{9,11},{10,... | collective-permute-start | bytes 3538952 | tf_op jit(solution)/shard_map/ppermute | solution.py:367
  419.8 33.4 %collective-permute-start.27 = (bf16[96,1536]{1,0:T(8,128)(2,1)}, bf16[96,1536]{1,0:T(8,128)(2,1)}, u32[]{:S(2)}, u32[]{:S(2)}) collective-permute-start(bf16[96,1536]{1,0:T(8,128)(2,1)} %get-tuple-element.187), channel_id=1, source_target_pairs={{0,8},{4,12},{8,0},{12,4},{16,24},{20,28},{24,16},{28,20},{1,9},{5... | collective-permute-start | bytes 884744 | tf_op jit(solution)/shard_map/ppermute | solution.py:367
  419.8 33.4 %collective-permute-start.28 = (bf16[96,1536]{1,0:T(8,128)(2,1)}, bf16[96,1536]{1,0:T(8,128)(2,1)}, u32[]{:S(2)}, u32[]{:S(2)}) collective-permute-start(bf16[96,1536]{1,0:T(8,128)(2,1)} %get-tuple-element.188), channel_id=1, source_target_pairs={{0,16},{4,20},{8,24},{12,28},{16,0},{20,4},{24,8},{28,12},{1,17},{... | collective-permute-start | bytes 884744 | tf_op jit(solution)/shard_map/ppermute | solution.py:367
  422.8 30.5 %collective-permute-start.29 = (bf16[96,1536]{1,0:T(8,128)(2,1)S(1)}, bf16[96,1536]{1,0:T(8,128)(2,1)}, u32[]{:S(2)}, u32[]{:S(2)}) collective-permute-start(bf16[96,1536]{1,0:T(8,128)(2,1)S(1)} %get-tuple-element.189), channel_id=1, source_target_pairs={{0,24},{4,28},{8,16},{12,20},{16,8},{20,12},{24,0},{28,4},{1,25},{... | collective-permute-start | bytes 884744 | tf_op jit(solution)/shard_map/ppermute | solution.py:367
  453.2 31.9 %collective-permute-start.35 = (bf16[768,768]{1,0:T(8,128)(2,1)}, bf16[768,768]{1,0:T(8,128)(2,1)}, u32[]{:S(2)}, u32[]{:S(2)}) collective-permute-start(bf16[768,768]{1,0:T(8,128)(2,1)} %get-tuple-element.200), channel_id=1, source_target_pairs={{0,1},{1,0},{2,3},{3,2},{4,5},{5,4},{6,7},{7,6},{8,9},{9,8},{10,11... | collective-permute-start | bytes 3538952 | tf_op jit(solution)/shard_map/ppermute | solution.py:367
  454.6 37.3 %collective-permute-start.30 = (bf16[96,1536]{1,0:T(8,128)(2,1)S(1)}, bf16[96,1536]{1,0:T(8,128)(2,1)S(1)}, u32[]{:S(2)}, u32[]{:S(2)}) collective-permute-start(bf16[96,1536]{1,0:T(8,128)(2,1)S(1)} %add_convert_fusion.12), channel_id=1, source_target_pairs={{0,8},{4,12},{8,0},{12,4},{16,24},{20,28},{24,16},{28,20},{1,9},{5... | collective-permute-start | bytes 884744 | tf_op jit(solution)/shard_map/ppermute | solution.py:367
  454.7 37.3 %collective-permute-start.31 = (bf16[96,1536]{1,0:T(8,128)(2,1)S(1)}, bf16[96,1536]{1,0:T(8,128)(2,1)}, u32[]{:S(2)}, u32[]{:S(2)}) collective-permute-start(bf16[96,1536]{1,0:T(8,128)(2,1)S(1)} %add_convert_fusion.12), channel_id=1, source_target_pairs={{0,16},{4,20},{8,24},{12,28},{16,0},{20,4},{24,8},{28,12},{1,17},{... | collective-permute-start | bytes 884744 | tf_op jit(solution)/shard_map/ppermute | solution.py:367
  457.6 34.4 %collective-permute-start.32 = (bf16[96,1536]{1,0:T(8,128)(2,1)S(1)}, bf16[96,1536]{1,0:T(8,128)(2,1)}, u32[]{:S(2)}, u32[]{:S(2)}) collective-permute-start(bf16[96,1536]{1,0:T(8,128)(2,1)S(1)} %add_convert_fusion.12), channel_id=1, source_target_pairs={{0,24},{4,28},{8,16},{12,20},{16,8},{20,12},{24,0},{28,4},{1,25},{... | collective-permute-start | bytes 884744 | tf_op jit(solution)/shard_map/ppermute | solution.py:367
  490.4 19.2 %collective-permute-start.36 = (bf16[384,768]{1,0:T(8,128)(2,1)}, bf16[384,768]{1,0:T(8,128)(2,1)}, u32[]{:S(2)}, u32[]{:S(2)}) collective-permute-start(bf16[384,768]{1,0:T(8,128)(2,1)} %constant_dynamic-slice_fusion.8), channel_id=1, source_target_pairs={{0,4},{4,0},{8,12},{12,8},{16,20},{20,16},{24,28},{28,24},{1,5},{5... | collective-permute-start | bytes 1769480 | tf_op jit(solution)/shard_map/ppermute | solution.py:367
  495.8 49.1 %collective-permute-start.33 = (bf16[3,208,768]{2,1,0:T(8,128)(2,1)}, bf16[3,208,768]{2,1,0:T(8,128)(2,1)}, u32[]{:S(2)}, u32[]{:S(2)}) collective-permute-start(bf16[3,208,768]{2,1,0:T(8,128)(2,1)} %get-tuple-element.329), channel_id=1, source_target_pairs={{0,1},{1,2},{2,3},{4,5},{5,6},{6,7},{8,9},{9,10},{10,11},{12,13},{... | collective-permute-start | bytes 2875400 | tf_op jit(solution)/shard_map/ppermute | solution.py:373
  507.2 39.4 %collective-permute-start.34 = (bf16[3,208,768]{2,1,0:T(8,128)(2,1)}, bf16[3,208,768]{2,1,0:T(8,128)(2,1)}, u32[]{:S(2)}, u32[]{:S(2)}) collective-permute-start(bf16[3,208,768]{2,1,0:T(8,128)(2,1)} %get-tuple-element.330), channel_id=1, source_target_pairs={{1,0},{2,1},{3,2},{5,4},{6,5},{7,6},{9,8},{10,9},{11,10},{13,12},{... | collective-permute-start | bytes 2875400 | tf_op jit(solution)/shard_map/ppermute | solution.py:373
  510.9 9.2 %collective-permute-start.37 = (bf16[96,768]{1,0:T(8,128)(2,1)S(1)}, bf16[96,768]{1,0:T(8,128)(2,1)S(1)}, u32[]{:S(2)}, u32[]{:S(2)}) collective-permute-start(bf16[96,768]{1,0:T(8,128)(2,1)S(1)} %get-tuple-element.374), channel_id=1, source_target_pairs={{0,8},{4,12},{8,0},{12,4},{16,24},{20,28},{24,16},{28,20},{1,9},{5... | collective-permute-start | bytes 442376 | tf_op jit(solution)/shard_map/ppermute | solution.py:367
  511.0 13.9 %collective-permute-start.38 = (bf16[96,768]{1,0:T(8,128)(2,1)S(1)}, bf16[96,768]{1,0:T(8,128)(2,1)S(1)}, u32[]{:S(2)}, u32[]{:S(2)}) collective-permute-start(bf16[96,768]{1,0:T(8,128)(2,1)S(1)} %get-tuple-element.376), channel_id=1, source_target_pairs={{0,16},{4,20},{8,24},{12,28},{16,0},{20,4},{24,8},{28,12},{1,17},{... | collective-permute-start | bytes 442376 | tf_op jit(solution)/shard_map/ppermute | solution.py:367
  513.9 11.0 %collective-permute-start.39 = (bf16[96,768]{1,0:T(8,128)(2,1)S(1)}, bf16[96,768]{1,0:T(8,128)(2,1)S(1)}, u32[]{:S(2)}, u32[]{:S(2)}) collective-permute-start(bf16[96,768]{1,0:T(8,128)(2,1)S(1)} %get-tuple-element.375), channel_id=1, source_target_pairs={{0,24},{4,28},{8,16},{12,20},{16,8},{20,12},{24,0},{28,4},{1,25},{... | collective-permute-start | bytes 442376 | tf_op jit(solution)/shard_map/ppermute | solution.py:367
  525.0 7.9 %collective-permute-start.42 = (bf16[96,768]{1,0:T(8,128)(2,1)S(1)}, bf16[96,768]{1,0:T(8,128)(2,1)S(1)}, u32[]{:S(2)}, u32[]{:S(2)}) collective-permute-start(bf16[96,768]{1,0:T(8,128)(2,1)S(1)} %add_convert_fusion.13), channel_id=1, source_target_pairs={{0,8},{4,12},{8,0},{12,4},{16,24},{20,28},{24,16},{28,20},{1,9},{5... | collective-permute-start | bytes 442376 | tf_op jit(solution)/shard_map/ppermute | solution.py:367
  529.9 67.1 %collective-permute-start.49 = (bf16[384,1536]{1,0:T(8,128)(2,1)}, bf16[384,1536]{1,0:T(8,128)(2,1)}, u32[]{:S(2)}, u32[]{:S(2)}) collective-permute-start(bf16[384,1536]{1,0:T(8,128)(2,1)} %bitcast.74), channel_id=1, source_target_pairs={{0,4},{4,0},{8,12},{12,8},{16,20},{20,16},{24,28},{28,24},{1,5},{5... | collective-permute-start | bytes 3538952 | tf_op jit(solution)/shard_map/ppermute | solution.py:367
  530.4 8.6 %collective-permute-start.40 = (bf16[96,768]{1,0:T(8,128)(2,1)S(1)}, bf16[96,768]{1,0:T(8,128)(2,1)S(1)}, u32[]{:S(2)}, u32[]{:S(2)}) collective-permute-start(bf16[96,768]{1,0:T(8,128)(2,1)S(1)} %add_convert_fusion.13), channel_id=1, source_target_pairs={{0,24},{4,28},{8,16},{12,20},{16,8},{20,12},{24,0},{28,4},{1,25},{... | collective-permute-start | bytes 442376 | tf_op jit(solution)/shard_map/ppermute | solution.py:367
  532.9 12.0 %collective-permute-start.41 = (bf16[96,768]{1,0:T(8,128)(2,1)S(1)}, bf16[96,768]{1,0:T(8,128)(2,1)S(1)}, u32[]{:S(2)}, u32[]{:S(2)}) collective-permute-start(bf16[96,768]{1,0:T(8,128)(2,1)S(1)} %add_convert_fusion.13), channel_id=1, source_target_pairs={{0,16},{4,20},{8,24},{12,28},{16,0},{20,4},{24,8},{28,12},{1,17},{... | collective-permute-start | bytes 442376 | tf_op jit(solution)/shard_map/ppermute | solution.py:367
  556.9 4.9 collective-permute-start.44
  563.5 40.3 %collective-permute-start.43 = (bf16[384,768]{1,0:T(8,128)(2,1)}, bf16[384,768]{1,0:T(8,128)(2,1)}, u32[]{:S(2)}, u32[]{:S(2)}) collective-permute-start(bf16[384,768]{1,0:T(8,128)(2,1)} %bitcast.52), channel_id=1, source_target_pairs={{0,4},{4,0},{8,12},{12,8},{16,20},{20,16},{24,28},{28,24},{1,5},{5... | collective-permute-start | bytes 1769480 | tf_op jit(solution)/shard_map/ppermute | solution.py:367
  567.4 11.1 %collective-permute-start.46 = (f32[84,128]{1,0:T(8,128)S(1)}, f32[84,128]{1,0:T(8,128)S(1)}, u32[]{:S(2)}, u32[]{:S(2)}) collective-permute-start(f32[84,128]{1,0:T(8,128)S(1)} %fusion.19), channel_id=1, source_target_pairs={{0,4},{4,0},{8,12},{12,8},{16,20},{20,16},{24,28},{28,24},{1,5},{5... | collective-permute-start | bytes 129032 | tf_op jit(solution)/shard_map/ppermute | solution.py:367
  578.5 8.8 %collective-permute-start.47 = (f32[84,128]{1,0:T(8,128)S(1)}, f32[84,128]{1,0:T(8,128)S(1)}, u32[]{:S(2)}, u32[]{:S(2)}) collective-permute-start(f32[84,128]{1,0:T(8,128)S(1)} %add.300), channel_id=1, source_target_pairs={{0,2},{1,3},{2,0},{3,1},{4,6},{5,7},{6,4},{7,5},{8,10},{9,11},{10,... | collective-permute-start | bytes 129032 | tf_op jit(solution)/shard_map/ppermute | solution.py:367
  587.3 7.6 %collective-permute-start.48 = (f32[84,128]{1,0:T(8,128)S(1)}, f32[84,128]{1,0:T(8,128)S(1)}, u32[]{:S(2)}, u32[]{:S(2)}) collective-permute-start(f32[84,128]{1,0:T(8,128)S(1)} %add.301), channel_id=1, source_target_pairs={{0,1},{1,0},{2,3},{3,2},{4,5},{5,4},{6,7},{7,6},{8,9},{9,8},{10,11... | collective-permute-start | bytes 129032 | tf_op jit(solution)/shard_map/ppermute | solution.py:367
  (54 other events, 462.5 us)

commit v3 on v2

--- a/solution.py
+++ b/solution.py
@@ -40,9 +40,7 @@
 
 
 def cost(flops, transcendentals, moved):
-    return pl.CostEstimate(
-        flops=int(flops), transcendentals=int(transcendentals), bytes_accessed=int(moved)
-    )
+    return pl.CostEstimate(flops=1024, transcendentals=0, bytes_accessed=1024)
 
 
 def full(shape):
@@ -144,21 +142,25 @@
     return result[0], [tuple(result[1 + 5 * i : 6 + 5 * i]) for i in range(count)]
 
 
-def attend_back_kernel(own, heads, count, first, off_ref, *refs):
-    xt_ref, xot_ref, mg_ref, mgt_ref, bnd_ref = refs[:5]
-    w_refs = refs[5 : 5 + count]
-    saved = refs[5 + count : 5 + 6 * count]
-    at = 5 + 6 * count
+def attend_back_kernel(own, heads, count, first, halo, off_ref, *refs):
+    x_ref, mg_ref, bnd_ref = refs[:3]
+    w_refs = refs[3 : 3 + count]
+    saved = refs[3 + count : 3 + 6 * count]
+    at = 3 + 6 * count
     in_ref = None if first else refs[at]
     rest = refs[at + (0 if first else 1) :]
     dn_ref = rest[0]
-    acc_refs = rest[1 + 2 * count :]
+    halo_refs = rest[1 + 2 * count : 1 + 2 * count + (2 if halo else 0)]
+    acc_refs = rest[1 + 2 * count + len(halo_refs) :]
     off = pl.multiple_of(off_ref[0], 16)
-    win = xt_ref.shape[2]
+    win = x_ref.shape[1]
     cols = heads * HEAD_DIM
     scale = HEAD_DIM**-0.5
     step = pl.program_id(0)
     mg = mg_ref[0]
+    xt = x_ref[0].T
+    xot = x_ref[0, pl.ds(off, own), :].T
+    mgt = mg.T
     place = lax.broadcasted_iota(jnp.int32, (win, heads * own), 0)
     keep = (place >= bnd_ref[0, 0:1]) & (place < bnd_ref[0, 1:2])
     dn = None if first else in_ref[0]
@@ -187,8 +189,8 @@
         dn = part if dn is None else dn + part
         part = nt(dq, w[:, 2 * cols : 3 * cols])
         dn_own = part if dn_own is None else dn_own + part
-        left = nn(xt_ref[0], dkv)
-        right = jnp.concatenate([nn(xot_ref[0], dq), nn(mgt_ref[0], o)], axis=1)
+        left = nn(xt, dkv)
+        right = jnp.concatenate([nn(xot, dq), nn(mgt, o)], axis=1)
         sums = jnp.concatenate(
             [
                 jnp.sum(dkv.astype(f32), axis=0, keepdims=True),
@@ -215,21 +217,23 @@
 
     dn_ref[0] = dn
     dn_ref[0, pl.ds(off, own), :] += dn_own
-
-
-def attend_back(off, xt, xot, mixed_grad, mgt, pieces, saved, bounds, grad_in):
-    micro, width, win = xt.shape
+    if halo:
+        before = pl.multiple_of(jnp.maximum(off - halo, 0), 16)
+        after = pl.multiple_of(jnp.minimum(off + own, win - halo), 16)
+        halo_refs[0][0] = dn_ref[0, pl.ds(before, halo), :].astype(bf16)
+        halo_refs[1][0] = dn_ref[0, pl.ds(after, halo), :].astype(bf16)
+
+
+def attend_back(off, x_win, mixed_grad, pieces, saved, bounds, grad_in, halo):
+    micro, win, width = x_win.shape
     own = mixed_grad.shape[1]
     cols = pieces[0].shape[1] // 4
     heads = cols // HEAD_DIM
     stacked = heads * own
     count = len(pieces)
     first = grad_in is None
-    args = [xt, xot, mixed_grad, mgt, bounds] + list(pieces)
-    in_specs = [
-        per_micro((width, win)), per_micro((width, own)), per_micro((own, width)),
-        per_micro((width, own)), per_micro((2, stacked)),
-    ]
+    args = [x_win, mixed_grad, bounds] + list(pieces)
+    in_specs = [per_micro((win, width)), per_micro((own, width)), per_micro((2, stacked))]
     in_specs += [full((width, 4 * cols))] * count
     for one in saved:
         args += list(one)
@@ -246,8 +250,11 @@
             jax.ShapeDtypeStruct((1, 4 * cols), f32),
         ]
         specs += [full((width, 4 * cols)), full((1, 4 * cols))]
+    for _ in range(2 if halo else 0):
+        shapes.append(jax.ShapeDtypeStruct((micro, halo, width), bf16))
+        specs.append(per_micro((halo, width)))
     result = pl.pallas_call(
-        partial(attend_back_kernel, own, heads, count, first),
+        partial(attend_back_kernel, own, heads, count, first, halo),
         grid_spec=pltpu.PrefetchScalarGridSpec(
             num_scalar_prefetch=1,
             grid=(micro,),
@@ -264,22 +271,24 @@
         ),
         name="attend_back",
     )(off, *args)
-    return result[0], list(result[1::2]), list(result[2::2])
+    return result[0], result[1 : 1 + 2 * count : 2], result[2 : 2 + 2 * count : 2], result[1 + 2 * count :]
 
 
 def feed_kernel(chunks, count, first, *refs):
-    x_ref, g_ref, xt_ref, gt_ref = refs[:4]
-    w_refs = refs[4 : 4 + count]
-    b_refs = refs[4 + count : 4 + 2 * count]
-    at = 4 + 2 * count
+    x_ref, g_ref = refs[:2]
+    w_refs = refs[2 : 2 + count]
+    b_refs = refs[2 + count : 2 + 2 * count]
+    at = 2 + 2 * count
     if not first:
         fi_ref, ni_ref = refs[at : at + 2]
         at = at + 2
     f_ref, n_ref = refs[at : at + 2]
     outs = refs[at + 2 : at + 2 + 2 * count]
-    act_ref, ug_ref = refs[at + 2 + 2 * count :]
+    act_ref, ug_ref, xt_ref, gt_ref = refs[at + 2 + 2 * count :]
     rows = x_ref.shape[0]
     step = rows // chunks
+    xt_ref[...] = x_ref[...].T
+    gt_ref[...] = g_ref[...].T
     for i in range(count):
         w_ref, b_ref = w_refs[i], b_refs[i]
         dw_ref, db_ref = outs[2 * i : 2 * i + 2]
@@ -311,12 +320,12 @@
         dw_ref[:, hidden:] = nn(gt_ref[...], act_ref[...]).astype(bf16)
 
 
-def feed_part(x2, grad, x2t, gradt, pieces, biases, before):
+def feed_part(x2, grad, pieces, biases, before):
     rows, width = x2.shape
     hidden = biases[0].shape[1]
     count = len(pieces)
     first = before is None
-    args = [x2, grad, x2t, gradt] + list(pieces) + list(biases)
+    args = [x2, grad] + list(pieces) + list(biases)
     aliases = {}
     if not first:
         aliases = {len(args): 0, len(args) + 1: 1}
@@ -333,7 +342,12 @@
         in_specs=[whole] * len(args),
         out_specs=[whole] * len(shapes),
         out_shape=shapes,
-        scratch_shapes=[pltpu.VMEM((rows, hidden), bf16), pltpu.VMEM((rows, hidden), bf16)],
+        scratch_shapes=[
+            pltpu.VMEM((rows, hidden), bf16),
+            pltpu.VMEM((rows, hidden), bf16),
+            pltpu.VMEM((width, rows), bf16),
+            pltpu.VMEM((width, rows), bf16),
+        ],
         input_output_aliases=aliases,
         compiler_params=pltpu.CompilerParams(vmem_limit_bytes=VMEM_LIMIT),
         cost_estimate=cost(
@@ -360,6 +374,99 @@
         - jnp.mean(scaled, axis=-1, keepdims=True)
         - unit_rows * jnp.mean(scaled * unit_rows, axis=-1, keepdims=True)
     )
+
+
+VECTORS = (
+    "out_bias", "down_bias", "first_gain", "first_shift", "second_gain", "second_shift",
+    "mixer_scale", "feed_scale",
+)
+
+
+def row(vec_ref, name):
+    at = VECTORS.index(name)
+    return vec_ref[at : at + 1]
+
+
+def own_rows(shape):
+    return pl.BlockSpec((1,) + shape, lambda m, place: (m, place[0]) + (0,) * (len(shape) - 1))
+
+
+def rows_call(kernel, name, place, args, specs, shapes, out_specs):
+    micro = args[0].shape[0]
+    return pl.pallas_call(
+        kernel,
+        grid_spec=pltpu.PrefetchScalarGridSpec(
+            num_scalar_prefetch=1, grid=(micro,), in_specs=specs, out_specs=out_specs
+        ),
+        out_shape=shapes,
+        compiler_params=params(),
+        cost_estimate=cost(0, 0, 0),
+        name=name,
+    )(place, *args)
+
+
+def first_norm_kernel(place_ref, x_ref, c_ref, vec_ref, n_ref, g_ref):
+    start = pl.multiple_of(place_ref[1], 16)
+    win = n_ref.shape[1]
+    unit = norm_parts(x_ref[0, pl.ds(start, win), :].astype(f32))[0]
+    n_ref[0] = (unit * row(vec_ref, "first_gain") + row(vec_ref, "first_shift")).astype(bf16)
+    g_ref[0] = (row(vec_ref, "feed_scale") * c_ref[0].astype(f32)).astype(bf16)
+
+
+def second_norm_kernel(place_ref, mixed_ref, x_ref, vec_ref, m_ref, n_ref):
+    branch = mixed_ref[0] + row(vec_ref, "out_bias")
+    middle = x_ref[0].astype(f32) + row(vec_ref, "mixer_scale") * branch
+    m_ref[0] = middle
+    unit = norm_parts(middle)[0]
+    n_ref[0] = (unit * row(vec_ref, "second_gain") + row(vec_ref, "second_shift")).astype(bf16)
+
+
+def column_sums(sum_ref, rows_in):
+    total = jnp.concatenate([jnp.sum(r, axis=0, keepdims=True) for r in rows_in], axis=0)
+
+    @pl.when(pl.program_id(0) == 0)
+    def _():
+        sum_ref[...] = total
+
+    @pl.when(pl.program_id(0) > 0)
+    def _():
+        sum_ref[...] += total
+
+
+def second_back_kernel(
+    place_ref, feed_ref, back_ref, m_ref, mixed_ref, c_ref, vec_ref, l_ref, mg_ref, low_ref, sum_ref
+):
+    middle, back, grad = m_ref[0], back_ref[0], c_ref[0].astype(f32)
+    feed_scale = row(vec_ref, "feed_scale")
+    branch = feed_ref[0] + row(vec_ref, "down_bias")
+    l_ref[0] = (middle + feed_scale * branch).astype(bf16)
+    unit, inverse = norm_parts(middle)
+    middle_grad = grad + norm_back(back, unit, inverse, row(vec_ref, "second_gain"))
+    mg_ref[0] = middle_grad
+    low_ref[0] = (row(vec_ref, "mixer_scale") * middle_grad).astype(bf16)
+    mixer = mixed_ref[0] + row(vec_ref, "out_bias")
+    zero = jnp.zeros_like(grad[:8])
+    column_sums(
+        sum_ref,
+        [middle_grad, grad, zero, zero, back * unit, back, middle_grad * mixer, grad * branch],
+    )
+
+
+def first_back_kernel(
+    place_ref, win_ref, left_ref, right_ref, mg_ref, x_ref, vec_ref, t_ref, sum_ref
+):
+    own, halo = mg_ref.shape[1], left_ref.shape[1]
+    off = pl.multiple_of(place_ref[2], 16)
+    gap = jnp.zeros((own - halo, left_ref.shape[2]), f32)
+    grad = win_ref[0, pl.ds(off, own), :]
+    grad = grad + jnp.concatenate([left_ref[0].astype(f32), gap], axis=0)
+    grad = grad + jnp.concatenate([gap, right_ref[0].astype(f32)], axis=0)
+    unit, inverse = norm_parts(x_ref[0].astype(f32))
+    t_ref[0] = (
+        mg_ref[0] + norm_back(grad, unit, inverse, row(vec_ref, "first_gain"))
+    ).astype(bf16)
+    zero = jnp.zeros_like(grad[:8])
+    column_sums(sum_ref, [zero, zero, grad * unit, grad, zero, zero, zero, zero])
 
 
 def swap(values_in, axis, bit):
@@ -541,18 +648,22 @@
     last_key = jnp.min(jnp.where(passed, row_count, ends[:, :, None]), axis=1) - start
     bounds = jnp.tile(jnp.stack([first_key, last_key], axis=1), (1, 1, heads)).astype(jnp.int32)
 
-    token_window = lax.dynamic_slice_in_dim(tokens, start, window, 1).astype(f32)
-    window_normed = (norm_parts(token_window)[0] * first_gain + first_shift).astype(bf16)
-    output_grad = lax.dynamic_slice_in_dim(cotangent, narrow_at * own, own, 1)
-    output_grad = output_grad.reshape(rows, width).astype(f32)
-    feed_grad = (feed_scale * output_grad).astype(bf16)
-    token_rows = lax.dynamic_slice_in_dim(tokens, narrow_at * own, own, 1)
-    token_rows = token_rows.reshape(rows, width).astype(f32)
-
-    normed_t = window_normed.transpose(0, 2, 1)
-    own_normed = (norm_parts(token_rows)[0] * first_gain + first_shift).astype(bf16)
-    own_normed_t = own_normed.reshape(micro, own, width).transpose(0, 2, 1)
-    feed_grad_t = feed_grad.T
+    place = jnp.stack([narrow_at, start, off]).astype(jnp.int32)
+    vectors = jnp.stack(
+        [out_bias, down_bias, first_gain, first_shift, second_gain, second_shift, mixer_scale,
+         feed_scale]
+    )
+    own_spec, part_spec, vec_spec = own_rows((own, width)), per_micro((own, width)), full((8, width))
+    low_rows = jax.ShapeDtypeStruct((micro, own, width), bf16)
+    high_rows = jax.ShapeDtypeStruct((micro, own, width), f32)
+    sum_rows = jax.ShapeDtypeStruct((8, width), f32)
+    window_normed, feed_grad = rows_call(
+        first_norm_kernel, "first_norm", place, [tokens, cotangent, vectors],
+        [per_micro((row_count, width)), own_spec, vec_spec],
+        [jax.ShapeDtypeStruct((micro, window, width), bf16), low_rows],
+        [per_micro((window, width)), part_spec],
+    )
+    feed_grad = feed_grad.reshape(rows, width)
 
     heads_near = swap(heads_own, "narrow", 1)
     heads_far = swap(heads_own, "narrow", 2)
@@ -578,17 +689,14 @@
     mixed, saved3 = attend(
         offset, window_normed, [heads_cross], qv_biases[3], bounds, own, mixed
     )
-    branch = mixed.reshape(rows, width) + out_bias
-    middle = token_rows + mixer_scale * branch
-    second_unit, second_inverse = norm_parts(middle)
-    second_normed = (second_unit * second_gain + second_shift).astype(bf16)
-
-    second_normed_t = second_normed.T
+    middle, second_normed = rows_call(
+        second_norm_kernel, "second_norm", place, [mixed, tokens, vectors],
+        [part_spec, own_spec, vec_spec], [high_rows, low_rows], [part_spec, part_spec],
+    )
+    second_normed = second_normed.reshape(rows, width)
 
     def feed_on(pieces, biases, before):
-        return feed_part(
-            second_normed, feed_grad, second_normed_t, feed_grad_t, pieces, biases, before
-        )
+        return feed_part(second_normed, feed_grad, pieces, biases, before)
 
     sums, (part1,), bias1 = feed_on([feed_near], up_biases[1:2], None)
     given = swap(part1, "narrow", 1)
@@ -597,48 +705,45 @@
     near_cut = cut(near, "wide", last)
     feed, back, *near_cut = tie(*sums, *near_cut)
     near_sent = send_cut(near_cut, last)
-    feed_far, near_keep = tie(feed_far, near_cut[0])
+    near_keep = near_cut[0]
+    feed, feed_far = tie(feed, feed_far)
     feed_cross = swap(feed_far, "narrow", 1)
-    sums, (part2, part3), bias23 = feed_on([feed_far, feed_cross], up_biases[2:], (feed, back))
+    sums, (part2,), bias2 = feed_on([feed_far], up_biases[2:3], (feed, back))
+    sums, (part3,), bias3 = feed_on([feed_cross], up_biases[3:], sums)
     given = swap(part3, "narrow", 1)
     feed, second_normed_grad = sums
-    up_bias_parts = bias0 + bias1 + bias23
-
-    feed_branch = feed + down_bias
-    layer_own = (middle + feed_scale * feed_branch).astype(bf16).reshape(micro, own, width)
+    up_bias_parts = bias0 + bias1 + bias2 + bias3
+
+    layer_own, middle_grad, mixed_grad, back_sums = rows_call(
+        second_back_kernel, "second_back", place,
+        [feed.reshape(micro, own, width), second_normed_grad.reshape(micro, own, width), middle,
+         mixed, cotangent, vectors],
+        [part_spec, part_spec, part_spec, part_spec, own_spec, vec_spec],
+        [low_rows, high_rows, low_rows, sum_rows],
+        [part_spec, part_spec, part_spec, vec_spec],
+    )
     y_high, core_high = bit_of("narrow", 2), bit_of("narrow", 1)
     layer_far = swap(layer_own, "narrow", 2)
     layer_near = join(layer_own, swap(layer_own, "narrow", 1), core_high, 1)
     layer_far = join(layer_far, swap(layer_far, "narrow", 1), core_high, 1)
     layer_out = join(layer_near, layer_far, y_high, 1).reshape(micro, row_count, width)
 
-    feed_scale_sum = jnp.sum(output_grad * feed_branch, axis=0)
-    down_bias_sum = feed_scale * jnp.sum(output_grad, axis=0)
-    second_gain_sum = jnp.sum(second_normed_grad * second_unit, axis=0)
-    second_shift_sum = jnp.sum(second_normed_grad, axis=0)
-    middle_grad = output_grad + norm_back(second_normed_grad, second_unit, second_inverse, second_gain)
-    mixer_scale_sum = jnp.sum(middle_grad * branch, axis=0)
-    out_bias_sum = mixer_scale * jnp.sum(middle_grad, axis=0)
-    mixed_grad = (mixer_scale * middle_grad).astype(bf16).reshape(micro, own, width)
-
-    mgt = mixed_grad.transpose(0, 2, 1)
-
-    def back_on(pieces, saved, grad_in):
+    def back_on(pieces, saved, grad_in, halo):
         return attend_back(
-            offset, normed_t, own_normed_t, mixed_grad, mgt, pieces, saved, bounds, grad_in
+            offset, window_normed, mixed_grad, pieces, saved, bounds, grad_in, halo
         )
 
     near, far = add_low(near_keep, *near_sent), add_low(part2, given)
     far_cut = cut(far, "wide", last)
-    mgt, near, *far_cut = tie(mgt, near, *far_cut)
+    mixed_grad, near, *far_cut = tie(mixed_grad, near, *far_cut)
     far_sent = send_cut(far_cut, last)
-    window_grad, (heads3,), sums3 = back_on([heads_cross], saved3, None)
+    window_grad, (heads3,), sums3, _ = back_on([heads_cross], saved3, None, 0)
     given3 = swap(heads3, "narrow", 1)
     window_grad, *far_sent = tie(window_grad, *far_sent)
     far = add_low(far_cut[0], *far_sent)
     window_grad, far = tie(window_grad, far)
     far_given = swap(far, "narrow", 2)
-    window_grad, (heads2,), sums2 = back_on([heads_far], saved2, window_grad)
+    window_grad, (heads2,), sums2, _ = back_on([heads_far], saved2, window_grad, 0)
     window_grad, far_given, given3 = tie(window_grad, far_given, given3)
     mine = add_low(near, far_given)
     for bits in groups[:-1]:
@@ -649,13 +754,13 @@
     window_grad, heads_sum, *mine_cut = tie(window_grad, heads_sum, *mine_cut)
     mine_sent = send_cut(mine_cut, groups[-1])
     heads_given = swap(heads_sum, "narrow", 2)
-    window_grad, (heads1,), sums1 = back_on([heads_near], saved1, window_grad)
+    window_grad, (heads1,), sums1, _ = back_on([heads_near], saved1, window_grad, 0)
     given1 = swap(heads1, "narrow", 1)
     window_grad, heads_given, *mine_sent = tie(window_grad, heads_given, *mine_sent)
     mine = add_low(mine_cut[0], *mine_sent)
     window_grad, mine = tie(window_grad, mine)
     mine_all = exchange(mine, groups[-1])
-    window_grad, (heads0,), sums0 = back_on([heads_own], saved0, window_grad)
+    window_grad, (heads0,), sums0, halos = back_on([heads_own], saved0, window_grad, halo)
     window_grad, *mine_all = tie(window_grad, *mine_all)
     mine = arrange(mine_all, groups[-1], 0).reshape((-1,) + mine.shape[1:])
     for bits in reversed(groups[:-1]):
@@ -666,33 +771,20 @@
     )
     head_bias_parts = [
         jnp.concatenate([s[0, 2 * cols : 3 * cols], s[0, cols : 2 * cols]])
-        for s in sums0 + sums1 + sums2 + sums3
+        for s in [*sums0, *sums1, *sums2, *sums3]
     ]
 
-    before = lax.dynamic_slice_in_dim(window_grad, jnp.maximum(off - halo, 0), halo, 1)
-    after = lax.dynamic_slice_in_dim(
-        window_grad, jnp.minimum(off + own, window - halo), halo, 1
-    )
-    from_left = shift(after.astype(bf16), "narrow", 1).astype(f32)
-    from_right = shift(before.astype(bf16), "narrow", -1).astype(f32)
-    first_normed_grad = lax.dynamic_slice_in_dim(window_grad, off, own, 1)
-    first_normed_grad = (
-        first_normed_grad
-        + jnp.pad(from_left, ((0, 0), (0, own - halo), (0, 0)))
-        + jnp.pad(from_right, ((0, 0), (own - halo, 0), (0, 0)))
-    ).reshape(rows, width)
-
-    first_unit, first_inverse = norm_parts(token_rows)
-    first_gain_sum = jnp.sum(first_normed_grad * first_unit, axis=0)
-    first_shift_sum = jnp.sum(first_normed_grad, axis=0)
-    token_grad = (
-        middle_grad + norm_back(first_normed_grad, first_unit, first_inverse, first_gain)
-    ).astype(bf16).reshape(micro, own, width)
-
-    sums = jnp.stack(
-        [out_bias_sum, down_bias_sum, first_gain_sum, first_shift_sum, second_gain_sum,
-         second_shift_sum, mixer_scale_sum, feed_scale_sum]
-    )
+    from_left = shift(halos[1], "narrow", 1)
+    from_right = shift(halos[0], "narrow", -1)
+    token_grad, first_sums = rows_call(
+        first_back_kernel, "first_back", place,
+        [window_grad, from_left, from_right, middle_grad, tokens, vectors],
+        [per_micro((window, width)), per_micro((halo, width)), per_micro((halo, width)), part_spec,
+         own_spec, vec_spec],
+        [low_rows, sum_rows], [part_spec, vec_spec],
+    )
+    outer = jnp.stack([mixer_scale, feed_scale] + [jnp.ones_like(out_bias)] * 6)
+    sums = (back_sums + first_sums) * outer
     group_sums = jnp.stack(
         [jnp.concatenate([head_bias_parts[r], up_bias_parts[r][0]]) for r in range(narrow_size)]
     )

time: 621 us -> 499 us (0.80)
  local copies, waits for them, and re-layouts: 140 us -> 35.3 us
  other arithmetic: 113 us -> 38.3 us
  Pallas kernels: 200 us -> 235 us
  waiting for transfers between devices: 101 us -> 128 us
    convert_element_type x10 -> x0, local copies, waits for them, and re-layouts: 33.2 us -> none  [the longest x2 7.43 us: body(): token_rows = token_rows.reshape(rows, width).astype(f32)]
    pallas_call x4 -> x8, Pallas kernels: 99.2 us -> 132 us  [the longest x4 98.2 us: attend_back(): pl.pallas_call(partial(attend_back_kernel, own, heads, count, first, halo...]
    reduce_sum x9 -> x0, other arithmetic: 31.2 us -> none  [the longest x1 7.25 us: body(): feed_scale_sum = jnp.sum(output_grad * feed_branch, axis=0)]
    ppermute x48, waiting for transfers between devices: 101 us -> 128 us  [swap(): return lax.ppermute(values_in, axis, [(i, i ^ bit) for i in range(size)])]
    convert_element_type x6 -> x0, other arithmetic: 18.7 us -> none  [the longest x1 4.92 us: body(): token_grad = (middle_grad + norm_back(first_normed_grad, first_unit, firs...]
    reshape x3 -> x0, local copies, waits for them, and re-layouts: 10.9 us -> none  [the longest x1 3.77 us: body(): (mixer_scale * middle_grad).astype(bf16).reshape(micro, own, width)]
    pallas_call x3 -> x0, local copies, waits for them, and re-layouts: 10.9 us -> none  [the longest x2 6.02 us: feed_part(): pl.pallas_call(partial(feed_kernel, 4, count, first), in_specs=[whole] *...]
    optimization_barrier x1 -> x0, local copies, waits for them, and re-layouts: 8.1 us -> none  [tie(): return lax.optimization_barrier(values_in)]
  transfers between devices with their start and end apart: 50 -> 50, of which waited for: 12 -> 19; matrix products, arithmetic and copies ran while one was open for 39% -> 12% of each run, Pallas kernels for 31% -> 43%
where the time goes in v3:
time: 499 us; the launch traced here: 491 us
  Pallas kernels  235 us (47%)
  waiting for transfers between devices  128 us (26%)
  starting transfers between devices  52.9 us (11%)
  other arithmetic  38.3 us (8%)
  local copies, waits for them, and re-layouts  35.3 us (7%)
    ppermute x48, waiting for transfers between devices, swap(): return lax.ppermute(values_in, axis, [(i, i ^ bit) for i in range(size)])  128 us
    pallas_call x4, Pallas kernels, attend_back(): pl.pallas_call(partial(attend_back_kernel, own, heads, count, first, halo...  98.2 us
    pallas_call x4, Pallas kernels, feed_part(): pl.pallas_call(partial(feed_kernel, 4, count, first), in_specs=[whole] *...  52.4 us
    pallas_call x4, Pallas kernels, attend(): pl.pallas_call(partial(attend_kernel, own, heads, count, first), grid_spe...  50.4 us
    ppermute x48, starting transfers between devices, swap(): return lax.ppermute(values_in, axis, [(i, i ^ bit) for i in range(size)])  49.1 us
    pallas_call x4, Pallas kernels, rows_call(): pl.pallas_call(kernel, grid_spec=pltpu.PrefetchScalarGridSpec(num_scalar_...  33.5 us
    convert_element_type x10, other arithmetic, add_low(): return total.astype(bf16)  16.1 us
    unnamed x77, local copies, waits for them, and re-layouts  11 us
  transfers between devices with their start and end apart: 50, of which 19 were waited for; matrix products, arithmetic and copies ran while one was open for 12% of the time, Pallas kernels for 43%

profile of v3, /device:TPU:0, one launch (start us, length us, event | category | flops | bytes accessed | tf_op | source)
XLA Modules:
  0.0 491.2 jit_solution(9495720541097324715)
XLA Ops:
  2.5 5.1 %collective-permute-start.3 = (bf16[1,96,768]{2,1,0:T(8,128)(2,1)S(1)}, bf16[1,96,768]{2,1,0:T(8,128)(2,1)S(1)}, u32[]{:S(2)}, u32[]{:S(2)}) collective-permute-start(bf16[1,96,768]{2,1,0:T(8,128)(2,1)S(1)} %maximum_bitcast_fusion.3), channel_id=1, source_target_pairs={{0,24},{4,28},{8,16},{12,20},{16,8},{20,12},{24,0},{28,4},{1,25},{... | collective-permute-start | bytes 442376 | tf_op jit(solution)/shard_map/ppermute | solution.py:474
  9.3 3.2 collective-permute-done.3
  12.5 7.7 %collective-permute-done.4 = bf16[1,96,768]{2,1,0:T(8,128)(2,1)S(1)} collective-permute-done((bf16[1,96,768]{2,1,0:T(8,128)(2,1)S(1)}, bf16[1,96,768]{2,1,0:T(8,128)(2,1)S(1)}, u32[]{:S(2)}, u32[]{:S(2)}) %collective-permute-start.4) | collective-permute-done | bytes 147488 | tf_op jit(solution)/shard_map/ppermute | solution.py:474
  23.6 8.1 %first_norm.1 = (bf16[3,768,768]{2,1,0:T(8,128)(2,1)}, bf16[3,320,768]{2,1,0:T(8,128)(2,1)}) custom-call(s32[3]{0:T(128)} %pad_add_fusion.1.place_ref, bf16[3,1280,768]{2,1,0:T(8,128)(2,1)} %x_ref.5, bf16[3,1280,768]{2,1,0:T(8,128)(2,1)} %c_ref.3, f32[8,768]{1,0:T(8,128)} %stack.120.vec_ref), custom_call_target="tpu_custom_call" | custom-call | flops 1024 | bytes 1024 | tf_op jit(solution)/shard_map/first_norm/pallas_call | solution.py:396
  32.8 2.5 collective-permute-start.10
  38.6 12.2 %attend.4 = (f32[3,320,768]{2,1,0:T(8,128)}, bf16[3,320,192]{2,1,0:T(8,128)(2,1)}, bf16[3,768,192]{2,1,0:T(8,128)(2,1)}, bf16[3,768,192]{2,1,0:T(8,128)(2,1)}, b...) custom-call(s32[1]{0:T(128)} %bitcast.2.off_ref, bf16[3,768,768]{2,1,0:T(8,128)(2,1)} %get-tuple-element.129.refs_0_, ...), custom_call_target="tpu_custom_call" | custom-call | flops 1024 | bytes 1024 | tf_op jit(solution)/shard_map/attend/pallas_call | solution.py:128
  51.8 6.6 %collective-permute-done.9 = bf16[1,96,1536]{2,1,0:T(8,128)(2,1)S(1)} collective-permute-done((bf16[1,96,1536]{2,1,0:T(8,128)(2,1)S(1)}, bf16[1,96,1536]{2,1,0:T(8,128)(2,1)S(1)}, u32[]{:S(2)}, u32[]{:S(2)}) %collective-permute-start.9) | collective-permute-done | bytes 294944 | tf_op jit(solution)/shard_map/ppermute | solution.py:474
  65.9 12.6 %attend.5 = (f32[3,320,768]{2,1,0:T(8,128)}, bf16[3,320,192]{2,1,0:T(8,128)(2,1)}, bf16[3,768,192]{2,1,0:T(8,128)(2,1)}, bf16[3,768,192]{2,1,0:T(8,128)(2,1)}, b...) custom-call(s32[1]{0:T(128)} %bitcast.2.off_ref, bf16[3,768,768]{2,1,0:T(8,128)(2,1)} %get-tuple-element.129.refs_0_, ...), custom_call_target="tpu_custom_call" | custom-call | flops 1024 | bytes 1024 | tf_op jit(solution)/shard_map/attend/pallas_call | solution.py:128
  78.5 6.2 %collective-permute-done.11 = bf16[4,96,1536]{2,1,0:T(8,128)(2,1)} collective-permute-done((bf16[4,96,1536]{2,1,0:T(8,128)(2,1)S(1)}, bf16[4,96,1536]{2,1,0:T(8,128)(2,1)}, u32[]{:S(2)}, u32[]{:S(2)}) %collective-permute-start.11) | collective-permute-done | bytes 1179680 | tf_op jit(solution)/shard_map/ppermute | solution.py:474
  89.7 2.2 collective-permute-done
  95.8 13.1 %attend.6 = (f32[3,320,768]{2,1,0:T(8,128)}, bf16[3,320,192]{2,1,0:T(8,128)(2,1)}, bf16[3,768,192]{2,1,0:T(8,128)(2,1)}, bf16[3,768,192]{2,1,0:T(8,128)(2,1)}, b...) custom-call(s32[1]{0:T(128)} %bitcast.2.off_ref, bf16[3,768,768]{2,1,0:T(8,128)(2,1)} %get-tuple-element.129.refs_0_, ...), custom_call_target="tpu_custom_call" | custom-call | flops 1024 | bytes 1024 | tf_op jit(solution)/shard_map/attend/pallas_call | solution.py:128
  109.9 12.6 %attend.7 = (f32[3,320,768]{2,1,0:T(8,128)}, bf16[3,320,192]{2,1,0:T(8,128)(2,1)}, bf16[3,768,192]{2,1,0:T(8,128)(2,1)}, bf16[3,768,192]{2,1,0:T(8,128)(2,1)}, b...) custom-call(s32[1]{0:T(128)} %bitcast.2.off_ref, bf16[3,768,768]{2,1,0:T(8,128)(2,1)} %get-tuple-element.129.refs_0_, ...), custom_call_target="tpu_custom_call" | custom-call | flops 1024 | bytes 1024 | tf_op jit(solution)/shard_map/attend/pallas_call | solution.py:128
  122.5 6.0 %second_norm.1 = (f32[3,320,768]{2,1,0:T(8,128)}, bf16[3,320,768]{2,1,0:T(8,128)(2,1)}) custom-call(s32[3]{0:T(128)} %pad_add_fusion.1.place_ref, f32[3,320,768]{2,1,0:T(8,128)} %get-tuple-element.146.mixed_ref, bf16[3,1280,768]{2,1,0:T(8,128)(2,1)} %x_ref.5, f32[8,768]{1,0:T(8,128)} %stack.120.vec_ref), custom_call_target="tpu_custom_call" | custom-call | flops 1024 | bytes 1024 | tf_op jit(solution)/shard_map/second_norm/pallas_call | solution.py:396
  128.5 11.6 %feed_part.4 = (f32[960,768]{1,0:T(8,128)}, f32[960,768]{1,0:T(8,128)}, bf16[768,1536]{1,0:T(8,128)(2,1)}, f32[1,768]{1,0:T(1,128)}) custom-call(bf16[960,768]{1,0:T(8,128)(2,1)} %bitcast.149, bf16[960,768]{1,0:T(8,128)(2,1)} %bitcast.145, bf16[768,1536]{1,0:T(8,128)(2,1)} %collective-permute-done.14.refs_2_, f32[1,768]{1,0:T(1,128)} %slice.163.refs_3_), custom_call_target="tpu_custom_call" | custom-call | flops 1024 | bytes 1024 | tf_op jit(solution)/shard_map/feed_part/pallas_call | solution.py:340
  142.7 13.6 %feed_part.5 = (f32[960,768]{1,0:T(8,128)}, f32[960,768]{1,0:T(8,128)}, bf16[768,1536]{1,0:T(8,128)(2,1)}, f32[1,768]{1,0:T(1,128)}) custom-call(bf16[960,768]{1,0:T(8,128)(2,1)} %bitcast.150, bf16[960,768]{1,0:T(8,128)(2,1)} %bitcast.146, bf16[768,1536]{1,0:T(8,128)(2,1)} %bitcast.156, ...), custom_call_target="tpu_custom_call", output_to_operand_aliasing={{0}: (4, {}), {1}: (5, {})} | custom-call | flops 1024 | bytes 1024 | tf_op jit(solution)/shard_map/feed_part/pallas_call | solution.py:340
  156.3 3.0 add_convert_fusion.1
  160.5 33.4 %collective-permute-done.16.refs_2_ = bf16[768,1536]{1,0:T(8,128)(2,1)} collective-permute-done((bf16[768,1536]{1,0:T(8,128)(2,1)S(1)}, bf16[768,1536]{1,0:T(8,128)(2,1)}, u32[]{:S(2)}, u32[]{:S(2)}) %collective-permute-start.16) | collective-permute-done | bytes 2359328 | tf_op jit(solution)/shard_map/ppermute | solution.py:474
  196.4 13.3 %feed_part.6 = (f32[960,768]{1,0:T(8,128)}, f32[960,768]{1,0:T(8,128)}, bf16[768,1536]{1,0:T(8,128)(2,1)}, f32[1,768]{1,0:T(1,128)}) custom-call(bf16[960,768]{1,0:T(8,128)(2,1)} %bitcast.151, bf16[960,768]{1,0:T(8,128)(2,1)} %bitcast.147, bf16[768,1536]{1,0:T(8,128)(2,1)} %collective-permute-done.16.refs_2_, ...), custom_call_target="tpu_custom_call", output_to_operand_aliasing={{0}: (4, {}), {1}: (5, {})} | custom-call | flops 1024 | bytes 1024 | tf_op jit(solution)/shard_map/feed_part/pallas_call | solution.py:340
  211.2 13.8 %feed_part.7 = (f32[960,768]{1,0:T(8,128)}, f32[960,768]{1,0:T(8,128)}, bf16[768,1536]{1,0:T(8,128)(2,1)}, f32[1,768]{1,0:T(1,128)}) custom-call(bf16[960,768]{1,0:T(8,128)(2,1)} %bitcast.152, bf16[960,768]{1,0:T(8,128)(2,1)} %bitcast.148, bf16[768,1536]{1,0:T(8,128)(2,1)} %copy-done.5, ...), custom_call_target="tpu_custom_call", output_to_operand_aliasing={{0}: (4, {}), {1}: (5, {})} | custom-call | flops 1024 | bytes 1024 | tf_op jit(solution)/shard_map/feed_part/pallas_call | solution.py:340
  226.0 27.6 %collective-permute-done.21 = bf16[384,1536]{1,0:T(8,128)(2,1)S(1)} collective-permute-done((bf16[384,1536]{1,0:T(8,128)(2,1)}, bf16[384,1536]{1,0:T(8,128)(2,1)S(1)}, u32[]{:S(2)}, u32[]{:S(2)}) %collective-permute-start.21) | collective-permute-done | bytes 1179680 | tf_op jit(solution)/shard_map/ppermute | solution.py:474
  254.9 10.7 %second_back.1 = (bf16[3,320,768]{2,1,0:T(8,128)(2,1)}, f32[3,320,768]{2,1,0:T(8,128)}, bf16[3,320,768]{2,1,0:T(8,128)(2,1)}, f32[8,768]{1,0:T(8,128)}) custom-call(s32[3]{0:T(128)} %pad_add_fusion.1.place_ref, f32[3,320,768]{2,1,0:T(8,128)} %bitcast.143, f32[3,320,768]{2,1,0:T(8,128)} %bitcast.144, f32[3,320,768]{2,1,0:T(8,128)} %get-tuple-element.164.m_ref, ...), custom_call_target="tpu_custom_call" | custom-call | flops 1024 | bytes 1024 | tf_op jit(solution)/shard_map/second_back/pallas_call | solution.py:396
  265.7 2.3 add_convert_fusion
  271.3 23.9 %attend_back.4 = (f32[3,768,768]{2,1,0:T(8,128)}, bf16[768,768]{1,0:T(8,128)(2,1)}, f32[1,768]{1,0:T(1,128)}) custom-call(s32[1]{0:T(128)} %bitcast.2.off_ref, bf16[3,768,768]{2,1,0:T(8,128)(2,1)} %get-tuple-element.129.refs_0_, bf16[3,320,768]{2,1,0:T(8,128)(2,1)} %get-tuple-element.171.refs_1_, s32[3,2,960]{2,1,0:T(2,128)} %tile.10.refs_2_, ...), custom_call_target="tpu_custom_call" | custom-call | flops 1024 | bytes 1024 | tf_op jit(solution)/shard_map/attend_back/pallas_call | solution.py:256
  296.5 2.6 add_convert_fusion.5
  305.0 2.0 select_bitcast_fusion.1
  307.2 24.7 %attend_back.5 = (f32[3,768,768]{2,1,0:T(8,128)}, bf16[768,768]{1,0:T(8,128)(2,1)}, f32[1,768]{1,0:T(1,128)}) custom-call(s32[1]{0:T(128)} %bitcast.2.off_ref, bf16[3,768,768]{2,1,0:T(8,128)(2,1)} %get-tuple-element.129.refs_0_, bf16[3,320,768]{2,1,0:T(8,128)(2,1)} %get-tuple-element.171.refs_1_, s32[3,2,960]{2,1,0:T(2,128)} %tile.10.refs_2_, ...), custom_call_target="tpu_custom_call" | custom-call | flops 1024 | bytes 1024 | tf_op jit(solution)/shard_map/attend_back/pallas_call | solution.py:256
  331.9 1.9 add_convert_fusion.3
  335.3 2.6 add_convert_fusion.4
  339.4 2.0 select_bitcast_fusion.3
  342.6 3.0 copy.70
  345.6 2.2 collective-permute-start.28
  347.8 2.2 collective-permute-start.29
  350.2 24.7 %attend_back.6 = (f32[3,768,768]{2,1,0:T(8,128)}, bf16[768,768]{1,0:T(8,128)(2,1)}, f32[1,768]{1,0:T(1,128)}) custom-call(s32[1]{0:T(128)} %bitcast.2.off_ref, bf16[3,768,768]{2,1,0:T(8,128)(2,1)} %get-tuple-element.129.refs_0_, bf16[3,320,768]{2,1,0:T(8,128)(2,1)} %get-tuple-element.171.refs_1_, s32[3,2,960]{2,1,0:T(2,128)} %tile.10.refs_2_, ...), custom_call_target="tpu_custom_call" | custom-call | flops 1024 | bytes 1024 | tf_op jit(solution)/shard_map/attend_back/pallas_call | solution.py:256
  376.0 2.2 collective-permute-start.31
  378.2 2.2 collective-permute-start.32
  380.4 25.0 %attend_back.7 = (f32[3,768,768]{2,1,0:T(8,128)}, bf16[768,768]{1,0:T(8,128)(2,1)}, f32[1,768]{1,0:T(1,128)}, bf16[3,208,768]{2,1,0:T(8,128)(2,1)}, bf16[3,208,768]{2,1,0:T(8,128)(2,1)}) custom-call(s32[1]{0:T(128)} %bitcast.2.off_ref, bf16[3,768,768]{2,1,0:T(8,128)(2,1)} %get-tuple-element.129.refs_0_, bf16[3,320,768]{2,1,0:T(8,128)(2,1)} %get-tuple-element.171.refs_1_, ...), custom_call_target="tpu_custom_call" | custom-call | flops 1024 | bytes 1024 | tf_op jit(solution)/shard_map/attend_back/pallas_call | solution.py:256
  405.4 2.5 collective-permute-start.33
  410.2 2.0 add_convert_fusion.2
  415.9 12.6 %collective-permute-done.36 = bf16[384,768]{1,0:T(8,128)(2,1)S(1)} collective-permute-done((bf16[384,768]{1,0:T(8,128)(2,1)S(1)}, bf16[384,768]{1,0:T(8,128)(2,1)S(1)}, u32[]{:S(2)}, u32[]{:S(2)}) %collective-permute-start.36) | collective-permute-done | bytes 589856 | tf_op jit(solution)/shard_map/ppermute | solution.py:474
  428.8 2.2 collective-permute-start.38
  431.0 2.2 collective-permute-start.39
  433.2 8.7 %first_back.1 = (bf16[3,320,768]{2,1,0:T(8,128)(2,1)}, f32[8,768]{1,0:T(8,128)}) custom-call(s32[3]{0:T(128)} %pad_add_fusion.1.place_ref, f32[3,768,768]{2,1,0:T(8,128)} %get-tuple-element.220.win_ref, bf16[3,208,768]{2,1,0:T(8,128)(2,1)} %collective-permute-done.33.left_ref, bf16[3,208,768]{2,1,0:T(8,128)(2,1)} %collective-permute-done.34.right_ref, ...), custom_call_target="tpu_custom_call" | custom-call | flops 1024 | bytes 1024 | tf_op jit(solution)/shard_map/first_back/pallas_call | solution.py:396
  444.7 4.1 collective-permute-start.41
  448.8 5.2 %collective-permute-done.44 = f32[84,128]{1,0:T(8,128)S(1)} collective-permute-done((f32[84,128]{1,0:T(8,128)S(1)}, f32[84,128]{1,0:T(8,128)S(1)}, u32[]{:S(2)}, u32[]{:S(2)}) %collective-permute-start.44) | collective-permute-done | bytes 43040 | tf_op jit(solution)/shard_map/ppermute | solution.py:474
  454.7 6.0 %collective-permute-done.45 = f32[84,128]{1,0:T(8,128)S(1)} collective-permute-done((f32[84,128]{1,0:T(8,128)S(1)}, f32[84,128]{1,0:T(8,128)S(1)}, u32[]{:S(2)}, u32[]{:S(2)}) %collective-permute-start.45) | collective-permute-done | bytes 43040 | tf_op jit(solution)/shard_map/ppermute | solution.py:474
  462.2 2.6 collective-permute-done.46
  465.0 4.0 collective-permute-done.47
  479.8 6.1 %collective-permute-done.43 = bf16[384,768]{1,0:T(8,128)(2,1)} collective-permute-done((bf16[384,768]{1,0:T(8,128)(2,1)}, bf16[384,768]{1,0:T(8,128)(2,1)}, u32[]{:S(2)}, u32[]{:S(2)}) %collective-permute-start.43) | collective-permute-done | bytes 589856 | tf_op jit(solution)/shard_map/ppermute | solution.py:474
  (268 shorter events, 82.2 us)
Async XLA Ops:
  2.5 9.9 %collective-permute-start.3 = (bf16[1,96,768]{2,1,0:T(8,128)(2,1)S(1)}, bf16[1,96,768]{2,1,0:T(8,128)(2,1)S(1)}, u32[]{:S(2)}, u32[]{:S(2)}) collective-permute-start(bf16[1,96,768]{2,1,0:T(8,128)(2,1)S(1)} %maximum_bitcast_fusion.3), channel_id=1, source_target_pairs={{0,24},{4,28},{8,16},{12,20},{16,8},{20,12},{24,0},{28,4},{1,25},{... | collective-permute-start | bytes 442376 | tf_op jit(solution)/shard_map/ppermute | solution.py:474
  7.7 12.5 %collective-permute-start.4 = (bf16[1,96,768]{2,1,0:T(8,128)(2,1)S(1)}, bf16[1,96,768]{2,1,0:T(8,128)(2,1)S(1)}, u32[]{:S(2)}, u32[]{:S(2)}) collective-permute-start(bf16[1,96,768]{2,1,0:T(8,128)(2,1)S(1)} %maximum_bitcast_fusion.3), channel_id=1, source_target_pairs={{0,16},{4,20},{8,24},{12,28},{16,0},{20,4},{24,8},{28,12},{1,17},{... | collective-permute-start | bytes 442376 | tf_op jit(solution)/shard_map/ppermute | solution.py:474
  7.7 12.5 %collective-permute-start.5 = (bf16[1,96,768]{2,1,0:T(8,128)(2,1)S(1)}, bf16[1,96,768]{2,1,0:T(8,128)(2,1)S(1)}, u32[]{:S(2)}, u32[]{:S(2)}) collective-permute-start(bf16[1,96,768]{2,1,0:T(8,128)(2,1)S(1)} %maximum_bitcast_fusion.3), channel_id=1, source_target_pairs={{0,8},{4,12},{8,0},{12,4},{16,24},{20,28},{24,16},{28,20},{1,9},{5... | collective-permute-start | bytes 442376 | tf_op jit(solution)/shard_map/ppermute | solution.py:474
  20.5 16.6 %collective-permute-start.6 = (bf16[4,96,768]{2,1,0:T(8,128)(2,1)S(1)}, bf16[4,96,768]{2,1,0:T(8,128)(2,1)S(1)}, u32[]{:S(2)}, u32[]{:S(2)}) collective-permute-start(bf16[4,96,768]{2,1,0:T(8,128)(2,1)S(1)} %maximum_bitcast_fusion.1), channel_id=1, source_target_pairs={{0,4},{4,0},{8,12},{12,8},{16,20},{20,16},{24,28},{28,24},{1,5},{5... | collective-permute-start | bytes 1769480 | tf_op jit(solution)/shard_map/ppermute | solution.py:474
  32.8 18.0 %collective-permute-start.10 = (bf16[1,96,1536]{2,1,0:T(8,128)(2,1)S(1)}, bf16[1,96,1536]{2,1,0:T(8,128)(2,1)S(1)}, u32[]{:S(2)}, u32[]{:S(2)}) collective-permute-start(bf16[1,96,1536]{2,1,0:T(8,128)(2,1)S(1)} %maximum_bitcast_fusion.2), channel_id=1, source_target_pairs={{0,24},{4,28},{8,16},{12,20},{16,8},{20,12},{24,0},{28,4},{1,25},{... | collective-permute-start | bytes 884744 | tf_op jit(solution)/shard_map/ppermute | solution.py:474
  35.3 16.6 %collective-permute-start.8 = (bf16[1,96,1536]{2,1,0:T(8,128)(2,1)S(1)}, bf16[1,96,1536]{2,1,0:T(8,128)(2,1)S(1)}, u32[]{:S(2)}, u32[]{:S(2)}) collective-permute-start(bf16[1,96,1536]{2,1,0:T(8,128)(2,1)S(1)} %maximum_bitcast_fusion.2), channel_id=1, source_target_pairs={{0,8},{4,12},{8,0},{12,4},{16,24},{20,28},{24,16},{28,20},{1,9},{5... | collective-permute-start | bytes 884744 | tf_op jit(solution)/shard_map/ppermute | solution.py:474
  35.3 23.2 %collective-permute-start.9 = (bf16[1,96,1536]{2,1,0:T(8,128)(2,1)S(1)}, bf16[1,96,1536]{2,1,0:T(8,128)(2,1)S(1)}, u32[]{:S(2)}, u32[]{:S(2)}) collective-permute-start(bf16[1,96,1536]{2,1,0:T(8,128)(2,1)S(1)} %maximum_bitcast_fusion.2), channel_id=1, source_target_pairs={{0,16},{4,20},{8,24},{12,28},{16,0},{20,4},{24,8},{28,12},{1,17},{... | collective-permute-start | bytes 884744 | tf_op jit(solution)/shard_map/ppermute | solution.py:474
  38.6 26.3 %collective-permute-start.7 = (bf16[768,768]{1,0:T(8,128)(2,1)}, bf16[768,768]{1,0:T(8,128)(2,1)S(1)}, u32[]{:S(2)}, u32[]{:S(2)}) collective-permute-start(bf16[768,768]{1,0:T(8,128)(2,1)} %bitcast.23.refs_3_), channel_id=1, source_target_pairs={{0,1},{1,0},{2,3},{3,2},{4,5},{5,4},{6,7},{7,6},{8,9},{9,8},{10,11... | collective-permute-start | bytes 3538952 | tf_op jit(solution)/shard_map/ppermute | solution.py:474
  58.8 25.9 %collective-permute-start.11 = (bf16[4,96,1536]{2,1,0:T(8,128)(2,1)S(1)}, bf16[4,96,1536]{2,1,0:T(8,128)(2,1)}, u32[]{:S(2)}, u32[]{:S(2)}) collective-permute-start(bf16[4,96,1536]{2,1,0:T(8,128)(2,1)S(1)} %maximum_bitcast_fusion), channel_id=1, source_target_pairs={{0,4},{4,0},{8,12},{12,8},{16,20},{20,16},{24,28},{28,24},{1,5},{5... | collective-permute-start | bytes 3538952 | tf_op jit(solution)/shard_map/ppermute | solution.py:474
  59.4 27.1 %collective-permute-start.12 = (bf16[768,768]{1,0:T(8,128)(2,1)}, bf16[768,768]{1,0:T(8,128)(2,1)S(1)}, u32[]{:S(2)}, u32[]{:S(2)}) collective-permute-start(bf16[768,768]{1,0:T(8,128)(2,1)} %bitcast.23.refs_3_), channel_id=1, source_target_pairs={{0,2},{1,3},{2,0},{3,1},{4,6},{5,7},{6,4},{7,5},{8,10},{9,11},{10,... | collective-permute-start | bytes 3538952 | tf_op jit(solution)/shard_map/ppermute | solution.py:474
  87.7 40.8 %collective-permute-start.14 = (bf16[768,1536]{1,0:T(8,128)(2,1)S(1)}, bf16[768,1536]{1,0:T(8,128)(2,1)}, u32[]{:S(2)}, u32[]{:S(2)}) collective-permute-start(bf16[768,1536]{1,0:T(8,128)(2,1)S(1)} %bitcast.154), channel_id=1, source_target_pairs={{0,1},{1,0},{2,3},{3,2},{4,5},{5,4},{6,7},{7,6},{8,9},{9,8},{10,11... | collective-permute-start | bytes 7077896 | tf_op jit(solution)/shard_map/ppermute | solution.py:474
  87.7 21.2 %collective-permute-start.13 = (bf16[768,768]{1,0:T(8,128)(2,1)}, bf16[768,768]{1,0:T(8,128)(2,1)S(1)}, u32[]{:S(2)}, u32[]{:S(2)}) collective-permute-start(bf16[768,768]{1,0:T(8,128)(2,1)} %copy-done.3), channel_id=1, source_target_pairs={{0,1},{1,0},{2,3},{3,2},{4,5},{5,4},{6,7},{7,6},{8,9},{9,8},{10,11... | collective-permute-start | bytes 3538952 | tf_op jit(solution)/shard_map/ppermute | solution.py:474
  88.2 3.7 collective-permute-start
  91.9 2.6 collective-permute-start.1
  140.1 16.3 %collective-permute-start.15 = (bf16[768,1536]{1,0:T(8,128)(2,1)}, bf16[768,1536]{1,0:T(8,128)(2,1)}, u32[]{:S(2)}, u32[]{:S(2)}) collective-permute-start(bf16[768,1536]{1,0:T(8,128)(2,1)} %get-tuple-element.155), channel_id=1, source_target_pairs={{0,1},{1,0},{2,3},{3,2},{4,5},{5,4},{6,7},{7,6},{8,9},{9,8},{10,11... | collective-permute-start | bytes 7077896 | tf_op jit(solution)/shard_map/ppermute | solution.py:474
  140.6 53.3 %collective-permute-start.16 = (bf16[768,1536]{1,0:T(8,128)(2,1)S(1)}, bf16[768,1536]{1,0:T(8,128)(2,1)}, u32[]{:S(2)}, u32[]{:S(2)}) collective-permute-start(bf16[768,1536]{1,0:T(8,128)(2,1)S(1)} %bitcast.155), channel_id=1, source_target_pairs={{0,2},{1,3},{2,0},{3,1},{4,6},{5,7},{6,4},{7,5},{8,10},{9,11},{10,... | collective-permute-start | bytes 7077896 | tf_op jit(solution)/shard_map/ppermute | solution.py:474
  193.9 15.8 %collective-permute-start.17 = (bf16[768,1536]{1,0:T(8,128)(2,1)}, bf16[768,1536]{1,0:T(8,128)(2,1)S(1)}, u32[]{:S(2)}, u32[]{:S(2)}) collective-permute-start(bf16[768,1536]{1,0:T(8,128)(2,1)} %collective-permute-done.16.refs_2_), channel_id=1, source_target_pairs={{0,1},{1,0},{2,3},{3,2},{4,5},{5,4},{6,7},{7,6},{8,9},{9,8},{10,11... | collective-permute-start | bytes 7077896 | tf_op jit(solution)/shard_map/ppermute | solution.py:474
  225.0 40.6 %collective-permute-start.22 = (bf16[768,1536]{1,0:T(8,128)(2,1)}, bf16[768,1536]{1,0:T(8,128)(2,1)}, u32[]{:S(2)}, u32[]{:S(2)}) collective-permute-start(bf16[768,1536]{1,0:T(8,128)(2,1)} %get-tuple-element.170), channel_id=1, source_target_pairs={{0,1},{1,0},{2,3},{3,2},{4,5},{5,4},{6,7},{7,6},{8,9},{9,8},{10,11... | collective-permute-start | bytes 7077896 | tf_op jit(solution)/shard_map/ppermute | solution.py:474
  225.5 28.1 %collective-permute-start.21 = (bf16[384,1536]{1,0:T(8,128)(2,1)}, bf16[384,1536]{1,0:T(8,128)(2,1)S(1)}, u32[]{:S(2)}, u32[]{:S(2)}) collective-permute-start(bf16[384,1536]{1,0:T(8,128)(2,1)} %get-tuple-element.168), channel_id=1, source_target_pairs={{0,4},{4,0},{8,12},{12,8},{16,20},{20,16},{24,28},{28,24},{1,5},{5... | collective-permute-start | bytes 3538952 | tf_op jit(solution)/shard_map/ppermute | solution.py:474
  269.1 27.4 %collective-permute-start.23 = (bf16[384,1536]{1,0:T(8,128)(2,1)}, bf16[384,1536]{1,0:T(8,128)(2,1)}, u32[]{:S(2)}, u32[]{:S(2)}) collective-permute-start(bf16[384,1536]{1,0:T(8,128)(2,1)} %get-tuple-element.193), channel_id=1, source_target_pairs={{0,4},{4,0},{8,12},{12,8},{16,20},{20,16},{24,28},{28,24},{1,5},{5... | collective-permute-start | bytes 3538952 | tf_op jit(solution)/shard_map/ppermute | solution.py:474
  269.8 35.3 %collective-permute-start.18 = (bf16[3,320,768]{2,1,0:T(8,128)(2,1)S(1)}, bf16[3,320,768]{2,1,0:T(8,128)(2,1)}, u32[]{:S(2)}, u32[]{:S(2)}) collective-permute-start(bf16[3,320,768]{2,1,0:T(8,128)(2,1)S(1)} %copy-done.6), channel_id=1, source_target_pairs={{0,2},{1,3},{2,0},{3,1},{4,6},{5,7},{6,4},{7,5},{8,10},{9,11},{10,... | collective-permute-start | bytes 4423688 | tf_op jit(solution)/shard_map/ppermute | solution.py:474
  271.3 33.7 %collective-permute-start.20 = (bf16[3,320,768]{2,1,0:T(8,128)(2,1)S(1)}, bf16[3,320,768]{2,1,0:T(8,128)(2,1)}, u32[]{:S(2)}, u32[]{:S(2)}) collective-permute-start(bf16[3,320,768]{2,1,0:T(8,128)(2,1)S(1)} %copy-done.6), channel_id=1, source_target_pairs={{0,1},{1,0},{2,3},{3,2},{4,5},{5,4},{6,7},{7,6},{8,9},{9,8},{10,11... | collective-permute-start | bytes 4423688 | tf_op jit(solution)/shard_map/ppermute | solution.py:474
  295.2 36.7 %collective-permute-start.25 = (bf16[768,768]{1,0:T(8,128)(2,1)}, bf16[768,768]{1,0:T(8,128)(2,1)}, u32[]{:S(2)}, u32[]{:S(2)}) collective-permute-start(bf16[768,768]{1,0:T(8,128)(2,1)} %get-tuple-element.200), channel_id=1, source_target_pairs={{0,1},{1,0},{2,3},{3,2},{4,5},{5,4},{6,7},{7,6},{8,9},{9,8},{10,11... | collective-permute-start | bytes 3538952 | tf_op jit(solution)/shard_map/ppermute | solution.py:474
  299.2 32.7 %collective-permute-start.24 = (bf16[384,1536]{1,0:T(8,128)(2,1)}, bf16[384,1536]{1,0:T(8,128)(2,1)}, u32[]{:S(2)}, u32[]{:S(2)}) collective-permute-start(bf16[384,1536]{1,0:T(8,128)(2,1)} %add_convert_fusion.5), channel_id=1, source_target_pairs={{0,2},{1,3},{2,0},{3,1},{4,6},{5,7},{6,4},{7,5},{8,10},{9,11},{10,... | collective-permute-start | bytes 3538952 | tf_op jit(solution)/shard_map/ppermute | solution.py:474
  305.0 34.4 %collective-permute-start.19 = (bf16[3,320,768]{2,1,0:T(8,128)(2,1)}, bf16[3,320,768]{2,1,0:T(8,128)(2,1)}, u32[]{:S(2)}, u32[]{:S(2)}) collective-permute-start(bf16[3,320,768]{2,1,0:T(8,128)(2,1)} %collective-permute-done.18), channel_id=1, source_target_pairs={{0,1},{1,0},{2,3},{3,2},{4,5},{5,4},{6,7},{7,6},{8,9},{9,8},{10,11... | collective-permute-start | bytes 4423688 | tf_op jit(solution)/shard_map/ppermute | solution.py:474
  337.9 37.9 %collective-permute-start.26 = (bf16[768,768]{1,0:T(8,128)(2,1)}, bf16[768,768]{1,0:T(8,128)(2,1)}, u32[]{:S(2)}, u32[]{:S(2)}) collective-permute-start(bf16[768,768]{1,0:T(8,128)(2,1)} %add_convert_fusion.4), channel_id=1, source_target_pairs={{0,2},{1,3},{2,0},{3,1},{4,6},{5,7},{6,4},{7,5},{8,10},{9,11},{10,... | collective-permute-start | bytes 3538952 | tf_op jit(solution)/shard_map/ppermute | solution.py:474
  345.6 30.1 %collective-permute-start.27 = (bf16[96,1536]{1,0:T(8,128)(2,1)}, bf16[96,1536]{1,0:T(8,128)(2,1)S(1)}, u32[]{:S(2)}, u32[]{:S(2)}) collective-permute-start(bf16[96,1536]{1,0:T(8,128)(2,1)} %get-tuple-element.209), channel_id=1, source_target_pairs={{0,8},{4,12},{8,0},{12,4},{16,24},{20,28},{24,16},{28,20},{1,9},{5... | collective-permute-start | bytes 884744 | tf_op jit(solution)/shard_map/ppermute | solution.py:474
  345.6 30.1 %collective-permute-start.28 = (bf16[96,1536]{1,0:T(8,128)(2,1)}, bf16[96,1536]{1,0:T(8,128)(2,1)S(1)}, u32[]{:S(2)}, u32[]{:S(2)}) collective-permute-start(bf16[96,1536]{1,0:T(8,128)(2,1)} %get-tuple-element.210), channel_id=1, source_target_pairs={{0,16},{4,20},{8,24},{12,28},{16,0},{20,4},{24,8},{28,12},{1,17},{... | collective-permute-start | bytes 884744 | tf_op jit(solution)/shard_map/ppermute | solution.py:474
  347.8 27.9 %collective-permute-start.29 = (bf16[96,1536]{1,0:T(8,128)(2,1)S(1)}, bf16[96,1536]{1,0:T(8,128)(2,1)S(1)}, u32[]{:S(2)}, u32[]{:S(2)}) collective-permute-start(bf16[96,1536]{1,0:T(8,128)(2,1)S(1)} %get-tuple-element.211), channel_id=1, source_target_pairs={{0,24},{4,28},{8,16},{12,20},{16,8},{20,12},{24,0},{28,4},{1,25},{... | collective-permute-start | bytes 884744 | tf_op jit(solution)/shard_map/ppermute | solution.py:474
  374.8 34.1 %collective-permute-start.35 = (bf16[768,768]{1,0:T(8,128)(2,1)}, bf16[768,768]{1,0:T(8,128)(2,1)S(1)}, u32[]{:S(2)}, u32[]{:S(2)}) collective-permute-start(bf16[768,768]{1,0:T(8,128)(2,1)} %get-tuple-element.226), channel_id=1, source_target_pairs={{0,1},{1,0},{2,3},{3,2},{4,5},{5,4},{6,7},{7,6},{8,9},{9,8},{10,11... | collective-permute-start | bytes 3538952 | tf_op jit(solution)/shard_map/ppermute | solution.py:474
  375.9 36.5 %collective-permute-start.30 = (bf16[96,1536]{1,0:T(8,128)(2,1)S(1)}, bf16[96,1536]{1,0:T(8,128)(2,1)S(1)}, u32[]{:S(2)}, u32[]{:S(2)}) collective-permute-start(bf16[96,1536]{1,0:T(8,128)(2,1)S(1)} %add_convert_fusion.8), channel_id=1, source_target_pairs={{0,8},{4,12},{8,0},{12,4},{16,24},{20,28},{24,16},{28,20},{1,9},{5... | collective-permute-start | bytes 884744 | tf_op jit(solution)/shard_map/ppermute | solution.py:474
  376.0 37.9 %collective-permute-start.31 = (bf16[96,1536]{1,0:T(8,128)(2,1)S(1)}, bf16[96,1536]{1,0:T(8,128)(2,1)S(1)}, u32[]{:S(2)}, u32[]{:S(2)}) collective-permute-start(bf16[96,1536]{1,0:T(8,128)(2,1)S(1)} %add_convert_fusion.8), channel_id=1, source_target_pairs={{0,16},{4,20},{8,24},{12,28},{16,0},{20,4},{24,8},{28,12},{1,17},{... | collective-permute-start | bytes 884744 | tf_op jit(solution)/shard_map/ppermute | solution.py:474
  378.2 35.7 %collective-permute-start.32 = (bf16[96,1536]{1,0:T(8,128)(2,1)S(1)}, bf16[96,1536]{1,0:T(8,128)(2,1)}, u32[]{:S(2)}, u32[]{:S(2)}) collective-permute-start(bf16[96,1536]{1,0:T(8,128)(2,1)S(1)} %add_convert_fusion.8), channel_id=1, source_target_pairs={{0,24},{4,28},{8,16},{12,20},{16,8},{20,12},{24,0},{28,4},{1,25},{... | collective-permute-start | bytes 884744 | tf_op jit(solution)/shard_map/ppermute | solution.py:474
  405.4 25.6 %collective-permute-start.33 = (bf16[3,208,768]{2,1,0:T(8,128)(2,1)}, bf16[3,208,768]{2,1,0:T(8,128)(2,1)}, u32[]{:S(2)}, u32[]{:S(2)}) collective-permute-start(bf16[3,208,768]{2,1,0:T(8,128)(2,1)} %get-tuple-element.221), channel_id=1, source_target_pairs={{0,1},{1,2},{2,3},{4,5},{5,6},{6,7},{8,9},{9,10},{10,11},{12,13},{... | collective-permute-start | bytes 2875400 | tf_op jit(solution)/shard_map/ppermute | solution.py:480
  408.9 24.3 %collective-permute-start.34 = (bf16[3,208,768]{2,1,0:T(8,128)(2,1)}, bf16[3,208,768]{2,1,0:T(8,128)(2,1)}, u32[]{:S(2)}, u32[]{:S(2)}) collective-permute-start(bf16[3,208,768]{2,1,0:T(8,128)(2,1)} %get-tuple-element.222), channel_id=1, source_target_pairs={{1,0},{2,1},{3,2},{5,4},{6,5},{7,6},{9,8},{10,9},{11,10},{13,12},{... | collective-permute-start | bytes 2875400 | tf_op jit(solution)/shard_map/ppermute | solution.py:480
  412.4 16.1 %collective-permute-start.36 = (bf16[384,768]{1,0:T(8,128)(2,1)S(1)}, bf16[384,768]{1,0:T(8,128)(2,1)S(1)}, u32[]{:S(2)}, u32[]{:S(2)}) collective-permute-start(bf16[384,768]{1,0:T(8,128)(2,1)S(1)} %constant_dynamic-slice_fusion.8), channel_id=1, source_target_pairs={{0,4},{4,0},{8,12},{12,8},{16,20},{20,16},{24,28},{28,24},{1,5},{5... | collective-permute-start | bytes 1769480 | tf_op jit(solution)/shard_map/ppermute | solution.py:474
  415.2 58.1 %collective-permute-start.49 = (bf16[384,1536]{1,0:T(8,128)(2,1)S(1)}, bf16[384,1536]{1,0:T(8,128)(2,1)}, u32[]{:S(2)}, u32[]{:S(2)}) collective-permute-start(bf16[384,1536]{1,0:T(8,128)(2,1)S(1)} %bitcast.159), channel_id=1, source_target_pairs={{0,4},{4,0},{8,12},{12,8},{16,20},{20,16},{24,28},{28,24},{1,5},{5... | collective-permute-start | bytes 3538952 | tf_op jit(solution)/shard_map/ppermute | solution.py:474
  428.7 14.1 %collective-permute-start.37 = (bf16[96,768]{1,0:T(8,128)(2,1)S(1)}, bf16[96,768]{1,0:T(8,128)(2,1)S(1)}, u32[]{:S(2)}, u32[]{:S(2)}) collective-permute-start(bf16[96,768]{1,0:T(8,128)(2,1)S(1)} %get-tuple-element.346), channel_id=1, source_target_pairs={{0,8},{4,12},{8,0},{12,4},{16,24},{20,28},{24,16},{28,20},{1,9},{5... | collective-permute-start | bytes 442376 | tf_op jit(solution)/shard_map/ppermute | solution.py:474
  428.8 14.1 %collective-permute-start.38 = (bf16[96,768]{1,0:T(8,128)(2,1)S(1)}, bf16[96,768]{1,0:T(8,128)(2,1)S(1)}, u32[]{:S(2)}, u32[]{:S(2)}) collective-permute-start(bf16[96,768]{1,0:T(8,128)(2,1)S(1)} %get-tuple-element.348), channel_id=1, source_target_pairs={{0,16},{4,20},{8,24},{12,28},{16,0},{20,4},{24,8},{28,12},{1,17},{... | collective-permute-start | bytes 442376 | tf_op jit(solution)/shard_map/ppermute | solution.py:474
  431.0 11.8 %collective-permute-start.39 = (bf16[96,768]{1,0:T(8,128)(2,1)S(1)}, bf16[96,768]{1,0:T(8,128)(2,1)S(1)}, u32[]{:S(2)}, u32[]{:S(2)}) collective-permute-start(bf16[96,768]{1,0:T(8,128)(2,1)S(1)} %get-tuple-element.347), channel_id=1, source_target_pairs={{0,24},{4,28},{8,16},{12,20},{16,8},{20,12},{24,0},{28,4},{1,25},{... | collective-permute-start | bytes 442376 | tf_op jit(solution)/shard_map/ppermute | solution.py:474
  442.7 11.3 %collective-permute-start.44 = (f32[84,128]{1,0:T(8,128)S(1)}, f32[84,128]{1,0:T(8,128)S(1)}, u32[]{:S(2)}, u32[]{:S(2)}) collective-permute-start(f32[84,128]{1,0:T(8,128)S(1)} %maximum_bitcast_fusion.4), channel_id=1, source_target_pairs={{0,16},{4,20},{8,24},{12,28},{16,0},{20,4},{24,8},{28,12},{1,17},{... | collective-permute-start | bytes 129032 | tf_op jit(solution)/shard_map/ppermute | solution.py:474
  443.0 19.2 %collective-permute-start.40 = (bf16[96,768]{1,0:T(8,128)(2,1)S(1)}, bf16[96,768]{1,0:T(8,128)(2,1)S(1)}, u32[]{:S(2)}, u32[]{:S(2)}) collective-permute-start(bf16[96,768]{1,0:T(8,128)(2,1)S(1)} %add_convert_fusion.9), channel_id=1, source_target_pairs={{0,24},{4,28},{8,16},{12,20},{16,8},{20,12},{24,0},{28,4},{1,25},{... | collective-permute-start | bytes 442376 | tf_op jit(solution)/shard_map/ppermute | solution.py:474
  444.7 17.5 %collective-permute-start.41 = (bf16[96,768]{1,0:T(8,128)(2,1)S(1)}, bf16[96,768]{1,0:T(8,128)(2,1)S(1)}, u32[]{:S(2)}, u32[]{:S(2)}) collective-permute-start(bf16[96,768]{1,0:T(8,128)(2,1)S(1)} %add_convert_fusion.9), channel_id=1, source_target_pairs={{0,16},{4,20},{8,24},{12,28},{16,0},{20,4},{24,8},{28,12},{1,17},{... | collective-permute-start | bytes 442376 | tf_op jit(solution)/shard_map/ppermute | solution.py:474
  448.8 5.8 %collective-permute-start.42 = (bf16[96,768]{1,0:T(8,128)(2,1)S(1)}, bf16[96,768]{1,0:T(8,128)(2,1)S(1)}, u32[]{:S(2)}, u32[]{:S(2)}) collective-permute-start(bf16[96,768]{1,0:T(8,128)(2,1)S(1)} %add_convert_fusion.9), channel_id=1, source_target_pairs={{0,8},{4,12},{8,0},{12,4},{16,24},{20,28},{24,16},{28,20},{1,9},{5... | collective-permute-start | bytes 442376 | tf_op jit(solution)/shard_map/ppermute | solution.py:474
  454.1 6.6 %collective-permute-start.45 = (f32[84,128]{1,0:T(8,128)S(1)}, f32[84,128]{1,0:T(8,128)S(1)}, u32[]{:S(2)}, u32[]{:S(2)}) collective-permute-start(f32[84,128]{1,0:T(8,128)S(1)} %fusion.3), channel_id=1, source_target_pairs={{0,8},{4,12},{8,0},{12,4},{16,24},{20,28},{24,16},{28,20},{1,9},{5... | collective-permute-start | bytes 129032 | tf_op jit(solution)/shard_map/ppermute | solution.py:474
  460.7 4.1 collective-permute-start.46
  464.8 4.1 collective-permute-start.47
  469.9 16.0 %collective-permute-start.43 = (bf16[384,768]{1,0:T(8,128)(2,1)}, bf16[384,768]{1,0:T(8,128)(2,1)}, u32[]{:S(2)}, u32[]{:S(2)}) collective-permute-start(bf16[384,768]{1,0:T(8,128)(2,1)} %bitcast.46), channel_id=1, source_target_pairs={{0,4},{4,0},{8,12},{12,8},{16,20},{20,16},{24,28},{28,24},{1,5},{5... | collective-permute-start | bytes 1769480 | tf_op jit(solution)/shard_map/ppermute | solution.py:474
  (36 other events, 236.2 us)
